TPU v7x, 32 devices: a whole 2x2x4 slice. The times are simulated.
32 devices in a mesh: section: 4 (over y, x), dp: 8 (over z, core).
Axes of the slice: x: 2, y: 2, z: 4, core: 2. Of those that a mesh axis runs over, the one named last changes fastest.
Arguments:
- token_ids: int32 [4, 512], P(None, 'dp'), may hold values from 0 to 127
- embed: bfloat16 [128, 512], replicated, may hold values from -6 to 6
- weights: bfloat16 [4, 2, 512, 2048], P('section'), may hold values from -0.25 to 0.25
- variance: bfloat16 [4, 1024, 2048], P('section', 'dp'), may hold values from 9.9658966e-05 to 0.0099487305
- momentum: bfloat16 [4, 1024, 2048], P('section', 'dp'), may hold values from -4 to 4
- worker_error: bfloat16 [4, 8, 2, 512, 2048], P('section', 'dp'), may hold values from -6 to 6
- server_error: float32 [4, 1024, 2048], P('section', 'dp'), may hold values from -0.75 to 0.75
- cotangent: bfloat16 [4, 512, 512], P(None, 'dp'), may hold values from -0.75 to 0.75
Outputs:
- new_weights: bfloat16 [4, 1024, 2048], P('section', 'dp')
- new_momentum: bfloat16 [4, 1024, 2048], P('section', 'dp')
- new_worker_error: bfloat16 [4, 8, 2, 512, 2048], P('section', 'dp')
- new_server_error: float32 [4, 1024, 2048], P('section', 'dp')
All inputs are finite; a program needn't handle non-finite values.
Results may differ from a plain program's by a relative error of at most 0.012.
Values may be sent and summed in bfloat16 or wider, within the bound.
No kernel may reach another device: no remote copies, remote signals or barrier semaphores. Data moves between devices by JAX's collectives and lax.ppermute only.
A program may use at most 128 MiB of HBM per device.

v0:
```python
import math

import jax
import jax.numpy as jnp
from jax import lax
from jax.sharding import PartitionSpec as P

gelu_coef = math.sqrt(2.0 / math.pi)


def passed_along(array, axis, by):
    count = lax.axis_size(axis)
    pairs = [(i, i + by) for i in range(count) if 0 <= i + by < count]
    return lax.ppermute(array, axis, pairs)


def gelu_value(upper):
    inner = gelu_coef * (upper + 0.044715 * upper * upper * upper)
    return 0.5 * upper * (1.0 + jnp.tanh(inner))


def gelu_slope(upper):
    inner = gelu_coef * (upper + 0.044715 * upper * upper * upper)
    bent = jnp.tanh(inner)
    return 0.5 * (1.0 + bent) + 0.5 * upper * (1.0 - bent * bent) * gelu_coef * (
        1.0 + 3.0 * 0.044715 * upper * upper
    )


def normalize(inputs):
    values = inputs.astype(jnp.float32)
    center = jnp.mean(values, axis=-1, keepdims=True)
    spread = jnp.mean((values - center) * (values - center), axis=-1, keepdims=True)
    scaled = lax.rsqrt(spread + 1e-05)
    return ((values - center) * scaled, scaled)


def forward_block(inputs, first_matrix, second_matrix):
    normed, scaled = normalize(inputs)
    normed_b = normed.astype(jnp.bfloat16)
    upper = jnp.dot(normed_b, first_matrix, preferred_element_type=jnp.float32)
    hidden = gelu_value(upper).astype(jnp.bfloat16)
    mixed = lax.dot_general(
        hidden, second_matrix, (((1,), (1,)), ((), ())), preferred_element_type=jnp.float32
    )
    output = (inputs.astype(jnp.float32) + mixed).astype(jnp.bfloat16)
    return (output, normed, scaled, normed_b, upper, hidden)


def backward_block(grad_out, normed, scaled, upper, first_matrix, second_matrix):
    back_hidden = jnp.dot(grad_out, second_matrix, preferred_element_type=jnp.float32)
    back_upper = (back_hidden * gelu_slope(upper)).astype(jnp.bfloat16)
    back_normed = lax.dot_general(
        back_upper, first_matrix, (((1,), (1,)), ((), ())), preferred_element_type=jnp.float32
    )
    first_mean = jnp.mean(back_normed, axis=-1, keepdims=True)
    second_mean = jnp.mean(back_normed * normed, axis=-1, keepdims=True)
    grad_in = (
        grad_out.astype(jnp.float32) + scaled * (back_normed - first_mean - normed * second_mean)
    ).astype(jnp.bfloat16)
    return (grad_in, back_upper)


def row_product(left, right):
    return lax.dot_general(
        left, right, (((0,), (0,)), ((), ())), preferred_element_type=jnp.float32
    )


def local(token_ids, embed, weights, variance, momentum, worker_error, server_error, cotangent):
    section_count = lax.axis_size("section")
    section_index = lax.axis_index("section")
    replicas = lax.axis_size("dp")
    micro = token_ids.shape[0]
    rows = token_ids.shape[1]
    vocab = embed.shape[0]
    width = embed.shape[1]
    channels = weights.shape[3]
    owned = 2 * width // replicas
    shared = lax.all_gather(momentum[0], "dp", axis=0, tiled=True)
    first_matrix = weights[0, 0]
    second_matrix = weights[0, 1]
    one_hot = (token_ids[:, :, None] == lax.broadcasted_iota(jnp.int32, (1, 1, vocab), 2)).astype(
        jnp.bfloat16
    )
    embedded = jnp.einsum("mtv,vd->mtd", one_hot, embed, preferred_element_type=jnp.float32).astype(
        jnp.bfloat16
    )
    steps = micro + section_count - 1
    incoming = jnp.zeros((rows, width), jnp.bfloat16)
    saved_normed, saved_scaled, saved_bf, saved_upper, saved_hidden = ([], [], [], [], [])
    for step in range(steps):
        index = jnp.clip(step - section_index, 0, micro - 1)
        fresh = lax.dynamic_index_in_dim(embedded, index, 0, keepdims=False)
        inputs = jnp.where(section_index == 0, fresh, incoming)
        output, normed, scaled, normed_b, upper, hidden = forward_block(
            inputs, first_matrix, second_matrix
        )
        saved_normed.append(normed)
        saved_scaled.append(scaled)
        saved_bf.append(normed_b)
        saved_upper.append(upper)
        saved_hidden.append(hidden)
        if step + 1 < steps:
            incoming = passed_along(output, "section", 1)
    normed_all = jnp.stack(saved_normed)
    scaled_all = jnp.stack(saved_scaled)
    normed_bf_all = jnp.stack(saved_bf)
    upper_all = jnp.stack(saved_upper)
    hidden_all = jnp.stack(saved_hidden)
    grad_first = jnp.zeros((width, channels), jnp.float32)
    grad_second = jnp.zeros((width, channels), jnp.float32)
    back_in = jnp.zeros((rows, width), jnp.bfloat16)
    for step in range(steps):
        micro_index = step - (section_count - 1 - section_index)
        valid = jnp.logical_and(micro_index >= 0, micro_index < micro)
        clipped = jnp.clip(micro_index, 0, micro - 1)
        slot = jnp.clip(micro_index + section_index, 0, steps - 1)
        arriving = lax.dynamic_index_in_dim(cotangent, clipped, 0, keepdims=False)
        grad_out = jnp.where(section_index == section_count - 1, arriving, back_in)
        normed = lax.dynamic_index_in_dim(normed_all, slot, 0, keepdims=False)
        scaled = lax.dynamic_index_in_dim(scaled_all, slot, 0, keepdims=False)
        normed_b = lax.dynamic_index_in_dim(normed_bf_all, slot, 0, keepdims=False)
        upper = lax.dynamic_index_in_dim(upper_all, slot, 0, keepdims=False)
        hidden = lax.dynamic_index_in_dim(hidden_all, slot, 0, keepdims=False)
        grad_in, back_upper = backward_block(
            grad_out, normed, scaled, upper, first_matrix, second_matrix
        )
        grad_first = grad_first + jnp.where(valid, row_product(normed_b, back_upper), 0.0)
        grad_second = grad_second + jnp.where(valid, row_product(grad_out, hidden), 0.0)
        if step + 1 < steps:
            back_in = passed_along(grad_in, "section", -1)
    gradient = jnp.stack([grad_first, grad_second])
    combined = (
        0.9 * shared.astype(jnp.float32).reshape(2, width, channels)
        + 0.1 * gradient
        + worker_error[0, 0].astype(jnp.float32)
    )
    worker_scale = jnp.sqrt(jnp.mean(combined * combined) + 0.01)
    packed = (worker_scale * jnp.tanh(combined / worker_scale)).astype(jnp.bfloat16)
    new_worker = (combined - packed.astype(jnp.float32)).astype(jnp.bfloat16)[None, None]
    flat = packed.reshape(2 * width, channels)
    total = lax.psum_scatter(flat.astype(jnp.float32), "dp", scatter_dimension=0, tiled=True)
    merged = total / replicas + server_error[0]
    server_scale = jnp.sqrt(jnp.mean(merged * merged) + 0.01)
    server_values = (server_scale * jnp.tanh(merged / server_scale)).astype(jnp.bfloat16)
    new_server = (merged - server_values.astype(jnp.float32))[None]
    start = lax.axis_index("dp") * owned
    own_weights = lax.dynamic_slice_in_dim(weights[0].reshape(2 * width, channels), start, owned, 0)
    step_size = (
        0.01
        * server_values.astype(jnp.float32)
        / (jnp.sqrt(variance[0].astype(jnp.float32)) + 1e-08)
    )
    new_weights = (own_weights.astype(jnp.float32) - step_size).astype(jnp.bfloat16)[None]
    return (new_weights, server_values[None], new_worker, new_server)


def solution(mesh):
    in_specs = (
        P(None, "dp"),
        P(),
        P("section", None, None, None),
        P("section", "dp", None),
        P("section", "dp", None),
        P("section", "dp", None, None, None),
        P("section", "dp", None),
        P(None, "dp", None),
    )
    out_specs = (
        P("section", "dp", None),
        P("section", "dp", None),
        P("section", "dp", None, None, None),
        P("section", "dp", None),
    )
    return jax.shard_map(local, mesh=mesh, in_specs=in_specs, out_specs=out_specs, check_vma=False)
```

profile of v0, /device:TPU:0, one launch (start us, length us, event | category | flops | bytes accessed | tf_op | source)
XLA Modules:
  0.0 279.5 jit_solution(15378231506081991087)
XLA Ops:
  7.2 0.8 copy-done
  8.1 0.9 convolution_convert_fusion
  9.4 2.9 %bitcast_dynamic-update-slice_fusion.6 = (f32[7,64,2048]{2,1,0:T(8,128)}, f32[64,2048]{1,0:T(8,128)S(1)}) fusion(bf16[1,2,512,2048]{3,2,1,0:T(8,128)(2,1)} %param.10, f32[64]{0:T(128)S(1)} %add_rsqrt_fusion.6, f32[64]{0:T(128)S(1)} %broadcast_multiply_fusion.18, bf16[4,64,512]{2,1,0:T(8,128)(2,1)S(1)} %convolution_convert_fusion, s32[]{:T(128)S(6)} %min.64, ...), kind=kOutput, calls=%fused_computation.214 | convolution fusion | flops 134381568 | bytes 3212293 | tf_op jit(solution)/shard_map/dot_general | solution.py:41
  12.3 2.4 fusion.88
  14.6 4.9 %collective-permute-start = (bf16[64,512]{1,0:T(8,128)(2,1)S(1)}, bf16[64,512]{1,0:T(8,128)(2,1)S(1)}, u32[]{:S(2)}, u32[]{:S(2)}) collective-permute-start(bf16[64,512]{1,0:T(8,128)(2,1)S(1)} %fusion.88), channel_id=1, source_target_pairs={{0,8},{8,16},{16,24},{1,9},{9,17},{17,25},{2,10},{10,18},{18,26},{... | collective-permute-start | bytes 196616 | tf_op jit(solution)/shard_map/ppermute | solution.py:14
  19.6 0.7 fusion.256
  21.7 0.8 fusion.242
  22.5 3.1 %bitcast_dynamic-update-slice_fusion.5 = (f32[7,64,2048]{2,1,0:T(8,128)}, f32[64,2048]{1,0:T(8,128)S(1)}) fusion(f32[7,64,2048]{2,1,0:T(8,128)} %get-tuple-element.36, bf16[1,2,512,2048]{3,2,1,0:T(8,128)(2,1)} %param.10, bf16[64,512]{1,0:T(8,128)(2,1)S(1)} %get-tuple-element.29, f32[64]{0:T(128)S(1)} %add_rsqrt_fusion.5, f32[64]{0:T(128)S(1)} %broadcast_multiply_fusion.17), kind=kOutput, calls=%fused_computation.213 | convolution fusion | flops 134348800 | bytes 3211776 | tf_op jit(solution)/shard_map/dot_general | solution.py:41
  25.5 2.5 fusion.85
  28.0 4.3 %collective-permute-start.1 = (bf16[64,512]{1,0:T(8,128)(2,1)S(1)}, bf16[64,512]{1,0:T(8,128)(2,1)S(1)}, u32[]{:S(2)}, u32[]{:S(2)}) collective-permute-start(bf16[64,512]{1,0:T(8,128)(2,1)S(1)} %fusion.85), channel_id=1, source_target_pairs={{0,8},{8,16},{16,24},{1,9},{9,17},{17,25},{2,10},{10,18},{18,26},{... | collective-permute-start | bytes 196616 | tf_op jit(solution)/shard_map/ppermute | solution.py:14
  32.6 1.6 collective-permute-done.1
  34.6 1.3 bitcast_dynamic-update-slice_fusion.4
  35.9 0.8 fusion.82
  36.7 4.4 %collective-permute-start.2 = (bf16[64,512]{1,0:T(8,128)(2,1)S(1)}, bf16[64,512]{1,0:T(8,128)(2,1)S(1)}, u32[]{:S(2)}, u32[]{:S(2)}) collective-permute-start(bf16[64,512]{1,0:T(8,128)(2,1)S(1)} %fusion.82), channel_id=1, source_target_pairs={{0,8},{8,16},{16,24},{1,9},{9,17},{17,25},{2,10},{10,18},{18,26},{... | collective-permute-start | bytes 196616 | tf_op jit(solution)/shard_map/ppermute | solution.py:14
  41.4 1.6 collective-permute-done.2
  44.0 0.8 fusion.79
  44.7 5.2 %collective-permute-start.3 = (bf16[64,512]{1,0:T(8,128)(2,1)S(1)}, bf16[64,512]{1,0:T(8,128)(2,1)S(1)}, u32[]{:S(2)}, u32[]{:S(2)}) collective-permute-start(bf16[64,512]{1,0:T(8,128)(2,1)S(1)} %fusion.79), channel_id=1, source_target_pairs={{0,8},{8,16},{16,24},{1,9},{9,17},{17,25},{2,10},{10,18},{18,26},{... | collective-permute-start | bytes 196616 | tf_op jit(solution)/shard_map/ppermute | solution.py:14
  50.2 1.6 collective-permute-done.3
  52.8 0.8 fusion.76
  53.5 5.2 %collective-permute-start.4 = (bf16[64,512]{1,0:T(8,128)(2,1)S(1)}, bf16[64,512]{1,0:T(8,128)(2,1)S(1)}, u32[]{:S(2)}, u32[]{:S(2)}) collective-permute-start(bf16[64,512]{1,0:T(8,128)(2,1)S(1)} %fusion.76), channel_id=1, source_target_pairs={{0,8},{8,16},{16,24},{1,9},{9,17},{17,25},{2,10},{10,18},{18,26},{... | collective-permute-start | bytes 196616 | tf_op jit(solution)/shard_map/ppermute | solution.py:14
  59.0 1.6 collective-permute-done.4
  61.6 0.8 fusion.73
  62.3 5.2 %collective-permute-start.5 = (bf16[64,512]{1,0:T(8,128)(2,1)S(1)}, bf16[64,512]{1,0:T(8,128)(2,1)S(1)}, u32[]{:S(2)}, u32[]{:S(2)}) collective-permute-start(bf16[64,512]{1,0:T(8,128)(2,1)S(1)} %fusion.73), channel_id=1, source_target_pairs={{0,8},{8,16},{16,24},{1,9},{9,17},{17,25},{2,10},{10,18},{18,26},{... | collective-permute-start | bytes 196616 | tf_op jit(solution)/shard_map/ppermute | solution.py:14
  67.8 1.6 collective-permute-done.5
  71.1 0.9 fusion.389
  72.1 1.5 collective-permute-start.6
  73.7 2.7 fusion.302
  76.6 0.7 fusion.202
  77.3 2.2 collective-permute-done.6
  80.2 0.9 fusion.388
  81.1 2.7 fusion.298
  83.9 1.3 collective-permute-start.7
  85.2 0.7 fusion.200
  86.0 5.4 %collective-permute-done.7 = bf16[64,512]{1,0:T(8,128)(2,1)S(1)} collective-permute-done((bf16[64,512]{1,0:T(8,128)(2,1)S(1)}, bf16[64,512]{1,0:T(8,128)(2,1)S(1)}, u32[]{:S(2)}, u32[]{:S(2)}) %collective-permute-start.7) | collective-permute-done | bytes 65568 | tf_op jit(solution)/shard_map/ppermute | solution.py:14
  92.1 0.9 fusion.387
  93.0 2.7 fusion.296
  95.8 1.3 collective-permute-start.8
  97.8 5.0 %collective-permute-done.8 = bf16[64,512]{1,0:T(8,128)(2,1)S(1)} collective-permute-done((bf16[64,512]{1,0:T(8,128)(2,1)S(1)}, bf16[64,512]{1,0:T(8,128)(2,1)S(1)}, u32[]{:S(2)}, u32[]{:S(2)}) %collective-permute-start.8) | collective-permute-done | bytes 65568 | tf_op jit(solution)/shard_map/ppermute | solution.py:14
  103.5 0.9 fusion.386
  104.4 2.7 fusion.294
  107.3 1.3 collective-permute-start.9
  109.3 5.0 %collective-permute-done.9 = bf16[64,512]{1,0:T(8,128)(2,1)S(1)} collective-permute-done((bf16[64,512]{1,0:T(8,128)(2,1)S(1)}, bf16[64,512]{1,0:T(8,128)(2,1)S(1)}, u32[]{:S(2)}, u32[]{:S(2)}) %collective-permute-start.9) | collective-permute-done | bytes 65568 | tf_op jit(solution)/shard_map/ppermute | solution.py:14
  115.0 0.9 fusion.385
  116.0 1.3 collective-permute-start.10
  117.3 2.7 fusion.292
  120.7 2.4 collective-permute-done.10
  123.8 0.9 fusion.384
  124.8 1.5 collective-permute-start.11
  126.3 2.7 fusion.290
  129.1 0.7 fusion.192
  129.8 2.1 collective-permute-done.11
  131.9 4.2 %select_add_fusion = f32[512,2048]{1,0:T(8,128)} fusion(f32[512,2048]{1,0:T(8,128)S(1)} %fusion.192, f32[512,2048]{1,0:T(8,128)S(1)} %fusion.194, f32[512,2048]{1,0:T(8,128)S(1)} %fusion.196, f32[512,2048]{1,0:T(8,128)S(1)} %fusion.198, f32[512,2048]{1,0:T(8,128)S(1)} %fusion.200, f32[512,2048]{1,0:T(8,128)S(1)} %fusion.202, pred[]{:T(512)S(6)} %and.29, ...), kind=kOutput, calls=%fused_computation.12 | convolution fusion | flops 147881984 | bytes 29753360 | tf_op jit(solution)/shard_map/dot_general | solution.py:65
  136.0 9.9 %select_add_fusion.1 = f32[512,2048]{1,0:T(8,128)} fusion(f32[512,2048]{1,0:T(8,128)} %fusion.290, f32[512,2048]{1,0:T(8,128)} %fusion.292, f32[512,2048]{1,0:T(8,128)} %fusion.294, f32[512,2048]{1,0:T(8,128)} %fusion.296, f32[512,2048]{1,0:T(8,128)} %fusion.298, f32[512,2048]{1,0:T(8,128)} %fusion.302, pred[]{:T(512)S(6)} %and.29, pred[]{:T(512)S(6)} %and.28, ...), kind=kOutput, calls=%fused_computation.13 | convolution fusion | flops 284590080 | bytes 32183808 | tf_op jit(solution)/shard_map/dot_general | solution.py:65
  145.9 8.5 %maximum_multiply_fusion = f32[2,512,2048]{2,1,0:T(8,128)} fusion(f32[1,512,2048]{2,1,0:T(8,128)} %bitcast.529, f32[1,512,2048]{2,1,0:T(8,128)} %bitcast.531), kind=kLoop, calls=%fused_computation | loop fusion | flops 4194304 | bytes 16777216 | tf_op jit(solution)/shard_map/mul | solution.py:136
  154.4 7.6 %multiply_reduce_fusion = f32[]{:T(128)} fusion(bf16[1,1,2,512,2048]{4,3,2,1,0:T(8,128)(2,1)} %param.13, f32[2,512,2048]{2,1,0:T(8,128)} %maximum_multiply_fusion, bf16[1,1024,2048]{2,1,0:T(8,128)(2,1)} %all-gather.3.cloned.1.call-done), kind=kLoop, calls=%fused_computation.10 | loop fusion | flops 14680063 | bytes 16777220 | tf_op jit(solution)/shard_map/reduce_sum | solution.py:139
  162.7 9.4 %fusion.2 = f32[1024,2048]{1,0:T(8,128)} fusion(f32[]{:T(128)S(6)} %sqrt.10, bf16[1,1,2,512,2048]{4,3,2,1,0:T(8,128)(2,1)} %param.13, f32[2,512,2048]{2,1,0:T(8,128)} %maximum_multiply_fusion, bf16[1,1024,2048]{2,1,0:T(8,128)(2,1)} %all-gather.3.cloned.1.call-done), kind=kLoop, calls=%fused_computation.11 | loop fusion | flops 18874368 | bytes 25165828 | tf_op jit(solution)/shard_map/convert_element_type | solution.py:143
  172.2 3.5 %convert_multiply_fusion = f32[1,1024,2048]{2,1,0:T(8,128)S(1)} fusion(bf16[1,1024,2048]{2,1,0:T(8,128)(2,1)} %all-gather.3.cloned.1.call-done), kind=kLoop, calls=%fused_computation.6 | loop fusion | flops 4194304 | bytes 12582912 | tf_op jit(solution)/shard_map/mul | solution.py:135
  175.7 1.1 copy-done.4
  176.9 1.2 copy-done.5
  178.1 4.1 %subtract_convert_fusion = bf16[1,1,2,512,2048]{4,3,2,1,0:T(8,128)(2,1)} fusion(f32[1,1,2,512,2048]{4,3,2,1,0:T(8,128)S(1)} %bitcast.533, f32[1,1,1,512,2048]{4,3,2,1,0:T(8,128)S(1)} %bitcast.530, f32[1,1,1,512,2048]{4,3,2,1,0:T(8,128)S(1)} %bitcast.532, f32[]{:T(128)S(6)} %sqrt.10, bf16[1,1,2,512,2048]{4,3,2,1,0:T(8,128)(2,1)S(1)} %copy-done.3), kind=kLoop, calls=%fused_computation.7 | loop fusion | flops 23068672 | bytes 25165828 | tf_op jit(solution)/shard_map/convert_element_type | solution.py:141
  182.1 82.7 %reduce-scatter.2.cloned.1.call-done = f32[128,2048]{1,0:T(8,128)} async-done(((f32[1024,2048]{1,0:T(8,128)}), f32[128,2048]{1,0:T(8,128)}) %reduce-scatter.2.cloned.1.call-update) | async-done | bytes 1048592 | tf_op jit(solution)/shard_map/reduce_scatter | solution.py:143
  264.8 2.1 multiply_reduce_fusion.1
  267.6 2.4 fusion.94
  270.1 2.6 fusion.190
  (125 shorter events, 14.6 us)
Async XLA Ops:
  7.2 0.9 copy-start
  7.2 147.2 %all-gather.3.cloned.1.call-start = ((), (), s32[]{:S(2)}) async-start(), calls=%async_computation.2 | async-start | bytes 4718592 | tf_op jit(solution)/shard_map/all_gather | solution.py:80
  14.6 6.8 %collective-permute-start = (bf16[64,512]{1,0:T(8,128)(2,1)S(1)}, bf16[64,512]{1,0:T(8,128)(2,1)S(1)}, u32[]{:S(2)}, u32[]{:S(2)}) collective-permute-start(bf16[64,512]{1,0:T(8,128)(2,1)S(1)} %fusion.88), channel_id=1, source_target_pairs={{0,8},{8,16},{16,24},{1,9},{9,17},{17,25},{2,10},{10,18},{18,26},{... | collective-permute-start | bytes 196616 | tf_op jit(solution)/shard_map/ppermute | solution.py:14
  19.5 245.3 %reduce-scatter.2.cloned.1.call-start = ((), (), s32[]{:S(2)}) async-start(), calls=%async_computation.1 | async-start | bytes 9437184 | tf_op jit(solution)/shard_map/reduce_scatter | solution.py:143
  22.5 12.0 %copy-start.9 = (f32[7,64,512]{2,1,0:T(8,128)S(1)}, f32[7,64,512]{2,1,0:T(8,128)}, u32[]{:S(2)}) copy-start(f32[7,64,512]{2,1,0:T(8,128)} %fusion.242) | copy-start | bytes 2752516
  22.5 12.1 %copy-start.2 = (bf16[1,2,512,2048]{3,2,1,0:T(8,128)(2,1)S(1)}, bf16[1,2,512,2048]{3,2,1,0:T(8,128)(2,1)}, u32[]{:S(2)}) copy-start(bf16[1,2,512,2048]{3,2,1,0:T(8,128)(2,1)} %param.10) | copy-start | bytes 12582916
  28.0 6.2 %collective-permute-start.1 = (bf16[64,512]{1,0:T(8,128)(2,1)S(1)}, bf16[64,512]{1,0:T(8,128)(2,1)S(1)}, u32[]{:S(2)}, u32[]{:S(2)}) collective-permute-start(bf16[64,512]{1,0:T(8,128)(2,1)S(1)} %fusion.85), channel_id=1, source_target_pairs={{0,8},{8,16},{16,24},{1,9},{9,17},{17,25},{2,10},{10,18},{18,26},{... | collective-permute-start | bytes 196616 | tf_op jit(solution)/shard_map/ppermute | solution.py:14
  35.9 7.5 %copy-start.14 = (f32[7,64,2048]{2,1,0:T(8,128)S(1)}, f32[7,64,2048]{2,1,0:T(8,128)}, u32[]{:S(2)}) copy-start(f32[7,64,2048]{2,1,0:T(8,128)} %get-tuple-element.40) | copy-start | bytes 11010052
  36.7 6.3 %collective-permute-start.2 = (bf16[64,512]{1,0:T(8,128)(2,1)S(1)}, bf16[64,512]{1,0:T(8,128)(2,1)S(1)}, u32[]{:S(2)}, u32[]{:S(2)}) collective-permute-start(bf16[64,512]{1,0:T(8,128)(2,1)S(1)} %fusion.82), channel_id=1, source_target_pairs={{0,8},{8,16},{16,24},{1,9},{9,17},{17,25},{2,10},{10,18},{18,26},{... | collective-permute-start | bytes 196616 | tf_op jit(solution)/shard_map/ppermute | solution.py:14
  44.7 7.1 %collective-permute-start.3 = (bf16[64,512]{1,0:T(8,128)(2,1)S(1)}, bf16[64,512]{1,0:T(8,128)(2,1)S(1)}, u32[]{:S(2)}, u32[]{:S(2)}) collective-permute-start(bf16[64,512]{1,0:T(8,128)(2,1)S(1)} %fusion.79), channel_id=1, source_target_pairs={{0,8},{8,16},{16,24},{1,9},{9,17},{17,25},{2,10},{10,18},{18,26},{... | collective-permute-start | bytes 196616 | tf_op jit(solution)/shard_map/ppermute | solution.py:14
  53.5 7.1 %collective-permute-start.4 = (bf16[64,512]{1,0:T(8,128)(2,1)S(1)}, bf16[64,512]{1,0:T(8,128)(2,1)S(1)}, u32[]{:S(2)}, u32[]{:S(2)}) collective-permute-start(bf16[64,512]{1,0:T(8,128)(2,1)S(1)} %fusion.76), channel_id=1, source_target_pairs={{0,8},{8,16},{16,24},{1,9},{9,17},{17,25},{2,10},{10,18},{18,26},{... | collective-permute-start | bytes 196616 | tf_op jit(solution)/shard_map/ppermute | solution.py:14
  59.0 2.0 copy-start.10
  61.6 6.1 %copy-start.11 = (bf16[7,64,512]{2,1,0:T(8,128)(2,1)S(1)}, bf16[7,64,512]{2,1,0:T(8,128)(2,1)}, u32[]{:S(2)}) copy-start(bf16[7,64,512]{2,1,0:T(8,128)(2,1)} %copy-done.10) | copy-start | bytes 1376260
  61.6 8.8 %copy-start.8 = (bf16[4,64,512]{2,1,0:T(8,128)(2,1)S(1)}, bf16[4,64,512]{2,1,0:T(8,128)(2,1)}, u32[]{:S(2)}) copy-start(bf16[4,64,512]{2,1,0:T(8,128)(2,1)} %param.15) | copy-start | bytes 786436
  62.3 7.1 %collective-permute-start.5 = (bf16[64,512]{1,0:T(8,128)(2,1)S(1)}, bf16[64,512]{1,0:T(8,128)(2,1)S(1)}, u32[]{:S(2)}, u32[]{:S(2)}) collective-permute-start(bf16[64,512]{1,0:T(8,128)(2,1)S(1)} %fusion.73), channel_id=1, source_target_pairs={{0,8},{8,16},{16,24},{1,9},{9,17},{17,25},{2,10},{10,18},{18,26},{... | collective-permute-start | bytes 196616 | tf_op jit(solution)/shard_map/ppermute | solution.py:14
  70.4 52.7 %copy-start.15 = (f32[7,64,2048]{2,1,0:T(8,128)}, f32[7,64,2048]{2,1,0:T(8,128)S(1)}, u32[]{:S(2)}) copy-start(f32[7,64,2048]{2,1,0:T(8,128)S(1)} %get-tuple-element.48) | copy-start | bytes 11010052
  72.1 7.4 %collective-permute-start.6 = (bf16[64,512]{1,0:T(8,128)(2,1)S(1)}, bf16[64,512]{1,0:T(8,128)(2,1)S(1)}, u32[]{:S(2)}, u32[]{:S(2)}) collective-permute-start(bf16[64,512]{1,0:T(8,128)(2,1)S(1)} %fusion.287), channel_id=1, source_target_pairs={{8,0},{16,8},{24,16},{9,1},{17,9},{25,17},{10,2},{18,10},{26,18},{... | collective-permute-start | bytes 196616 | tf_op jit(solution)/shard_map/ppermute | solution.py:14
  73.7 52.6 %copy-start.12 = (bf16[7,64,512]{2,1,0:T(8,128)(2,1)}, bf16[7,64,512]{2,1,0:T(8,128)(2,1)S(1)}, u32[]{:S(2)}) copy-start(bf16[7,64,512]{2,1,0:T(8,128)(2,1)S(1)} %constant_dynamic-update-slice_fusion) | copy-start | bytes 1376260
  83.9 7.4 %collective-permute-start.7 = (bf16[64,512]{1,0:T(8,128)(2,1)S(1)}, bf16[64,512]{1,0:T(8,128)(2,1)S(1)}, u32[]{:S(2)}, u32[]{:S(2)}) collective-permute-start(bf16[64,512]{1,0:T(8,128)(2,1)S(1)} %fusion.282), channel_id=1, source_target_pairs={{8,0},{16,8},{24,16},{9,1},{17,9},{25,17},{10,2},{18,10},{26,18},{... | collective-permute-start | bytes 196616 | tf_op jit(solution)/shard_map/ppermute | solution.py:14
  95.8 7.1 %collective-permute-start.8 = (bf16[64,512]{1,0:T(8,128)(2,1)S(1)}, bf16[64,512]{1,0:T(8,128)(2,1)S(1)}, u32[]{:S(2)}, u32[]{:S(2)}) collective-permute-start(bf16[64,512]{1,0:T(8,128)(2,1)S(1)} %fusion.277), channel_id=1, source_target_pairs={{8,0},{16,8},{24,16},{9,1},{17,9},{25,17},{10,2},{18,10},{26,18},{... | collective-permute-start | bytes 196616 | tf_op jit(solution)/shard_map/ppermute | solution.py:14
  107.3 7.1 %collective-permute-start.9 = (bf16[64,512]{1,0:T(8,128)(2,1)S(1)}, bf16[64,512]{1,0:T(8,128)(2,1)S(1)}, u32[]{:S(2)}, u32[]{:S(2)}) collective-permute-start(bf16[64,512]{1,0:T(8,128)(2,1)S(1)} %fusion.272), channel_id=1, source_target_pairs={{8,0},{16,8},{24,16},{9,1},{17,9},{25,17},{10,2},{18,10},{26,18},{... | collective-permute-start | bytes 196616 | tf_op jit(solution)/shard_map/ppermute | solution.py:14
  116.0 7.1 %collective-permute-start.10 = (bf16[64,512]{1,0:T(8,128)(2,1)S(1)}, bf16[64,512]{1,0:T(8,128)(2,1)S(1)}, u32[]{:S(2)}, u32[]{:S(2)}) collective-permute-start(bf16[64,512]{1,0:T(8,128)(2,1)S(1)} %fusion.267), channel_id=1, source_target_pairs={{8,0},{16,8},{24,16},{9,1},{17,9},{25,17},{10,2},{18,10},{26,18},{... | collective-permute-start | bytes 196616 | tf_op jit(solution)/shard_map/ppermute | solution.py:14
  124.8 7.1 %collective-permute-start.11 = (bf16[64,512]{1,0:T(8,128)(2,1)S(1)}, bf16[64,512]{1,0:T(8,128)(2,1)S(1)}, u32[]{:S(2)}, u32[]{:S(2)}) collective-permute-start(bf16[64,512]{1,0:T(8,128)(2,1)S(1)} %fusion.262), channel_id=1, source_target_pairs={{8,0},{16,8},{24,16},{9,1},{17,9},{25,17},{10,2},{18,10},{26,18},{... | collective-permute-start | bytes 196616 | tf_op jit(solution)/shard_map/ppermute | solution.py:14
  172.1 3.6 %copy-start.3 = (bf16[1,1,2,512,2048]{4,3,2,1,0:T(8,128)(2,1)S(1)}, bf16[1,1,2,512,2048]{4,3,2,1,0:T(8,128)(2,1)}, u32[]{:S(2)}) copy-start(bf16[1,1,2,512,2048]{4,3,2,1,0:T(8,128)(2,1)} %param.13) | copy-start | bytes 12582916
  172.1 4.7 %copy-start.4 = (f32[512,2048]{1,0:T(8,128)S(1)}, f32[512,2048]{1,0:T(8,128)}, u32[]{:S(2)}) copy-start(f32[512,2048]{1,0:T(8,128)} %select_add_fusion) | copy-start | bytes 12582916
  172.2 5.9 %copy-start.5 = (f32[512,2048]{1,0:T(8,128)S(1)}, f32[512,2048]{1,0:T(8,128)}, u32[]{:S(2)}) copy-start(f32[512,2048]{1,0:T(8,128)} %select_add_fusion.1) | copy-start | bytes 12582916
  178.1 86.8 %copy-start.6 = (f32[1,128,2048]{2,1,0:T(8,128)S(1)}, f32[1,128,2048]{2,1,0:T(8,128)}, u32[]{:S(2)}) copy-start(f32[1,128,2048]{2,1,0:T(8,128)} %param.14) | copy-start | bytes 3145732
  178.1 94.6 %copy-start.1 = (bf16[128,512]{1,0:T(8,128)(2,1)S(1)}, bf16[128,512]{1,0:T(8,128)(2,1)}, u32[]{:S(2)}) copy-start(bf16[128,512]{1,0:T(8,128)(2,1)} %param.9) | copy-start | bytes 393220
  182.1 87.9 %copy-start.13 = (bf16[1,128,2048]{2,1,0:T(8,128)(2,1)S(1)}, bf16[1,128,2048]{2,1,0:T(8,128)(2,1)}, u32[]{:S(2)}) copy-start(bf16[1,128,2048]{2,1,0:T(8,128)(2,1)} %param.11) | copy-start | bytes 1572868
  270.1 2.6 copy-start.7
Sparse Core Ops, SparseCore 0:
  19.7 47.1 all-gather.2
  172.3 92.5 reduce-scatter.1
where the time goes:
time: 280 us; the launch traced here: 279 us
  waiting for transfers between devices  114 us (41%)
  matrix products  62.2 us (22%)
  other arithmetic  46.9 us (17%)
  starting transfers between devices  37.3 us (13%)
  between operations  16.3 us (6%)
  local copies, waits for them, and re-layouts  3.27 us (1%)
    reduce_scatter x1, waiting for transfers between devices, local(): lax.psum_scatter(flat.astype(jnp.float32), 'dp', scatter_dimension=0, til...  82.7 us
    ppermute x12, starting transfers between devices, passed_along(): return lax.ppermute(array, axis, pairs)  37.2 us
    dot_general x14, matrix products, row_product(): lax.dot_general(left, right, (((0,), (0,)), ((), ())), preferred_element_...  34.6 us
    ppermute x12, waiting for transfers between devices, passed_along(): return lax.ppermute(array, axis, pairs)  30.8 us
    dot_general x7, matrix products, forward_block(): upper = jnp.dot(normed_b, first_matrix, preferred_element_type=jnp.float32)  9.4 us
    convert_element_type x1, other arithmetic, local(): flat.astype(jnp.float32)  9.37 us
    mul x1, other arithmetic, local(): 0.1 * gradient  8.49 us
    dot_general x6, matrix products, forward_block(): lax.dot_general(hidden, second_matrix, (((1,), (1,)), ((), ())), preferre...  7.88 us
  transfers between devices with their start and end apart: 14, of which 13 were waited for; matrix products, arithmetic and copies ran while one was open for 28% of the time, Pallas kernels for 0%

commit v1 on v0

v1 whole, which is shorter than its diff:
```python
import math

import jax
import jax.numpy as jnp
from jax import lax
from jax.experimental import pallas as pl
from jax.experimental.pallas import tpu as pltpu
from jax.sharding import PartitionSpec as P


gelu_coef = math.sqrt(2.0 / math.pi)
bf16, f32 = jnp.bfloat16, jnp.float32
whole = pl.BlockSpec(memory_space=pltpu.VMEM)
scalars = pl.BlockSpec(memory_space=pltpu.SMEM)


def held(array):
    return pltpu.with_memory_space_constraint(array, pltpu.VMEM)


def call(kernel, outs, scalar_args, arrays, aliases=None, limit=8, flops=0, transcendentals=0):
    moved = sum(math.prod(a.shape) * a.dtype.itemsize for a in arrays)
    return pl.pallas_call(
        kernel,
        out_shape=[pltpu.VMEM(shape, dtype) for shape, dtype in outs],
        in_specs=[scalars] * len(scalar_args) + [whole] * len(arrays),
        out_specs=[whole] * len(outs),
        input_output_aliases={len(scalar_args) + i: o for i, o in (aliases or {}).items()},
        compiler_params=pltpu.CompilerParams(vmem_limit_bytes=limit << 20),
        cost_estimate=pl.CostEstimate(flops=flops, bytes_accessed=moved, transcendentals=transcendentals),
    )(*scalar_args, *[held(a) for a in arrays])


def across(left, right):
    return lax.dot_general(left, right, (((1,), (1,)), ((), ())), preferred_element_type=f32)


def down(left, right):
    return lax.dot_general(left, right, (((0,), (0,)), ((), ())), preferred_element_type=f32)


def normalize(inputs):
    values = inputs.astype(f32)
    center = jnp.mean(values, axis=-1, keepdims=True)
    shifted = values - center
    scaled = lax.rsqrt(jnp.mean(shifted * shifted, axis=-1, keepdims=True) + 1e-05)
    return shifted * scaled, scaled


def embed_rows(token_ids, embed):
    micro, rows = token_ids.shape
    vocab, width = embed.shape

    def kernel(ids_ref, embed_ref, out_ref):
        for m in range(micro):
            ids = ids_ref[m : m + 1, :]
            hot = (lax.broadcasted_iota(jnp.int32, (vocab, rows), 0) == ids).astype(f32).astype(bf16)
            out_ref[m * rows : (m + 1) * rows, :] = down(hot, embed_ref[...]).astype(bf16)

    return call(kernel, [((micro * rows, width), bf16)], [], [token_ids, embed])[0]


slabs = 2


def spot_of(where_ref, turn, tokens):
    return jnp.where(where_ref[7] == turn, 0, tokens)


def rows_of(ref, chunk, rows):
    return ref[...] if ref.shape[0] == rows else ref[chunk * rows : (chunk + 1) * rows, :]


def forward(where, turn, inputs, weights, saved, chunk, rows, tokens):
    width = inputs.shape[1]
    channels = weights.shape[2]
    step = channels // slabs
    outs = [((rows, width), bf16)] + [
        ((2 * tokens, width), bf16),
        ((2 * tokens, width), bf16),
        ((2 * tokens, channels), bf16),
        ((2 * tokens, channels), f32),
    ]

    def kernel(where_ref, x_ref, w_ref, *refs):
        out_ref, x_out, normed_out, hidden_out, slope_out = refs[-5:]
        place = pl.ds(pl.multiple_of(spot_of(where_ref, turn, tokens) + chunk * rows, rows), rows)
        inputs = rows_of(x_ref, chunk, rows)
        normed_b = normalize(inputs)[0].astype(bf16)
        x_out[place, :] = inputs
        normed_out[place, :] = normed_b
        total = inputs.astype(f32)
        for i in range(slabs):
            part = pl.ds(i * step, step)
            upper = jnp.dot(normed_b, w_ref[0, :, part], preferred_element_type=f32)
            square = upper * upper
            bent = jnp.tanh(gelu_coef * upper * (1.0 + 0.044715 * square))
            half = 0.5 + 0.5 * bent
            hidden = (upper * half).astype(bf16)
            hidden_out[place, part] = hidden
            slope_out[place, part] = half + 0.5 * upper * (1.0 - bent * bent) * (
                gelu_coef * (1.0 + 3.0 * 0.044715 * square)
            )
            total = total + across(hidden, w_ref[1, :, part])
        out_ref[...] = total.astype(bf16)

    got = call(
        kernel,
        outs,
        [where],
        [inputs, weights, *saved],
        {2 + i: 1 + i for i in range(len(saved))},
        flops=4 * rows * width * channels,
        transcendentals=rows * channels,
    )
    return got[0], got[1:]


def backward(where, turn, grad, weights, saved, kept, chunk, rows, tokens, last):
    width = grad.shape[1]
    channels = weights.shape[2]
    step = channels // slabs
    outs = [((2 * tokens, width), bf16), ((2 * tokens, channels), bf16)]
    if not last:
        outs = outs + [((rows, width), bf16)]

    def kernel(where_ref, grad_ref, w_ref, x_ref, slope_ref, *refs):
        refs = refs[len(kept) :]
        grad_out, upper_out = refs[:2]
        place = pl.ds(pl.multiple_of(spot_of(where_ref, turn, tokens) + chunk * rows, rows), rows)
        here = pl.ds(chunk * rows, rows)
        grad = rows_of(grad_ref, chunk, rows)
        grad_out[place, :] = grad
        total = jnp.zeros((rows, width), f32)
        for i in range(slabs):
            part = pl.ds(i * step, step)
            back_hidden = jnp.dot(grad, w_ref[1, :, part], preferred_element_type=f32)
            back_upper = (back_hidden * slope_ref[here, part]).astype(bf16)
            upper_out[place, part] = back_upper
            if not last:
                total = total + across(back_upper, w_ref[0, :, part])
        if not last:
            normed, scaled = normalize(x_ref[here, :])
            first = jnp.mean(total, axis=-1, keepdims=True)
            second = jnp.mean(total * normed, axis=-1, keepdims=True)
            refs[2][...] = (grad.astype(f32) + scaled * (total - first - normed * second)).astype(bf16)

    got = call(
        kernel,
        outs,
        [where],
        [grad, weights, *saved, *kept],
        {4 + i: i for i in range(len(kept))},
        flops=(2 if last else 4) * rows * width * channels,
    )
    return (None if last else got[2]), got[:2]


def relay(where, token_ids, embed, weights, cotangent, between):
    count = lax.axis_size("section")
    micro, per_micro = token_ids.shape
    tokens = micro * per_micro
    chunks = 2 if micro % 2 == 0 else 1
    rows = tokens // chunks
    width = embed.shape[1]
    state = [embed_rows(token_ids, embed)] * chunks
    grads = [cotangent.reshape(tokens, width)] * chunks
    saved, kept = [], []

    def passed(array, source, target):
        return lax.ppermute(array, "section", [(source, target)])

    def back(hop, c):
        nonlocal kept
        out, kept = backward(where, hop, grads[c], weights, [saved[0], saved[3]], kept, c, rows, tokens, hop == 0)
        if hop:
            grads[c] = passed(out, hop, hop - 1)

    for hop in range(count):
        for c in range(chunks):
            out, saved = forward(where, hop, state[c], weights, saved, c, rows, tokens)
            if hop + 1 < count:
                state[c] = passed(out, hop, hop + 1)
            else:
                back(hop, c)
        between(hop)
    for hop in range(count - 2, -1, -1):
        for c in range(chunks):
            back(hop, c)
        between(2 * count - 2 - hop)
    return saved[1], saved[2], kept[0], kept[1]


def along(array, pairs):
    return lax.ppermute(array, "dp", [(2 * a + c, 2 * b + c) for a, b in pairs for c in (0, 1)])


def swapped(array):
    return lax.ppermute(array, "dp", [(i, i ^ 1) for i in range(lax.axis_size("dp"))])


def known_mine(where, error, known, parts):
    owned, channels = parts[0][1].shape

    def kernel(where_ref, error_ref, *refs):
        known_out, pass_out = refs[-2:]
        refs = refs[len(known) : -2]
        z, core = where_ref[0], where_ref[1]
        for (by, _, slot), ref in zip(parts, refs):

            def fill(ref=ref, by=by, slot=slot):
                rows = pl.ds(pl.multiple_of((2 * (z + by) + core) * owned, owned), owned)
                values = ref[...]
                pass_out[slot(z)] = values
                known_out[0, z + by] = 0.9 * values.astype(f32) + error_ref[rows, :].astype(f32)

            pl.when(jnp.logical_and(z + by >= 0, z + by < 4))(fill)

    return call(
        kernel,
        [((2, 4, owned, channels), f32), ((2, owned, channels), bf16)],
        [where],
        [error, *known, *[a for _, a, _ in parts]],
        {1: 0} if known else {},
        transcendentals=0,
    )


def known_other(where, error, known, first, second):
    owned, _ = first.shape[1:]

    def kernel(where_ref, error_ref, known_ref, first_ref, second_ref, out_ref):
        z, other = where_ref[0], 1 - where_ref[1]
        two_off = jnp.where(z < 2, z + 2, z - 2)
        one_off = z ^ 1
        last = 3 - z
        for chip, ref, slot in ((z, first_ref, 0), (two_off, first_ref, 1), (one_off, second_ref, 0), (last, second_ref, 1)):
            rows = pl.ds(pl.multiple_of((2 * chip + other) * owned, owned), owned)
            out_ref[1, chip] = 0.9 * ref[slot].astype(f32) + error_ref[rows, :].astype(f32)

    return call(kernel, [(known.shape, f32)], [where], [error, known, first, second], {1: 0})[0]


def add_gradient(where, known, normed, upper, grad, hidden, width):
    _, _, owned, channels = known.shape
    tokens = normed.shape[0] // 2

    def kernel(where_ref, known_ref, normed_ref, upper_ref, grad_ref, hidden_ref, out_ref, sum_ref):
        core = where_ref[1]
        total = jnp.zeros((8, channels), f32)
        for side in (0, 1):
            parity = core if side == 0 else 1 - core
            for z in range(4):
                first = 2 * z < width // owned
                left, right = (normed_ref, upper_ref) if first else (grad_ref, hidden_ref)
                column = (2 * z + parity) * owned - (0 if first else width)
                part = left[0:tokens, pl.ds(pl.multiple_of(column, owned), owned)]
                combined = known_ref[side, z] + 0.1 * down(part, right[0:tokens, :])
                out_ref[side, z] = combined
                total = total + jnp.sum((combined * combined).reshape(owned // 8, 8, channels), axis=0)
        sum_ref[0, 0] = jnp.sum(total)

    return pl.pallas_call(
        kernel,
        out_shape=[pltpu.VMEM(known.shape, f32), jax.ShapeDtypeStruct((1, 1), f32)],
        in_specs=[scalars] + [whole] * 5,
        out_specs=[whole, scalars],
        input_output_aliases={1: 0},
        compiler_params=pltpu.CompilerParams(vmem_limit_bytes=8 << 20),
        cost_estimate=pl.CostEstimate(
            flops=2 * 8 * owned * tokens * channels, bytes_accessed=16 * 8 * owned * channels, transcendentals=0
        ),
        name="add_gradient",
    )(where, *[held(a) for a in (known, normed, upper, grad, hidden)])


def scale_of(sum_ref, count):
    scale = jnp.sqrt(jnp.full((8, 128), sum_ref[0, 0], f32) * (1.0 / count) + 0.01)[0:1, 0:1]
    return scale, 1.0 / scale


def packed_part(where, sums, combined, places):
    _, _, owned, channels = combined.shape
    count = 8 * owned * channels

    def kernel(where_ref, sum_ref, combined_ref, *outs):
        scale, inverse = scale_of(sum_ref, count)
        for i, place in enumerate(places):
            for side in (1, 0):
                values = combined_ref[side, where_ref[2 + place]]
                outs[2 * i + 1 - side][...] = (scale * jnp.tanh(values * inverse)).astype(bf16)

    return call(
        kernel,
        [((owned, channels), bf16)] * (2 * len(places)),
        [where, sums],
        [combined],
        transcendentals=2 * len(places) * owned * channels,
    )


def fresh_worker(where, sums, combined):
    _, _, owned, channels = combined.shape
    count = 8 * owned * channels

    def kernel(where_ref, sum_ref, combined_ref, out_ref):
        core = where_ref[1]
        scale, inverse = scale_of(sum_ref, count)
        for side in (0, 1):
            parity = core if side == 0 else 1 - core
            for z in range(4):
                values = combined_ref[side, z]
                packed = (scale * jnp.tanh(values * inverse)).astype(bf16)
                rows = pl.ds(pl.multiple_of((2 * z + parity) * owned, owned), owned)
                out_ref[rows, :] = (values - packed.astype(f32)).astype(bf16)

    return call(kernel, [((8 * owned, channels), bf16)], [where, sums], [combined], transcendentals=count)[0]


def added(*arrays):
    def kernel(*refs):
        total = refs[0][...].astype(f32)
        for ref in refs[1:-1]:
            total = total + ref[...].astype(f32)
        refs[-1][...] = total.astype(bf16)

    return call(kernel, [(arrays[0].shape, bf16)], [], list(arrays))[0]


def server(where, parts, error, variance, weights, replicas):
    owned, channels = error.shape
    width = weights.shape[1]

    def kernel(where_ref, error_ref, variance_ref, weights_ref, *refs):
        parts, (weights_out, momentum_out, error_out) = refs[:-3], refs[-3:]
        total = parts[0][...].astype(f32)
        for ref in parts[1:]:
            total = total + ref[...].astype(f32)
        merged = total * (1.0 / replicas) + error_ref[...]
        squares = jnp.sum((merged * merged).reshape(owned // 8, 8, channels), axis=0)
        mean = jnp.sum(squares, axis=(0, 1), keepdims=True) * (1.0 / (owned * channels))
        scale = jnp.sqrt(mean + 0.01)
        values = (scale * jnp.tanh(merged * (1.0 / scale))).astype(bf16)
        momentum_out[...] = values
        wide = values.astype(f32)
        error_out[...] = merged - wide
        start = where_ref[6]
        rows = pl.ds(pl.multiple_of(lax.rem(start, width), owned), owned)
        own = weights_ref[start // width, rows, :].astype(f32)
        step = 0.01 * wide / (jnp.sqrt(variance_ref[...].astype(f32)) + 1e-08)
        weights_out[...] = (own - step).astype(bf16)

    shape = (owned, channels)
    return call(
        kernel,
        [(shape, bf16), (shape, bf16), (shape, f32)],
        [where],
        [error, variance, weights, *parts],
        transcendentals=3 * owned * channels,
    )


def on_a_line(where, token_ids, embed, weights, variance, momentum, error, server_error, cotangent):
    replicas = lax.axis_size("dp")
    width = weights.shape[1]
    far_down, far_up = [(0, 2), (1, 3)], [(3, 1), (2, 0)]
    f2 = along(momentum, far_down)
    r2 = along(momentum, far_up)
    f3 = along(momentum, [(0, 3)])
    r3 = along(momentum, [(3, 0)])
    f1 = along(momentum, [(0, 1), (1, 2), (2, 3)])
    r1 = along(momentum, [(3, 2), (2, 1), (1, 0)])
    known, out_a = known_mine(
        where, error, [], [(0, momentum, lambda z: 0), (-2, f2, lambda z: 1), (2, r2, lambda z: 1)]
    )
    in_a = swapped(out_a)
    known, out_b = known_mine(
        where,
        error,
        [known],
        [
            (-1, f1, lambda z: jnp.where(z == 2, 1, 0)),
            (1, r1, lambda z: jnp.where(z == 1, 1, 0)),
            (-3, f3, lambda z: 1),
            (3, r3, lambda z: 1),
        ],
    )
    in_b = swapped(out_b)
    normed, hidden, grad, upper = relay(where, token_ids, embed, weights, cotangent, lambda hop: None)
    known = known_other(where, error, known, in_a, in_b)
    combined, sums = add_gradient(where, known, normed, upper, grad, hidden, width)
    far_out, far = packed_part(where, sums, combined, (0,))
    far_in = swapped(far_out)
    mid_out, mid, near_out, near, own_out, own = packed_part(where, sums, combined, (1, 2, 3))
    mid_in = swapped(mid_out)
    near_in = swapped(near_out)
    own_in = swapped(own_out)
    ends, inner, outer = [(0, 1), (3, 2)], [(1, 2), (2, 1)], [(2, 3), (1, 0)]
    a1 = along(added(far, far_in), ends)
    a2 = along(added(mid, mid_in), ends)
    a3 = along(added(near, near_in), ends)
    b2 = along(added(far, far_in, a1), inner)
    b3 = along(added(mid, mid_in, a2), inner)
    c3 = along(added(near, near_in, b2), outer)
    new_worker = fresh_worker(where, sums, combined)
    new_weights, new_momentum, new_server = server(
        where, [own, own_in, a3, b3, c3], server_error, variance, weights, replicas
    )
    return new_weights, new_momentum, new_worker, new_server


def in_general(where, token_ids, embed, weights, variance, momentum, error, server_error, cotangent):
    replicas = lax.axis_size("dp")
    width, channels = weights.shape[1:]
    owned = 2 * width // replicas
    tokens = token_ids.shape[0] * token_ids.shape[1]
    shared = lax.all_gather(momentum, "dp", axis=0, tiled=True)
    normed, hidden, grad, upper = relay(where, token_ids, embed, weights, cotangent, lambda hop: None)
    gradient = jnp.concatenate(
        [down(normed[:tokens], upper[:tokens]), down(grad[:tokens], hidden[:tokens])], axis=0
    )
    combined = 0.9 * shared.astype(f32) + 0.1 * gradient + error.astype(f32)
    worker_scale = jnp.sqrt(jnp.mean(combined * combined) + 0.01)
    packed = (worker_scale * jnp.tanh(combined / worker_scale)).astype(bf16)
    new_worker = (combined - packed.astype(f32)).astype(bf16)
    total = lax.psum_scatter(packed.astype(f32), "dp", scatter_dimension=0, tiled=True)
    merged = total / replicas + server_error
    server_scale = jnp.sqrt(jnp.mean(merged * merged) + 0.01)
    values = (server_scale * jnp.tanh(merged / server_scale)).astype(bf16)
    wide = values.astype(f32)
    start = lax.axis_index("dp") * owned
    own = lax.dynamic_slice_in_dim(weights.reshape(2 * width, channels), start, owned, 0)
    step = 0.01 * wide / (jnp.sqrt(variance.astype(f32)) + 1e-08)
    return (own.astype(f32) - step).astype(bf16), values, new_worker, merged - wide


def local(token_ids, embed, weights, variance, momentum, worker_error, server_error, cotangent):
    _, _, width, channels = weights.shape
    replicas = lax.axis_size("dp")
    rank = lax.axis_index("dp")
    z = rank // 2
    upper_half = z >= 2
    order = [jnp.where(upper_half, 0, 3), jnp.where(upper_half, 1, 2), z ^ 1, z]
    start = rank * (2 * width // replicas)
    where = jnp.stack([z, rank % 2, *order, start, lax.axis_index("section")]).astype(jnp.int32)
    plan = on_a_line if replicas == 8 else in_general
    new_weights, values, new_worker, new_server = plan(
        where,
        token_ids,
        embed,
        weights[0],
        variance[0],
        momentum[0],
        worker_error.reshape(2 * width, channels),
        server_error[0],
        cotangent,
    )
    return new_weights[None], values[None], new_worker.reshape(worker_error.shape), new_server[None]


def solution(mesh):
    in_specs = (
        P(None, "dp"),
        P(),
        P("section", None, None, None),
        P("section", "dp", None),
        P("section", "dp", None),
        P("section", "dp", None, None, None),
        P("section", "dp", None),
        P(None, "dp", None),
    )
    out_specs = (
        P("section", "dp", None),
        P("section", "dp", None),
        P("section", "dp", None, None, None),
        P("section", "dp", None),
    )
    return jax.shard_map(local, mesh=mesh, in_specs=in_specs, out_specs=out_specs, check_vma=False)
```

time: 280 us -> 169 us (0.60)
  matrix products: 62.2 us -> 0 us
  waiting for transfers between devices: 114 us -> 52.6 us
  Pallas kernels: 0 us -> 49.6 us
  other arithmetic: 46.9 us -> 0 us
  starting transfers between devices: 37.3 us -> 55.7 us
  between operations: 16.3 us -> 1.28 us
  local copies, waits for them, and re-layouts: 3.27 us -> 9.16 us
    reduce_scatter x1 -> x0, waiting for transfers between devices: 82.7 us -> none  [local(): lax.psum_scatter(flat.astype(jnp.float32), 'dp', scatter_dimension=0, til...]
    dot_general x40 -> x0, matrix products: 62.2 us -> none  [the longest x14 34.6 us: row_product(): lax.dot_general(left, right, (((0,), (0,)), ((), ())), preferred_element_...]
    pallas_call x0 -> x31, Pallas kernels: none -> 49.6 us  [the longest x30 45.1 us: call(): pl.pallas_call(kernel, out_shape=[pltpu.VMEM(shape, dtype) for shape, dty...]
    ppermute x12 -> x30, waiting for transfers between devices: 30.8 us -> 52.6 us  [the longest x12 36.8 us: along(): lax.ppermute(array, 'dp', [(2 * a + c, 2 * b + c) for a, b in pairs for c...]
    ppermute x12 -> x30, starting transfers between devices: 37.2 us -> 55.7 us  [the longest x12 41.4 us: along(): lax.ppermute(array, 'dp', [(2 * a + c, 2 * b + c) for a, b in pairs for c...]
    convert_element_type x8 -> x0, other arithmetic: 14.1 us -> none  [the longest x1 9.37 us: local(): flat.astype(jnp.float32)]
    mul x2 -> x0, other arithmetic: 12 us -> none  [the longest x1 8.49 us: local(): 0.1 * gradient]
    reduce_sum x16 -> x0, other arithmetic: 11.8 us -> none  [the longest x1 7.61 us: local(): worker_scale = jnp.sqrt(jnp.mean(combined * combined) + 0.01)]
  transfers between devices with their start and end apart: 14 -> 30, of which waited for: 13 -> 8; matrix products, arithmetic and copies ran while one was open for 28% -> 1% of each run, Pallas kernels for 0% -> 24%
where the time goes in v1:
time: 169 us; the launch traced here: 168 us
  starting transfers between devices  55.7 us (33%)
  waiting for transfers between devices  52.6 us (31%)
  Pallas kernels  49.6 us (29%)
  local copies, waits for them, and re-layouts  9.16 us (5%)
    pallas_call x30, Pallas kernels, call(): pl.pallas_call(kernel, out_shape=[pltpu.VMEM(shape, dtype) for shape, dty...  45.1 us
    ppermute x12, starting transfers between devices, along(): lax.ppermute(array, 'dp', [(2 * a + c, 2 * b + c) for a, b in pairs for c...  41.4 us
    ppermute x12, waiting for transfers between devices, along(): lax.ppermute(array, 'dp', [(2 * a + c, 2 * b + c) for a, b in pairs for c...  36.8 us
    ppermute x12, waiting for transfers between devices, passed(): return lax.ppermute(array, 'section', [(source, target)])  15.8 us
    ppermute x12, starting transfers between devices, passed(): return lax.ppermute(array, 'section', [(source, target)])  13 us
    unnamed x22, local copies, waits for them, and re-layouts  9.07 us
    pallas_call x1, Pallas kernels, add_gradient(): pl.pallas_call(kernel, out_shape=[pltpu.VMEM(known.shape, f32), jax.Shape...  4.55 us
  transfers between devices with their start and end apart: 30, of which 8 were waited for; matrix products, arithmetic and copies ran while one was open for 1% of the time, Pallas kernels for 24%

profile of v1, /device:TPU:0, one launch (start us, length us, event | category | flops | bytes accessed | tf_op | source)
XLA Modules:
  0.0 168.4 jit_solution(3427894347520788053)
XLA Ops:
  0.6 6.0 %collective-permute-start = (bf16[128,2048]{1,0:T(8,128)(2,1)}, bf16[128,2048]{1,0:T(8,128)(2,1)S(1)}, u32[]{:S(2)}, u32[]{:S(2)}) collective-permute-start(bf16[128,2048]{1,0:T(8,128)(2,1)} %bitcast.44), channel_id=1, source_target_pairs={{0,4},{1,5},{2,6},{3,7},{8,12},{9,13},{10,14},{11,15},{16,20},{17,... | collective-permute-start | bytes 1572872 | tf_op jit(solution)/shard_map/ppermute | solution.py:195
  6.6 1.3 collective-permute-start.1
  7.9 3.5 %collective-permute-start.2 = (bf16[128,2048]{1,0:T(8,128)(2,1)}, bf16[128,2048]{1,0:T(8,128)(2,1)S(1)}, u32[]{:S(2)}, u32[]{:S(2)}) collective-permute-start(bf16[128,2048]{1,0:T(8,128)(2,1)} %bitcast.46), channel_id=1, source_target_pairs={{0,2},{1,3},{2,4},{3,5},{4,6},{5,7},{8,10},{9,11},{10,12},{11,13},... | collective-permute-start | bytes 1572872 | tf_op jit(solution)/shard_map/ppermute | solution.py:195
  11.5 1.3 collective-permute-start.3
  12.8 7.6 %collective-permute-start.4 = (bf16[128,2048]{1,0:T(8,128)(2,1)}, bf16[128,2048]{1,0:T(8,128)(2,1)S(1)}, u32[]{:S(2)}, u32[]{:S(2)}) collective-permute-start(bf16[128,2048]{1,0:T(8,128)(2,1)} %bitcast.48), channel_id=1, source_target_pairs={{0,6},{1,7},{8,14},{9,15},{16,22},{17,23},{24,30},{25,31}} | collective-permute-start | bytes 1572872 | tf_op jit(solution)/shard_map/ppermute | solution.py:195
  20.4 1.3 collective-permute-start.5
  21.7 0.9 copy-done.7
  22.6 0.7 copy-done.8
  23.6 2.2 %copy-done = bf16[1,2,512,2048]{3,2,1,0:T(8,128)(2,1)S(1)} copy-done((bf16[1,2,512,2048]{3,2,1,0:T(8,128)(2,1)S(1)}, bf16[1,2,512,2048]{3,2,1,0:T(8,128)(2,1)}, u32[]{:S(2)}) %copy-start) | copy-done | bytes 4194328
  25.8 2.2 %shard_map.115 = (bf16[128,512]{1,0:T(8,128)(2,1)S(1)}, bf16[512,512]{1,0:T(8,128)(2,1)S(1)}, bf16[512,512]{1,0:T(8,128)(2,1)S(1)}, bf16[512,2048]{1,0:T(8,128)(2,1)S(1)}, f32[512,2048]{1,0:T(8,128)S(1)}) custom-call(s32[8]{0:T(128)S(1)} %stack.32.where_ref, bf16[256,512]{1,0:T(8,128)(2,1)S(1)} %shard_map.114.x_ref, bf16[2,512,2048]{2,1,0:T(8,128)(2,1)S(1)} %bitcast.21), custom_call_target="tpu_custom_call" | custom-call | flops 536870912 | bytes 4456448 | tf_op jit(solution)/shard_map/pallas_call | solution.py:23
  28.1 7.3 %collective-permute-done.1.refs_2_ = bf16[128,2048]{1,0:T(8,128)(2,1)S(1)} collective-permute-done((bf16[128,2048]{1,0:T(8,128)(2,1)}, bf16[128,2048]{1,0:T(8,128)(2,1)S(1)}, u32[]{:S(2)}, u32[]{:S(2)}) %collective-permute-start.1) | collective-permute-done | bytes 524320 | tf_op jit(solution)/shard_map/ppermute | solution.py:195
  35.4 3.4 %collective-permute-start.9 = (bf16[128,512]{1,0:T(8,128)(2,1)S(1)}, bf16[128,512]{1,0:T(8,128)(2,1)S(1)}, u32[]{:S(2)}, u32[]{:S(2)}) collective-permute-start(bf16[128,512]{1,0:T(8,128)(2,1)S(1)} %get-tuple-element.90), channel_id=1, source_target_pairs={{0,8},{1,9},{2,10},{3,11},{4,12},{5,13},{6,14},{7,15}} | collective-permute-start | bytes 393224 | tf_op jit(solution)/shard_map/ppermute | solution.py:171
  38.8 2.3 %shard_map.116 = (bf16[128,512]{1,0:T(8,128)(2,1)S(1)}, bf16[512,512]{1,0:T(8,128)(2,1)S(1)}, bf16[512,512]{1,0:T(8,128)(2,1)S(1)}, bf16[512,2048]{1,0:T(8,128)(2,1)S(1)}, f32[512,2048]{1,0:T(8,128)S(1)}) custom-call(s32[8]{0:T(128)S(1)} %stack.32.where_ref, ...), custom_call_target="tpu_custom_call", output_to_operand_aliasing={{1}: (3, {}), {2}: (4, {}), {3}: (5, {}), {4}: (6, {})} | custom-call | flops 536870912 | bytes 11796480 | tf_op jit(solution)/shard_map/pallas_call | solution.py:23
  41.1 1.3 collective-permute-start.8
  42.4 0.9 shard_map.111
  43.4 5.2 %collective-permute-done.3.refs_2_ = bf16[128,2048]{1,0:T(8,128)(2,1)S(1)} collective-permute-done((bf16[128,2048]{1,0:T(8,128)(2,1)}, bf16[128,2048]{1,0:T(8,128)(2,1)S(1)}, u32[]{:S(2)}, u32[]{:S(2)}) %collective-permute-start.3) | collective-permute-done | bytes 524320 | tf_op jit(solution)/shard_map/ppermute | solution.py:195
  48.6 0.9 shard_map.112
  50.1 0.7 copy-done.1
  50.8 2.2 %shard_map.117 = (bf16[128,512]{1,0:T(8,128)(2,1)S(1)}, bf16[512,512]{1,0:T(8,128)(2,1)S(1)}, bf16[512,512]{1,0:T(8,128)(2,1)S(1)}, bf16[512,2048]{1,0:T(8,128)(2,1)S(1)}, f32[512,2048]{1,0:T(8,128)S(1)}) custom-call(s32[8]{0:T(128)S(1)} %stack.32.where_ref, ...), custom_call_target="tpu_custom_call", output_to_operand_aliasing={{1}: (3, {}), {2}: (4, {}), {3}: (5, {}), {4}: (6, {})} | custom-call | flops 536870912 | bytes 11665408 | tf_op jit(solution)/shard_map/pallas_call | solution.py:23
  53.0 0.7 collective-permute-start.11
  53.7 2.2 %shard_map.118 = (bf16[128,512]{1,0:T(8,128)(2,1)S(1)}, bf16[512,512]{1,0:T(8,128)(2,1)S(1)}, bf16[512,512]{1,0:T(8,128)(2,1)S(1)}, bf16[512,2048]{1,0:T(8,128)(2,1)S(1)}, f32[512,2048]{1,0:T(8,128)S(1)}) custom-call(s32[8]{0:T(128)S(1)} %stack.32.where_ref, ...), custom_call_target="tpu_custom_call", output_to_operand_aliasing={{1}: (3, {}), {2}: (4, {}), {3}: (5, {}), {4}: (6, {})} | custom-call | flops 536870912 | bytes 11665408 | tf_op jit(solution)/shard_map/pallas_call | solution.py:23
  55.9 0.7 collective-permute-start.10
  56.6 2.3 %shard_map.119 = (bf16[128,512]{1,0:T(8,128)(2,1)S(1)}, bf16[512,512]{1,0:T(8,128)(2,1)S(1)}, bf16[512,512]{1,0:T(8,128)(2,1)S(1)}, bf16[512,2048]{1,0:T(8,128)(2,1)S(1)}, f32[512,2048]{1,0:T(8,128)S(1)}) custom-call(s32[8]{0:T(128)S(1)} %stack.32.where_ref, ...), custom_call_target="tpu_custom_call", output_to_operand_aliasing={{1}: (3, {}), {2}: (4, {}), {3}: (5, {}), {4}: (6, {})} | custom-call | flops 536870912 | bytes 11665408 | tf_op jit(solution)/shard_map/pallas_call | solution.py:23
  58.9 0.7 collective-permute-start.13
  59.6 2.2 %shard_map.120 = (bf16[128,512]{1,0:T(8,128)(2,1)S(1)}, bf16[512,512]{1,0:T(8,128)(2,1)S(1)}, bf16[512,512]{1,0:T(8,128)(2,1)S(1)}, bf16[512,2048]{1,0:T(8,128)(2,1)S(1)}, f32[512,2048]{1,0:T(8,128)S(1)}) custom-call(s32[8]{0:T(128)S(1)} %stack.32.where_ref, ...), custom_call_target="tpu_custom_call", output_to_operand_aliasing={{1}: (3, {}), {2}: (4, {}), {3}: (5, {}), {4}: (6, {})} | custom-call | flops 536870912 | bytes 11665408 | tf_op jit(solution)/shard_map/pallas_call | solution.py:23
  61.8 0.8 collective-permute-start.12
  62.7 2.9 %shard_map.121 = (bf16[128,512]{1,0:T(8,128)(2,1)}, bf16[512,512]{1,0:T(8,128)(2,1)S(1)}, bf16[512,512]{1,0:T(8,128)(2,1)S(1)}, bf16[512,2048]{1,0:T(8,128)(2,1)S(1)}, f32[512,2048]{1,0:T(8,128)S(1)}) custom-call(s32[8]{0:T(128)S(1)} %stack.32.where_ref, ...), custom_call_target="tpu_custom_call", output_to_operand_aliasing={{1}: (3, {}), {2}: (4, {}), {3}: (5, {}), {4}: (6, {})} | custom-call | flops 536870912 | bytes 11665408 | tf_op jit(solution)/shard_map/pallas_call | solution.py:23
  65.6 1.8 %shard_map.123 = (bf16[512,512]{1,0:T(8,128)(2,1)S(1)}, bf16[512,2048]{1,0:T(8,128)(2,1)S(1)}, bf16[128,512]{1,0:T(8,128)(2,1)S(1)}) custom-call(s32[8]{0:T(128)S(1)} %stack.32.where_ref, bf16[256,512]{1,0:T(8,128)(2,1)S(1)} %bitcast.42, bf16[2,512,2048]{2,1,0:T(8,128)(2,1)S(1)} %bitcast.28, bf16[512,512]{1,0:T(8,128)(2,1)S(1)} %get-tuple-element.115.refs_0_.x_ref, ...), custom_call_target="tpu_custom_call" | custom-call | flops 536870912 | bytes 9175040 | tf_op jit(solution)/shard_map/pallas_call | solution.py:23
  67.4 0.7 collective-permute-start.15
  68.1 2.9 %shard_map.122 = (bf16[128,512]{1,0:T(8,128)(2,1)}, bf16[512,512]{1,0:T(8,128)(2,1)S(1)}, bf16[512,512]{1,0:T(8,128)(2,1)S(1)}, bf16[512,2048]{1,0:T(8,128)(2,1)S(1)}, f32[512,2048]{1,0:T(8,128)S(1)}) custom-call(s32[8]{0:T(128)S(1)} %stack.32.where_ref, ...), custom_call_target="tpu_custom_call", output_to_operand_aliasing={{1}: (3, {}), {2}: (4, {}), {3}: (5, {}), {4}: (6, {})} | custom-call | flops 536870912 | bytes 11665408 | tf_op jit(solution)/shard_map/pallas_call | solution.py:23
  71.0 1.8 %shard_map.124 = (bf16[512,512]{1,0:T(8,128)(2,1)S(1)}, bf16[512,2048]{1,0:T(8,128)(2,1)S(1)}, bf16[128,512]{1,0:T(8,128)(2,1)S(1)}) custom-call(s32[8]{0:T(128)S(1)} %stack.32.where_ref, bf16[256,512]{1,0:T(8,128)(2,1)S(1)} %bitcast.43, bf16[2,512,2048]{2,1,0:T(8,128)(2,1)S(1)} %bitcast.30, ...), custom_call_target="tpu_custom_call", output_to_operand_aliasing={{0}: (5, {}), {1}: (6, {})} | custom-call | flops 536870912 | bytes 11796480 | tf_op jit(solution)/shard_map/pallas_call | solution.py:23
  72.8 0.7 collective-permute-start.14
  73.5 1.8 %shard_map.125 = (bf16[512,512]{1,0:T(8,128)(2,1)S(1)}, bf16[512,2048]{1,0:T(8,128)(2,1)S(1)}, bf16[128,512]{1,0:T(8,128)(2,1)S(1)}) custom-call(s32[8]{0:T(128)S(1)} %stack.32.where_ref, bf16[128,512]{1,0:T(8,128)(2,1)S(1)} %collective-permute-done.15.grad_ref, bf16[2,512,2048]{2,1,0:T(8,128)(2,1)S(1)} %bitcast.31, ...), custom_call_target="tpu_custom_call", output_to_operand_aliasing={{0}: (5, {}), {1}: (6, {})} | custom-call | flops 536870912 | bytes 11665408 | tf_op jit(solution)/shard_map/pallas_call | solution.py:23
  75.3 0.7 collective-permute-start.17
  76.0 1.8 %shard_map.126 = (bf16[512,512]{1,0:T(8,128)(2,1)S(1)}, bf16[512,2048]{1,0:T(8,128)(2,1)S(1)}, bf16[128,512]{1,0:T(8,128)(2,1)S(1)}) custom-call(s32[8]{0:T(128)S(1)} %stack.32.where_ref, bf16[128,512]{1,0:T(8,128)(2,1)S(1)} %collective-permute-done.14.grad_ref, bf16[2,512,2048]{2,1,0:T(8,128)(2,1)S(1)} %bitcast.32, ...), custom_call_target="tpu_custom_call", output_to_operand_aliasing={{0}: (5, {}), {1}: (6, {})} | custom-call | flops 536870912 | bytes 11665408 | tf_op jit(solution)/shard_map/pallas_call | solution.py:23
  77.8 0.7 collective-permute-start.16
  78.5 1.8 %shard_map.127 = (bf16[512,512]{1,0:T(8,128)(2,1)S(1)}, bf16[512,2048]{1,0:T(8,128)(2,1)S(1)}, bf16[128,512]{1,0:T(8,128)(2,1)S(1)}) custom-call(s32[8]{0:T(128)S(1)} %stack.32.where_ref, bf16[128,512]{1,0:T(8,128)(2,1)S(1)} %collective-permute-done.17.grad_ref, bf16[2,512,2048]{2,1,0:T(8,128)(2,1)S(1)} %bitcast.33, ...), custom_call_target="tpu_custom_call", output_to_operand_aliasing={{0}: (5, {}), {1}: (6, {})} | custom-call | flops 536870912 | bytes 11665408 | tf_op jit(solution)/shard_map/pallas_call | solution.py:23
  80.3 1.3 collective-permute-start.19
  81.6 1.8 %shard_map.128 = (bf16[512,512]{1,0:T(8,128)(2,1)S(1)}, bf16[512,2048]{1,0:T(8,128)(2,1)S(1)}, bf16[128,512]{1,0:T(8,128)(2,1)S(1)}) custom-call(s32[8]{0:T(128)S(1)} %stack.32.where_ref, bf16[128,512]{1,0:T(8,128)(2,1)S(1)} %collective-permute-done.16.grad_ref, bf16[2,512,2048]{2,1,0:T(8,128)(2,1)S(1)} %bitcast.34, ...), custom_call_target="tpu_custom_call", output_to_operand_aliasing={{0}: (5, {}), {1}: (6, {})} | custom-call | flops 536870912 | bytes 11665408 | tf_op jit(solution)/shard_map/pallas_call | solution.py:23
  83.5 1.5 collective-permute-start.18
  85.0 11.5 %collective-permute-done.19.grad_ref = bf16[128,512]{1,0:T(8,128)(2,1)S(1)} collective-permute-done((bf16[128,512]{1,0:T(8,128)(2,1)S(1)}, bf16[128,512]{1,0:T(8,128)(2,1)S(1)}, u32[]{:S(2)}, u32[]{:S(2)}) %collective-permute-start.19) | collective-permute-done | bytes 131104 | tf_op jit(solution)/shard_map/ppermute | solution.py:171
  96.5 1.0 shard_map.129
  97.5 4.3 %collective-permute-done.18.grad_ref = bf16[128,512]{1,0:T(8,128)(2,1)S(1)} collective-permute-done((bf16[128,512]{1,0:T(8,128)(2,1)S(1)}, bf16[128,512]{1,0:T(8,128)(2,1)S(1)}, u32[]{:S(2)}, u32[]{:S(2)}) %collective-permute-start.18) | collective-permute-done | bytes 131104 | tf_op jit(solution)/shard_map/ppermute | solution.py:171
  101.8 1.0 shard_map.130
  102.8 1.1 shard_map.113.known_ref
  103.9 4.5 %add_gradient.1 = (f32[2,4,128,2048]{3,2,1,0:T(8,128)S(1)}, f32[1,1]{1,0:T(1,128)}) custom-call(s32[8]{0:T(128)S(1)} %stack.32.where_ref, f32[2,4,128,2048]{3,2,1,0:T(8,128)S(1)} %shard_map.113.known_ref, bf16[512,512]{1,0:T(8,128)(2,1)S(1)} %get-tuple-element.119.normed_ref, ...), custom_call_target="tpu_custom_call", output_to_operand_aliasing={{0}: (1, {})} | custom-call | flops 1073741824 | bytes 33554432 | tf_op jit(solution)/shard_map/add_gradient/pallas_call | solution.py:263
  108.4 1.5 shard_map.135
  110.0 2.0 %shard_map.131 = (bf16[128,2048]{1,0:T(8,128)(2,1)S(1)}, bf16[128,2048]{1,0:T(8,128)(2,1)S(1)}, bf16[128,2048]{1,0:T(8,128)(2,1)S(1)}, bf16[128,2048]{1,0:T(8,12...) custom-call(s32[8]{0:T(128)S(1)} %stack.32.where_ref, f32[1,1]{1,0:T(1,128)} %get-tuple-element.145.sum_ref, ...), custom_call_target="tpu_custom_call" | custom-call | bytes 8388608 | tf_op jit(solution)/shard_map/pallas_call | solution.py:23
  112.7 10.7 %collective-permute-start.27 = (bf16[128,2048]{1,0:T(8,128)(2,1)S(1)}, bf16[128,2048]{1,0:T(8,128)(2,1)S(1)}, u32[]{:S(2)}, u32[]{:S(2)}) collective-permute-start(bf16[128,2048]{1,0:T(8,128)(2,1)S(1)} %shard_map.136), channel_id=1, source_target_pairs={{0,2},{1,3},{6,4},{7,5},{8,10},{9,11},{14,12},{15,13},{16,18},{17,... | collective-permute-start | bytes 1572872 | tf_op jit(solution)/shard_map/ppermute | solution.py:195
  123.7 1.3 collective-permute-start.24
  125.0 10.7 %collective-permute-done.27.refs_2_ = bf16[128,2048]{1,0:T(8,128)(2,1)S(1)} collective-permute-done((bf16[128,2048]{1,0:T(8,128)(2,1)S(1)}, bf16[128,2048]{1,0:T(8,128)(2,1)S(1)}, u32[]{:S(2)}, u32[]{:S(2)}) %collective-permute-start.27) | collective-permute-done | bytes 524320 | tf_op jit(solution)/shard_map/ppermute | solution.py:195
  135.9 0.7 collective-permute-start.28
  136.8 5.6 %collective-permute-start.22 = (bf16[128,2048]{1,0:T(8,128)(2,1)S(1)}, bf16[128,2048]{1,0:T(8,128)(2,1)S(1)}, u32[]{:S(2)}, u32[]{:S(2)}) collective-permute-start(bf16[128,2048]{1,0:T(8,128)(2,1)S(1)} %shard_map.132), channel_id=1, source_target_pairs={{0,2},{1,3},{6,4},{7,5},{8,10},{9,11},{14,12},{15,13},{16,18},{17,... | collective-permute-start | bytes 1572872 | tf_op jit(solution)/shard_map/ppermute | solution.py:195
  142.5 4.5 %collective-permute-done.24.refs_2_ = bf16[128,2048]{1,0:T(8,128)(2,1)S(1)} collective-permute-done((bf16[128,2048]{1,0:T(8,128)(2,1)S(1)}, bf16[128,2048]{1,0:T(8,128)(2,1)S(1)}, u32[]{:S(2)}, u32[]{:S(2)}) %collective-permute-start.24) | collective-permute-done | bytes 524320 | tf_op jit(solution)/shard_map/ppermute | solution.py:195
  147.2 0.7 collective-permute-start.25
  148.1 1.3 collective-permute-start.29
  149.4 2.9 %shard_map.140 = bf16[1024,2048]{1,0:T(8,128)(2,1)S(1)} custom-call(s32[8]{0:T(128)S(1)} %stack.32.where_ref, f32[1,1]{1,0:T(1,128)} %get-tuple-element.145.sum_ref, f32[2,4,128,2048]{3,2,1,0:T(8,128)S(1)} %get-tuple-element.146.combined_ref), custom_call_target="tpu_custom_call" | custom-call | bytes 8388608 | tf_op jit(solution)/shard_map/pallas_call | solution.py:23
  152.2 2.0 %copy.104 = bf16[1,1,2,512,2048]{4,3,2,1,0:T(8,128)(2,1)} copy(bf16[1,1,2,512,2048]{4,3,2,1,0:T(8,128)(2,1)S(1)} %bitcast.17) | data formatting | bytes 8388608
  154.3 3.0 %collective-permute-done.22.refs_2_ = bf16[128,2048]{1,0:T(8,128)(2,1)S(1)} collective-permute-done((bf16[128,2048]{1,0:T(8,128)(2,1)S(1)}, bf16[128,2048]{1,0:T(8,128)(2,1)S(1)}, u32[]{:S(2)}, u32[]{:S(2)}) %collective-permute-start.22) | collective-permute-done | bytes 524320 | tf_op jit(solution)/shard_map/ppermute | solution.py:195
  157.3 6.1 %collective-permute-done.29.refs_4_ = bf16[128,2048]{1,0:T(8,128)(2,1)S(1)} collective-permute-done((bf16[128,2048]{1,0:T(8,128)(2,1)S(1)}, bf16[128,2048]{1,0:T(8,128)(2,1)S(1)}, u32[]{:S(2)}, u32[]{:S(2)}) %collective-permute-start.29) | collective-permute-done | bytes 524320 | tf_op jit(solution)/shard_map/ppermute | solution.py:195
  163.4 2.5 %shard_map.139 = (bf16[128,2048]{1,0:T(8,128)(2,1)S(1)}, bf16[128,2048]{1,0:T(8,128)(2,1)S(1)}, f32[128,2048]{1,0:T(8,128)S(1)}) custom-call(s32[8]{0:T(128)S(1)} %stack.32.where_ref, f32[128,2048]{1,0:T(8,128)S(1)} %bitcast.41, bf16[128,2048]{1,0:T(8,128)(2,1)S(1)} %bitcast.51, bf16[2,512,2048]{2,1,0:T(8,128)(2,1)S(1)} %bitcast.37, ...), custom_call_target="tpu_custom_call" | custom-call | bytes 8388608 | tf_op jit(solution)/shard_map/pallas_call | solution.py:23
  165.9 0.8 copy.102
  166.7 0.8 copy.103
  167.5 1.0 copy.105
  (50 shorter events, 2.7 us)
Async XLA Ops:
  0.6 19.7 %collective-permute-start = (bf16[128,2048]{1,0:T(8,128)(2,1)}, bf16[128,2048]{1,0:T(8,128)(2,1)S(1)}, u32[]{:S(2)}, u32[]{:S(2)}) collective-permute-start(bf16[128,2048]{1,0:T(8,128)(2,1)} %bitcast.44), channel_id=1, source_target_pairs={{0,4},{1,5},{2,6},{3,7},{8,12},{9,13},{10,14},{11,15},{16,20},{17,... | collective-permute-start | bytes 1572872 | tf_op jit(solution)/shard_map/ppermute | solution.py:195
  6.6 28.8 %collective-permute-start.1 = (bf16[128,2048]{1,0:T(8,128)(2,1)}, bf16[128,2048]{1,0:T(8,128)(2,1)S(1)}, u32[]{:S(2)}, u32[]{:S(2)}) collective-permute-start(bf16[128,2048]{1,0:T(8,128)(2,1)} %bitcast.45), channel_id=1, source_target_pairs={{6,2},{7,3},{4,0},{5,1},{14,10},{15,11},{12,8},{13,9},{22,18},{23,... | collective-permute-start | bytes 1572872 | tf_op jit(solution)/shard_map/ppermute | solution.py:195
  7.9 33.2 %collective-permute-start.2 = (bf16[128,2048]{1,0:T(8,128)(2,1)}, bf16[128,2048]{1,0:T(8,128)(2,1)S(1)}, u32[]{:S(2)}, u32[]{:S(2)}) collective-permute-start(bf16[128,2048]{1,0:T(8,128)(2,1)} %bitcast.46), channel_id=1, source_target_pairs={{0,2},{1,3},{2,4},{3,5},{4,6},{5,7},{8,10},{9,11},{10,12},{11,13},... | collective-permute-start | bytes 1572872 | tf_op jit(solution)/shard_map/ppermute | solution.py:195
  11.5 37.1 %collective-permute-start.3 = (bf16[128,2048]{1,0:T(8,128)(2,1)}, bf16[128,2048]{1,0:T(8,128)(2,1)S(1)}, u32[]{:S(2)}, u32[]{:S(2)}) collective-permute-start(bf16[128,2048]{1,0:T(8,128)(2,1)} %bitcast.47), channel_id=1, source_target_pairs={{6,4},{7,5},{4,2},{5,3},{2,0},{3,1},{14,12},{15,13},{12,10},{13,11... | collective-permute-start | bytes 1572872 | tf_op jit(solution)/shard_map/ppermute | solution.py:195
  12.8 35.8 %collective-permute-start.4 = (bf16[128,2048]{1,0:T(8,128)(2,1)}, bf16[128,2048]{1,0:T(8,128)(2,1)S(1)}, u32[]{:S(2)}, u32[]{:S(2)}) collective-permute-start(bf16[128,2048]{1,0:T(8,128)(2,1)} %bitcast.48), channel_id=1, source_target_pairs={{0,6},{1,7},{8,14},{9,15},{16,22},{17,23},{24,30},{25,31}} | collective-permute-start | bytes 1572872 | tf_op jit(solution)/shard_map/ppermute | solution.py:195
  20.4 28.2 %collective-permute-start.5 = (bf16[128,2048]{1,0:T(8,128)(2,1)}, bf16[128,2048]{1,0:T(8,128)(2,1)S(1)}, u32[]{:S(2)}, u32[]{:S(2)}) collective-permute-start(bf16[128,2048]{1,0:T(8,128)(2,1)} %bitcast.49), channel_id=1, source_target_pairs={{6,0},{7,1},{14,8},{15,9},{22,16},{23,17},{30,24},{31,25}} | collective-permute-start | bytes 1572872 | tf_op jit(solution)/shard_map/ppermute | solution.py:195
  21.7 0.9 copy-start.7
  22.6 0.7 copy-start.8
  23.6 2.2 %copy-start = (bf16[1,2,512,2048]{3,2,1,0:T(8,128)(2,1)S(1)}, bf16[1,2,512,2048]{3,2,1,0:T(8,128)(2,1)}, u32[]{:S(2)}) copy-start(bf16[1,2,512,2048]{3,2,1,0:T(8,128)(2,1)} %param.10) | copy-start | bytes 12582916
  35.4 14.6 %collective-permute-start.9 = (bf16[128,512]{1,0:T(8,128)(2,1)S(1)}, bf16[128,512]{1,0:T(8,128)(2,1)S(1)}, u32[]{:S(2)}, u32[]{:S(2)}) collective-permute-start(bf16[128,512]{1,0:T(8,128)(2,1)S(1)} %get-tuple-element.90), channel_id=1, source_target_pairs={{0,8},{1,9},{2,10},{3,11},{4,12},{5,13},{6,14},{7,15}} | collective-permute-start | bytes 393224 | tf_op jit(solution)/shard_map/ppermute | solution.py:171
  38.8 3.6 %copy-start.2 = (bf16[1,1,2,512,2048]{4,3,2,1,0:T(8,128)(2,1)S(1)}, bf16[1,1,2,512,2048]{4,3,2,1,0:T(8,128)(2,1)}, u32[]{:S(2)}) copy-start(bf16[1,1,2,512,2048]{4,3,2,1,0:T(8,128)(2,1)} %param.13) | copy-start | bytes 12582916
  38.8 3.6 %copy-start.5 = (bf16[1,128,2048]{2,1,0:T(8,128)(2,1)S(1)}, bf16[1,128,2048]{2,1,0:T(8,128)(2,1)}, u32[]{:S(2)}) copy-start(bf16[1,128,2048]{2,1,0:T(8,128)(2,1)} %param.12) | copy-start | bytes 1572868
  41.1 12.6 %collective-permute-start.8 = (bf16[128,512]{1,0:T(8,128)(2,1)S(1)}, bf16[128,512]{1,0:T(8,128)(2,1)S(1)}, u32[]{:S(2)}, u32[]{:S(2)}) collective-permute-start(bf16[128,512]{1,0:T(8,128)(2,1)S(1)} %get-tuple-element.89), channel_id=1, source_target_pairs={{0,8},{1,9},{2,10},{3,11},{4,12},{5,13},{6,14},{7,15}} | collective-permute-start | bytes 393224 | tf_op jit(solution)/shard_map/ppermute | solution.py:171
  48.5 54.2 %collective-permute-start.6 = (bf16[2,128,2048]{2,1,0:T(8,128)(2,1)S(1)}, bf16[2,128,2048]{2,1,0:T(8,128)(2,1)S(1)}, u32[]{:S(2)}, u32[]{:S(2)}) collective-permute-start(bf16[2,128,2048]{2,1,0:T(8,128)(2,1)S(1)} %get-tuple-element.83), channel_id=1, source_target_pairs={{0,1},{1,0},{2,3},{3,2},{4,5},{5,4},{6,7},{7,6},{8,9},{9,8},{10,11... | collective-permute-start | bytes 3145736 | tf_op jit(solution)/shard_map/ppermute | solution.py:199
  48.6 2.2 %copy-start.1 = (bf16[1,2,512,2048]{3,2,1,0:T(8,128)(2,1)S(1)}, bf16[1,2,512,2048]{3,2,1,0:T(8,128)(2,1)}, u32[]{:S(2)}) copy-start(bf16[1,2,512,2048]{3,2,1,0:T(8,128)(2,1)} %param.10) | copy-start | bytes 12582916
  49.5 53.3 %collective-permute-start.7 = (bf16[2,128,2048]{2,1,0:T(8,128)(2,1)S(1)}, bf16[2,128,2048]{2,1,0:T(8,128)(2,1)S(1)}, u32[]{:S(2)}, u32[]{:S(2)}) collective-permute-start(bf16[2,128,2048]{2,1,0:T(8,128)(2,1)S(1)} %get-tuple-element.84), channel_id=1, source_target_pairs={{0,1},{1,0},{2,3},{3,2},{4,5},{5,4},{6,7},{7,6},{8,9},{9,8},{10,11... | collective-permute-start | bytes 3145736 | tf_op jit(solution)/shard_map/ppermute | solution.py:199
  53.0 3.6 %collective-permute-start.11 = (bf16[128,512]{1,0:T(8,128)(2,1)S(1)}, bf16[128,512]{1,0:T(8,128)(2,1)S(1)}, u32[]{:S(2)}, u32[]{:S(2)}) collective-permute-start(bf16[128,512]{1,0:T(8,128)(2,1)S(1)} %get-tuple-element.100), channel_id=1, source_target_pairs={{8,16},{9,17},{10,18},{11,19},{12,20},{13,21},{14,22},{15,23}} | collective-permute-start | bytes 393224 | tf_op jit(solution)/shard_map/ppermute | solution.py:171
  55.9 3.6 %collective-permute-start.10 = (bf16[128,512]{1,0:T(8,128)(2,1)S(1)}, bf16[128,512]{1,0:T(8,128)(2,1)S(1)}, u32[]{:S(2)}, u32[]{:S(2)}) collective-permute-start(bf16[128,512]{1,0:T(8,128)(2,1)S(1)} %get-tuple-element.99), channel_id=1, source_target_pairs={{8,16},{9,17},{10,18},{11,19},{12,20},{13,21},{14,22},{15,23}} | collective-permute-start | bytes 393224 | tf_op jit(solution)/shard_map/ppermute | solution.py:171
  58.9 3.8 %collective-permute-start.13 = (bf16[128,512]{1,0:T(8,128)(2,1)S(1)}, bf16[128,512]{1,0:T(8,128)(2,1)S(1)}, u32[]{:S(2)}, u32[]{:S(2)}) collective-permute-start(bf16[128,512]{1,0:T(8,128)(2,1)S(1)} %get-tuple-element.110), channel_id=1, source_target_pairs={{16,24},{17,25},{18,26},{19,27},{20,28},{21,29},{22,30},{23,31}} | collective-permute-start | bytes 393224 | tf_op jit(solution)/shard_map/ppermute | solution.py:171
  61.8 6.3 %collective-permute-start.12 = (bf16[128,512]{1,0:T(8,128)(2,1)S(1)}, bf16[128,512]{1,0:T(8,128)(2,1)S(1)}, u32[]{:S(2)}, u32[]{:S(2)}) collective-permute-start(bf16[128,512]{1,0:T(8,128)(2,1)S(1)} %get-tuple-element.109), channel_id=1, source_target_pairs={{16,24},{17,25},{18,26},{19,27},{20,28},{21,29},{22,30},{23,31}} | collective-permute-start | bytes 393224 | tf_op jit(solution)/shard_map/ppermute | solution.py:171
  62.7 2.9 %copy-start.4 = (bf16[4,64,512]{2,1,0:T(8,128)(2,1)S(1)}, bf16[4,64,512]{2,1,0:T(8,128)(2,1)}, u32[]{:S(2)}) copy-start(bf16[4,64,512]{2,1,0:T(8,128)(2,1)} %param.15) | copy-start | bytes 786436
  67.4 6.1 %collective-permute-start.15 = (bf16[128,512]{1,0:T(8,128)(2,1)S(1)}, bf16[128,512]{1,0:T(8,128)(2,1)S(1)}, u32[]{:S(2)}, u32[]{:S(2)}) collective-permute-start(bf16[128,512]{1,0:T(8,128)(2,1)S(1)} %get-tuple-element.125), channel_id=1, source_target_pairs={{24,16},{25,17},{26,18},{27,19},{28,20},{29,21},{30,22},{31,23}} | collective-permute-start | bytes 393224 | tf_op jit(solution)/shard_map/ppermute | solution.py:171
  72.8 3.2 %collective-permute-start.14 = (bf16[128,512]{1,0:T(8,128)(2,1)S(1)}, bf16[128,512]{1,0:T(8,128)(2,1)S(1)}, u32[]{:S(2)}, u32[]{:S(2)}) collective-permute-start(bf16[128,512]{1,0:T(8,128)(2,1)S(1)} %get-tuple-element.124), channel_id=1, source_target_pairs={{24,16},{25,17},{26,18},{27,19},{28,20},{29,21},{30,22},{31,23}} | collective-permute-start | bytes 393224 | tf_op jit(solution)/shard_map/ppermute | solution.py:171
  75.3 3.2 %collective-permute-start.17 = (bf16[128,512]{1,0:T(8,128)(2,1)S(1)}, bf16[128,512]{1,0:T(8,128)(2,1)S(1)}, u32[]{:S(2)}, u32[]{:S(2)}) collective-permute-start(bf16[128,512]{1,0:T(8,128)(2,1)S(1)} %get-tuple-element.131), channel_id=1, source_target_pairs={{16,8},{17,9},{18,10},{19,11},{20,12},{21,13},{22,14},{23,15}} | collective-permute-start | bytes 393224 | tf_op jit(solution)/shard_map/ppermute | solution.py:171
  77.8 3.8 %collective-permute-start.16 = (bf16[128,512]{1,0:T(8,128)(2,1)S(1)}, bf16[128,512]{1,0:T(8,128)(2,1)S(1)}, u32[]{:S(2)}, u32[]{:S(2)}) collective-permute-start(bf16[128,512]{1,0:T(8,128)(2,1)S(1)} %get-tuple-element.130), channel_id=1, source_target_pairs={{16,8},{17,9},{18,10},{19,11},{20,12},{21,13},{22,14},{23,15}} | collective-permute-start | bytes 393224 | tf_op jit(solution)/shard_map/ppermute | solution.py:171
  80.3 16.2 %collective-permute-start.19 = (bf16[128,512]{1,0:T(8,128)(2,1)S(1)}, bf16[128,512]{1,0:T(8,128)(2,1)S(1)}, u32[]{:S(2)}, u32[]{:S(2)}) collective-permute-start(bf16[128,512]{1,0:T(8,128)(2,1)S(1)} %get-tuple-element.137), channel_id=1, source_target_pairs={{8,0},{9,1},{10,2},{11,3},{12,4},{13,5},{14,6},{15,7}} | collective-permute-start | bytes 393224 | tf_op jit(solution)/shard_map/ppermute | solution.py:171
  83.5 18.3 %collective-permute-start.18 = (bf16[128,512]{1,0:T(8,128)(2,1)S(1)}, bf16[128,512]{1,0:T(8,128)(2,1)S(1)}, u32[]{:S(2)}, u32[]{:S(2)}) collective-permute-start(bf16[128,512]{1,0:T(8,128)(2,1)S(1)} %get-tuple-element.136), channel_id=1, source_target_pairs={{8,0},{9,1},{10,2},{11,3},{12,4},{13,5},{14,6},{15,7}} | collective-permute-start | bytes 393224 | tf_op jit(solution)/shard_map/ppermute | solution.py:171
  109.9 2.7 %collective-permute-start.26 = (bf16[128,2048]{1,0:T(8,128)(2,1)S(1)}, bf16[128,2048]{1,0:T(8,128)(2,1)S(1)}, u32[]{:S(2)}, u32[]{:S(2)}) collective-permute-start(bf16[128,2048]{1,0:T(8,128)(2,1)S(1)} %get-tuple-element.154), channel_id=1, source_target_pairs={{0,1},{1,0},{2,3},{3,2},{4,5},{5,4},{6,7},{7,6},{8,9},{9,8},{10,11... | collective-permute-start | bytes 1572872 | tf_op jit(solution)/shard_map/ppermute | solution.py:199
  112.0 11.5 %collective-permute-start.23 = (bf16[128,2048]{1,0:T(8,128)(2,1)S(1)}, bf16[128,2048]{1,0:T(8,128)(2,1)S(1)}, u32[]{:S(2)}, u32[]{:S(2)}) collective-permute-start(bf16[128,2048]{1,0:T(8,128)(2,1)S(1)} %get-tuple-element.152), channel_id=1, source_target_pairs={{0,1},{1,0},{2,3},{3,2},{4,5},{5,4},{6,7},{7,6},{8,9},{9,8},{10,11... | collective-permute-start | bytes 1572872 | tf_op jit(solution)/shard_map/ppermute | solution.py:199
  112.7 23.0 %collective-permute-start.27 = (bf16[128,2048]{1,0:T(8,128)(2,1)S(1)}, bf16[128,2048]{1,0:T(8,128)(2,1)S(1)}, u32[]{:S(2)}, u32[]{:S(2)}) collective-permute-start(bf16[128,2048]{1,0:T(8,128)(2,1)S(1)} %shard_map.136), channel_id=1, source_target_pairs={{0,2},{1,3},{6,4},{7,5},{8,10},{9,11},{14,12},{15,13},{16,18},{17,... | collective-permute-start | bytes 1572872 | tf_op jit(solution)/shard_map/ppermute | solution.py:195
  123.5 13.2 %collective-permute-start.21 = (bf16[128,2048]{1,0:T(8,128)(2,1)S(1)}, bf16[128,2048]{1,0:T(8,128)(2,1)S(1)}, u32[]{:S(2)}, u32[]{:S(2)}) collective-permute-start(bf16[128,2048]{1,0:T(8,128)(2,1)S(1)} %get-tuple-element.150), channel_id=1, source_target_pairs={{0,1},{1,0},{2,3},{3,2},{4,5},{5,4},{6,7},{7,6},{8,9},{9,8},{10,11... | collective-permute-start | bytes 1572872 | tf_op jit(solution)/shard_map/ppermute | solution.py:199
  123.7 23.3 %collective-permute-start.24 = (bf16[128,2048]{1,0:T(8,128)(2,1)S(1)}, bf16[128,2048]{1,0:T(8,128)(2,1)S(1)}, u32[]{:S(2)}, u32[]{:S(2)}) collective-permute-start(bf16[128,2048]{1,0:T(8,128)(2,1)S(1)} %shard_map.133), channel_id=1, source_target_pairs={{0,2},{1,3},{6,4},{7,5},{8,10},{9,11},{14,12},{15,13},{16,18},{17,... | collective-permute-start | bytes 1572872 | tf_op jit(solution)/shard_map/ppermute | solution.py:195
  135.9 11.9 %collective-permute-start.28 = (bf16[128,2048]{1,0:T(8,128)(2,1)S(1)}, bf16[128,2048]{1,0:T(8,128)(2,1)S(1)}, u32[]{:S(2)}, u32[]{:S(2)}) collective-permute-start(bf16[128,2048]{1,0:T(8,128)(2,1)S(1)} %shard_map.137), channel_id=1, source_target_pairs={{2,4},{3,5},{4,2},{5,3},{10,12},{11,13},{12,10},{13,11},{18,20},{1... | collective-permute-start | bytes 1572872 | tf_op jit(solution)/shard_map/ppermute | solution.py:195
  136.6 17.6 %collective-permute-start.20 = (bf16[128,2048]{1,0:T(8,128)(2,1)S(1)}, bf16[128,2048]{1,0:T(8,128)(2,1)S(1)}, u32[]{:S(2)}, u32[]{:S(2)}) collective-permute-start(bf16[128,2048]{1,0:T(8,128)(2,1)S(1)} %get-tuple-element.148), channel_id=1, source_target_pairs={{0,1},{1,0},{2,3},{3,2},{4,5},{5,4},{6,7},{7,6},{8,9},{9,8},{10,11... | collective-permute-start | bytes 1572872 | tf_op jit(solution)/shard_map/ppermute | solution.py:199
  136.8 20.4 %collective-permute-start.22 = (bf16[128,2048]{1,0:T(8,128)(2,1)S(1)}, bf16[128,2048]{1,0:T(8,128)(2,1)S(1)}, u32[]{:S(2)}, u32[]{:S(2)}) collective-permute-start(bf16[128,2048]{1,0:T(8,128)(2,1)S(1)} %shard_map.132), channel_id=1, source_target_pairs={{0,2},{1,3},{6,4},{7,5},{8,10},{9,11},{14,12},{15,13},{16,18},{17,... | collective-permute-start | bytes 1572872 | tf_op jit(solution)/shard_map/ppermute | solution.py:195
  147.2 10.1 %collective-permute-start.25 = (bf16[128,2048]{1,0:T(8,128)(2,1)S(1)}, bf16[128,2048]{1,0:T(8,128)(2,1)S(1)}, u32[]{:S(2)}, u32[]{:S(2)}) collective-permute-start(bf16[128,2048]{1,0:T(8,128)(2,1)S(1)} %shard_map.134), channel_id=1, source_target_pairs={{2,4},{3,5},{4,2},{5,3},{10,12},{11,13},{12,10},{13,11},{18,20},{1... | collective-permute-start | bytes 1572872 | tf_op jit(solution)/shard_map/ppermute | solution.py:195
  148.1 15.3 %collective-permute-start.29 = (bf16[128,2048]{1,0:T(8,128)(2,1)S(1)}, bf16[128,2048]{1,0:T(8,128)(2,1)S(1)}, u32[]{:S(2)}, u32[]{:S(2)}) collective-permute-start(bf16[128,2048]{1,0:T(8,128)(2,1)S(1)} %shard_map.138), channel_id=1, source_target_pairs={{4,6},{5,7},{2,0},{3,1},{12,14},{13,15},{10,8},{11,9},{20,22},{21,... | collective-permute-start | bytes 1572872 | tf_op jit(solution)/shard_map/ppermute | solution.py:195
  152.2 11.1 %copy-start.3 = (f32[1,128,2048]{2,1,0:T(8,128)S(1)}, f32[1,128,2048]{2,1,0:T(8,128)}, u32[]{:S(2)}) copy-start(f32[1,128,2048]{2,1,0:T(8,128)} %param.14) | copy-start | bytes 3145732
  152.2 11.1 %copy-start.6 = (bf16[1,128,2048]{2,1,0:T(8,128)(2,1)S(1)}, bf16[1,128,2048]{2,1,0:T(8,128)(2,1)}, u32[]{:S(2)}) copy-start(bf16[1,128,2048]{2,1,0:T(8,128)(2,1)} %param.11) | copy-start | bytes 1572868

commit v2 on v1

v2 whole, which is shorter than its diff:
```python
import math

import jax
import jax.numpy as jnp
from jax import lax
from jax.experimental import pallas as pl
from jax.experimental.pallas import tpu as pltpu
from jax.sharding import PartitionSpec as P


gelu_coef = math.sqrt(2.0 / math.pi)
bf16, f32 = jnp.bfloat16, jnp.float32
whole = pl.BlockSpec(memory_space=pltpu.VMEM)
outside = pl.BlockSpec(memory_space=pl.ANY)


def held(array):
    return pltpu.with_memory_space_constraint(array, pltpu.VMEM)


def call(kernel, outs, arrays, aliases=None, limit=8, flops=0, transcendentals=0, written=(), scratch=()):
    moved = sum(math.prod(a.shape) * a.dtype.itemsize for a in arrays)
    return pl.pallas_call(
        kernel,
        out_shape=[pltpu.VMEM(shape, dtype) for shape, dtype in outs]
        + [jax.ShapeDtypeStruct(shape, dtype) for shape, dtype in written],
        in_specs=[whole] * len(arrays),
        out_specs=[whole] * len(outs) + [outside] * len(written),
        input_output_aliases=aliases or {},
        scratch_shapes=list(scratch),
        compiler_params=pltpu.CompilerParams(vmem_limit_bytes=limit << 20),
        cost_estimate=pl.CostEstimate(flops=flops, bytes_accessed=moved, transcendentals=transcendentals),
    )(*[held(a) for a in arrays])


def place_on_line():
    rank = lax.axis_index("dp")
    return rank >> 1, rank & 1


def across(left, right):
    return lax.dot_general(left, right, (((1,), (1,)), ((), ())), preferred_element_type=f32)


def down(left, right):
    return lax.dot_general(left, right, (((0,), (0,)), ((), ())), preferred_element_type=f32)


def normalize(inputs):
    values = inputs.astype(f32)
    center = jnp.mean(values, axis=-1, keepdims=True)
    shifted = values - center
    scaled = lax.rsqrt(jnp.mean(shifted * shifted, axis=-1, keepdims=True) + 1e-05)
    return shifted * scaled, scaled


def embed_rows(token_ids, embed):
    micro, rows = token_ids.shape
    vocab, width = embed.shape

    def kernel(ids_ref, embed_ref, out_ref):
        for m in range(micro):
            ids = ids_ref[m : m + 1, :]
            hot = (lax.broadcasted_iota(jnp.int32, (vocab, rows), 0) == ids).astype(f32).astype(bf16)
            out_ref[m * rows : (m + 1) * rows, :] = down(hot, embed_ref[...]).astype(bf16)

    return call(kernel, [((micro * rows, width), bf16)], [token_ids, embed])[0]


slabs = 2


def spot_of(turn, tokens):
    return jnp.where(lax.axis_index("section") == turn, 0, tokens)


def rows_of(ref, chunk, rows):
    return ref[...] if ref.shape[0] == rows else ref[chunk * rows : (chunk + 1) * rows, :]


def forward(turn, inputs, weights, saved, chunk, rows, tokens):
    width = inputs.shape[1]
    channels = weights.shape[2]
    step = channels // slabs
    outs = [((rows, width), bf16)] + [
        ((2 * tokens, width), bf16),
        ((2 * tokens, width), bf16),
        ((2 * tokens, channels), bf16),
        ((2 * tokens, channels), f32),
    ]

    def kernel(x_ref, w_ref, *refs):
        out_ref, x_out, normed_out, hidden_out, slope_out = refs[-5:]
        place = pl.ds(pl.multiple_of(spot_of(turn, tokens) + chunk * rows, rows), rows)
        inputs = rows_of(x_ref, chunk, rows)
        normed_b = normalize(inputs)[0].astype(bf16)
        x_out[place, :] = inputs
        normed_out[place, :] = normed_b
        total = inputs.astype(f32)
        for i in range(slabs):
            part = pl.ds(i * step, step)
            upper = jnp.dot(normed_b, w_ref[0, :, part], preferred_element_type=f32)
            square = upper * upper
            bent = jnp.tanh(gelu_coef * upper * (1.0 + 0.044715 * square))
            half = 0.5 + 0.5 * bent
            hidden = (upper * half).astype(bf16)
            hidden_out[place, part] = hidden
            slope_out[place, part] = half + 0.5 * upper * (1.0 - bent * bent) * (
                gelu_coef * (1.0 + 3.0 * 0.044715 * square)
            )
            total = total + across(hidden, w_ref[1, :, part])
        out_ref[...] = total.astype(bf16)

    got = call(
        kernel,
        outs,
        [inputs, weights, *saved],
        {2 + i: 1 + i for i in range(len(saved))},
        flops=4 * rows * width * channels,
        transcendentals=rows * channels,
    )
    return got[0], got[1:]


def backward(turn, grad, weights, saved, kept, chunk, rows, tokens, last):
    width = grad.shape[1]
    channels = weights.shape[2]
    step = channels // slabs
    outs = [((2 * tokens, width), bf16), ((2 * tokens, channels), bf16)]
    if not last:
        outs = outs + [((rows, width), bf16)]

    def kernel(grad_ref, w_ref, x_ref, slope_ref, *refs):
        refs = refs[len(kept) :]
        grad_out, upper_out = refs[:2]
        place = pl.ds(pl.multiple_of(spot_of(turn, tokens) + chunk * rows, rows), rows)
        here = pl.ds(chunk * rows, rows)
        grad = rows_of(grad_ref, chunk, rows)
        grad_out[place, :] = grad
        total = jnp.zeros((rows, width), f32)
        for i in range(slabs):
            part = pl.ds(i * step, step)
            back_hidden = jnp.dot(grad, w_ref[1, :, part], preferred_element_type=f32)
            back_upper = (back_hidden * slope_ref[here, part]).astype(bf16)
            upper_out[place, part] = back_upper
            if not last:
                total = total + across(back_upper, w_ref[0, :, part])
        if not last:
            normed, scaled = normalize(x_ref[here, :])
            first = jnp.mean(total, axis=-1, keepdims=True)
            second = jnp.mean(total * normed, axis=-1, keepdims=True)
            refs[2][...] = (grad.astype(f32) + scaled * (total - first - normed * second)).astype(bf16)

    got = call(
        kernel,
        outs,
        [grad, weights, *saved, *kept],
        {4 + i: i for i in range(len(kept))},
        flops=(2 if last else 4) * rows * width * channels,
    )
    return (None if last else got[2]), got[:2]


def relay(token_ids, embed, weights, cotangent):
    count = lax.axis_size("section")
    micro, per_micro = token_ids.shape
    tokens = micro * per_micro
    chunks = 2 if micro % 2 == 0 else 1
    rows = tokens // chunks
    width = embed.shape[1]
    state = [embed_rows(token_ids, embed)] * chunks
    grads = [cotangent.reshape(tokens, width)] * chunks
    saved, kept = [], []

    def passed(array, source, target):
        return lax.ppermute(array, "section", [(source, target)])

    def back(hop, c):
        nonlocal kept
        out, kept = backward(hop, grads[c], weights, [saved[0], saved[3]], kept, c, rows, tokens, hop == 0)
        if hop:
            grads[c] = passed(out, hop, hop - 1)

    for hop in range(count):
        for c in range(chunks):
            out, saved = forward(hop, state[c], weights, saved, c, rows, tokens)
            if hop + 1 < count:
                state[c] = passed(out, hop, hop + 1)
            else:
                back(hop, c)
    for hop in range(count - 2, -1, -1):
        for c in range(chunks):
            back(hop, c)
    return saved[1], saved[2], kept[0], kept[1]


def along(array, pairs):
    return lax.ppermute(array, "dp", [(2 * a + c, 2 * b + c) for a, b in pairs for c in (0, 1)])


def swapped(array):
    return lax.ppermute(array, "dp", [(i, i ^ 1) for i in range(lax.axis_size("dp"))])


def known_mine(error, known, parts):
    owned, channels = parts[0][1].shape

    def kernel(error_ref, *refs):
        known_out, pass_out = refs[-2:]
        z, core = place_on_line()
        for slot, ((by, _), ref) in enumerate(zip(parts, refs[len(known) : -2])):
            block = 2 * ((z + by) & 3) + core
            rows = pl.ds(pl.multiple_of(block * owned, owned), owned)
            values = ref[...]
            pass_out[slot] = values
            known_out[block] = 0.9 * values.astype(f32) + error_ref[rows, :].astype(f32)

    return call(
        kernel,
        [((8, owned, channels), f32), ((len(parts), owned, channels), bf16)],
        [error, *known, *[a for _, a in parts]],
        {1: 0} if known else {},
    )


def known_other(error, known, parts):
    owned, _ = known.shape[1:]

    def kernel(error_ref, known_ref, *refs):
        z, core = place_on_line()
        for (by, _, slot), ref in zip(parts, refs):
            block = 2 * ((z + by) & 3) + 1 - core
            rows = pl.ds(pl.multiple_of(block * owned, owned), owned)
            refs[-1][block] = 0.9 * ref[slot].astype(f32) + error_ref[rows, :].astype(f32)

    return call(kernel, [(known.shape, f32)], [error, known, *[a for _, a, _ in parts]], {1: 0})[0]


def add_gradient(known, normed, upper, grad, hidden):
    blocks, owned, channels = known.shape
    tokens, width = normed.shape[0] // 2, normed.shape[1]
    step = channels // 4
    per = blocks // 2

    def kernel(known_ref, normed_ref, upper_ref, grad_ref, hidden_ref, out_ref, sum_ref):
        total = jnp.zeros((8, step), f32)
        for m, (left, right) in enumerate(((normed_ref, upper_ref), (grad_ref, hidden_ref))):
            turned = left[0:tokens, :].T
            for c in range(channels // step):
                part = pl.ds(c * step, step)
                gradient = jnp.dot(turned, right[0:tokens, part], preferred_element_type=f32)
                for b in range(per):
                    block = m * per + b
                    combined = known_ref[block, :, part] + 0.1 * gradient[b * owned : (b + 1) * owned]
                    out_ref[block, :, part] = combined
                    total = total + jnp.sum((combined * combined).reshape(owned // 8, 8, step), axis=0)
        sum_ref[...] = jnp.broadcast_to(jnp.sum(total, axis=(0, 1), keepdims=True), sum_ref.shape)

    return call(
        kernel,
        [(known.shape, f32), ((8, 128), f32)],
        [known, normed, upper, grad, hidden],
        {0: 0},
        limit=12,
        flops=4 * tokens * width * channels,
    )


def scale_of(sum_ref, count):
    scale = jnp.sqrt(sum_ref[0:1, 0:1] * (1.0 / count) + 0.01)
    return scale, 1.0 / scale


def chips_in_order(z):
    upper_half = z >> 1
    return (3 - 3 * upper_half, 2 - upper_half, z ^ 1, z)


def packed_part(sums, combined, places):
    blocks, owned, channels = combined.shape
    count = blocks * owned * channels

    def kernel(sum_ref, combined_ref, *outs):
        z, core = place_on_line()
        order = chips_in_order(z)
        scale, inverse = scale_of(sum_ref, count)
        for i, place in enumerate(places):
            for j, side in enumerate((1 - core, core)):
                values = combined_ref[2 * order[place] + side]
                outs[2 * i + j][...] = (scale * jnp.tanh(values * inverse)).astype(bf16)

    return call(
        kernel,
        [((owned, channels), bf16)] * (2 * len(places)),
        [sums, combined],
        transcendentals=2 * len(places) * owned * channels,
    )


def fresh_worker(sums, combined):
    blocks, owned, channels = combined.shape
    count = blocks * owned * channels

    def kernel(sum_ref, combined_ref, out_ref, made, done):
        scale, inverse = scale_of(sum_ref, count)
        copies = []
        for b in range(blocks):
            values = combined_ref[b]
            packed = (scale * jnp.tanh(values * inverse)).astype(bf16)
            made[b] = (values - packed.astype(f32)).astype(bf16)
            copies.append(pltpu.make_async_copy(made.at[b], out_ref.at[pl.ds(b * owned, owned), :], done.at[b]))
            copies[-1].start()
        for copy in copies:
            copy.wait()

    return call(
        kernel,
        [],
        [sums, combined],
        transcendentals=count,
        written=[((blocks * owned, channels), bf16)],
        scratch=[pltpu.VMEM((blocks, owned, channels), bf16), pltpu.SemaphoreType.DMA((blocks,))],
    )[0]


def added(*arrays):
    def kernel(*refs):
        total = refs[0][...].astype(f32)
        for ref in refs[1:-1]:
            total = total + ref[...].astype(f32)
        refs[-1][...] = total.astype(bf16)

    return call(kernel, [(arrays[0].shape, bf16)], list(arrays))[0]


def server(parts, error, variance, weights, replicas):
    owned, channels = error.shape
    per = weights.shape[1] // owned
    cuts = 4 if owned % 64 == 0 else 1
    rows = owned // cuts

    def kernel(error_ref, variance_ref, weights_ref, *refs):
        parts, outs, (merged_ref, w_made, m_made, e_made, done) = refs[:-8], refs[-8:-5], refs[-5:]
        squares = jnp.zeros((8, channels), f32)
        for i in range(cuts):
            here = pl.ds(i * rows, rows)
            total = parts[0][here, :].astype(f32)
            for ref in parts[1:]:
                total = total + ref[here, :].astype(f32)
            merged = total * (1.0 / replicas) + error_ref[here, :]
            merged_ref[here, :] = merged
            squares = squares + jnp.sum((merged * merged).reshape(rows // 8, 8, channels), axis=0)
        mean = jnp.sum(squares, axis=(0, 1), keepdims=True) * (1.0 / (owned * channels))
        scale = jnp.sqrt(mean + 0.01)
        inverse = 1.0 / scale
        rank = lax.axis_index("dp")
        matrix = jnp.where(rank >= per, 1, 0)
        first = (rank - per * matrix) * owned
        copies = []
        for i in range(cuts):
            here = pl.ds(i * rows, rows)
            merged = merged_ref[here, :]
            values = (scale * jnp.tanh(merged * inverse)).astype(bf16)
            m_made[here, :] = values
            wide = values.astype(f32)
            e_made[here, :] = merged - wide
            own = weights_ref[matrix, pl.ds(pl.multiple_of(first + i * rows, rows), rows), :].astype(f32)
            step = 0.01 * wide / (jnp.sqrt(variance_ref[here, :].astype(f32)) + 1e-08)
            w_made[here, :] = (own - step).astype(bf16)
            for j, made in enumerate((w_made, m_made, e_made)):
                copies.append(pltpu.make_async_copy(made.at[here, :], outs[j].at[here, :], done.at[3 * i + j]))
                copies[-1].start()
        for copy in copies:
            copy.wait()

    shape = (owned, channels)
    return call(
        kernel,
        [],
        [error, variance, weights, *parts],
        transcendentals=3 * owned * channels,
        written=[(shape, bf16), (shape, bf16), (shape, f32)],
        scratch=[
            pltpu.VMEM(shape, f32),
            pltpu.VMEM(shape, bf16),
            pltpu.VMEM(shape, bf16),
            pltpu.VMEM(shape, f32),
            pltpu.SemaphoreType.DMA((3 * cuts,)),
        ],
    )


def on_a_line(token_ids, embed, weights, variance, momentum, error, server_error, cotangent):
    replicas = lax.axis_size("dp")
    shared = {}
    for by in (2, 3, 1):
        shared[by] = along(momentum, [(i, (i + by) % 4) for i in range(4)])
    known, out_a = known_mine(error, [], [(0, momentum), (2, shared[2])])
    in_a = swapped(out_a)
    known, out_b = known_mine(error, [known], [(1, shared[3]), (3, shared[1])])
    in_b = swapped(out_b)
    normed, hidden, grad, upper = relay(token_ids, embed, weights, cotangent)
    known = known_other(error, known, [(0, in_a, 0), (2, in_a, 1), (1, in_b, 0), (3, in_b, 1)])
    combined, sums = add_gradient(known, normed, upper, grad, hidden)
    names = ("far", "mid", "near", "own")
    made = packed_part(sums, combined, (0,)) + packed_part(sums, combined, (1, 2, 3))
    mine, other = {}, {}
    for i, name in enumerate(names):
        mine[name] = made[2 * i + 1]
        other[name] = swapped(made[2 * i])

    def summed(name, pairs, *more):
        total = added(mine[name], other[name], *more)
        return along(total, pairs)

    ends, inner, outer = [(0, 1), (3, 2)], [(1, 2), (2, 1)], [(2, 3), (1, 0)]
    a1, a2, a3 = summed("far", ends), summed("mid", ends), summed("near", ends)
    b2 = summed("far", inner, a1)
    b3 = summed("mid", inner, a2)
    c3 = summed("near", outer, b2)
    new_worker = fresh_worker(sums, combined)
    new_weights, new_momentum, new_server = server(
        [mine["own"], other["own"], a3, b3, c3], server_error, variance, weights, replicas
    )
    return new_weights, new_momentum, new_worker, new_server


def in_general(token_ids, embed, weights, variance, momentum, error, server_error, cotangent):
    replicas = lax.axis_size("dp")
    width, channels = weights.shape[1:]
    owned = 2 * width // replicas
    tokens = token_ids.shape[0] * token_ids.shape[1]
    shared = lax.all_gather(momentum, "dp", axis=0, tiled=True)
    normed, hidden, grad, upper = relay(token_ids, embed, weights, cotangent)
    gradient = jnp.concatenate(
        [down(normed[:tokens], upper[:tokens]), down(grad[:tokens], hidden[:tokens])], axis=0
    )
    combined = 0.9 * shared.astype(f32) + 0.1 * gradient + error.astype(f32)
    worker_scale = jnp.sqrt(jnp.mean(combined * combined) + 0.01)
    packed = (worker_scale * jnp.tanh(combined / worker_scale)).astype(bf16)
    new_worker = (combined - packed.astype(f32)).astype(bf16)
    total = lax.psum_scatter(packed.astype(f32), "dp", scatter_dimension=0, tiled=True)
    merged = total / replicas + server_error
    server_scale = jnp.sqrt(jnp.mean(merged * merged) + 0.01)
    values = (server_scale * jnp.tanh(merged / server_scale)).astype(bf16)
    wide = values.astype(f32)
    start = lax.axis_index("dp") * owned
    own = lax.dynamic_slice_in_dim(weights.reshape(2 * width, channels), start, owned, 0)
    step = 0.01 * wide / (jnp.sqrt(variance.astype(f32)) + 1e-08)
    return (own.astype(f32) - step).astype(bf16), values, new_worker, merged - wide


def local(token_ids, embed, weights, variance, momentum, worker_error, server_error, cotangent):
    _, _, width, channels = weights.shape
    plan = on_a_line if lax.axis_size("dp") == 8 else in_general
    new_weights, values, new_worker, new_server = plan(
        token_ids,
        embed,
        weights[0],
        variance[0],
        momentum[0],
        worker_error.reshape(2 * width, channels),
        server_error[0],
        cotangent,
    )
    return new_weights[None], values[None], new_worker.reshape(worker_error.shape), new_server[None]


def solution(mesh):
    in_specs = (
        P(None, "dp"),
        P(),
        P("section", None, None, None),
        P("section", "dp", None),
        P("section", "dp", None),
        P("section", "dp", None, None, None),
        P("section", "dp", None),
        P(None, "dp", None),
    )
    out_specs = (
        P("section", "dp", None),
        P("section", "dp", None),
        P("section", "dp", None, None, None),
        P("section", "dp", None),
    )
    return jax.shard_map(local, mesh=mesh, in_specs=in_specs, out_specs=out_specs, check_vma=False)
```

time: 169 us -> 153 us (0.905)
  Pallas kernels: 49.6 us -> 36.6 us
  waiting for transfers between devices: 52.6 us -> 63.2 us
  starting transfers between devices: 55.7 us -> 46.4 us
  local copies, waits for them, and re-layouts: 9.16 us -> 5.04 us
    ppermute x12 -> x9, starting transfers between devices: 41.4 us -> 32 us  [along(): lax.ppermute(array, 'dp', [(2 * a + c, 2 * b + c) for a, b in pairs for c...]
    pallas_call x30 -> x31, Pallas kernels: 45.1 us -> 36.6 us  [call(): pl.pallas_call(kernel, out_shape=[pltpu.VMEM(shape, dtype) for shape, dty...]
    ppermute x12 -> x9, waiting for transfers between devices: 36.8 us -> 45 us  [along(): lax.ppermute(array, 'dp', [(2 * a + c, 2 * b + c) for a, b in pairs for c...]
    pallas_call x1 -> x0, Pallas kernels: 4.55 us -> none  [add_gradient(): pl.pallas_call(kernel, out_shape=[pltpu.VMEM(known.shape, f32), jax.Shape...]
    unnamed x22 -> x18, local copies, waits for them, and re-layouts: 9.07 us -> 5.04 us
    ppermute x12, waiting for transfers between devices: 15.8 us -> 18 us  [passed(): return lax.ppermute(array, 'section', [(source, target)])]
  transfers between devices with their start and end apart: 30 -> 27, of which waited for: 8 -> 9; matrix products, arithmetic and copies ran while one was open for 1% -> 0% of each run, Pallas kernels for 24% -> 20%
where the time goes in v2:
time: 153 us
  waiting for transfers between devices  63.2 us (41%)
  starting transfers between devices  46.4 us (30%)
  Pallas kernels  36.6 us (24%)
  local copies, waits for them, and re-layouts  5.04 us (3%)
    ppermute x9, waiting for transfers between devices, along(): lax.ppermute(array, 'dp', [(2 * a + c, 2 * b + c) for a, b in pairs for c...  45 us
    pallas_call x31, Pallas kernels, call(): pl.pallas_call(kernel, out_shape=[pltpu.VMEM(shape, dtype) for shape, dty...  36.6 us
    ppermute x9, starting transfers between devices, along(): lax.ppermute(array, 'dp', [(2 * a + c, 2 * b + c) for a, b in pairs for c...  32 us
    ppermute x12, waiting for transfers between devices, passed(): return lax.ppermute(array, 'section', [(source, target)])  18 us
    ppermute x12, starting transfers between devices, passed(): return lax.ppermute(array, 'section', [(source, target)])  13 us
    unnamed x18, local copies, waits for them, and re-layouts  5.04 us
  transfers between devices with their start and end apart: 27, of which 9 were waited for; matrix products, arithmetic and copies ran while one was open for 0% of the time, Pallas kernels for 20%

profile of v2, /device:TPU:0, one launch (start us, length us, event | category | flops | bytes accessed | tf_op | source)
XLA Modules:
  0.0 152.5 jit_solution(7525732755165980996)
XLA Ops:
  0.6 4.1 %collective-permute-start = (bf16[128,2048]{1,0:T(8,128)(2,1)}, bf16[128,2048]{1,0:T(8,128)(2,1)S(1)}, u32[]{:S(2)}, u32[]{:S(2)}) collective-permute-start(bf16[128,2048]{1,0:T(8,128)(2,1)} %bitcast.33), channel_id=1, source_target_pairs={{0,4},{1,5},{2,6},{3,7},{4,0},{5,1},{6,2},{7,3},{8,12},{9,13},{10,... | collective-permute-start | bytes 1572872 | tf_op jit(solution)/shard_map/ppermute | solution.py:198
  4.8 1.6 %collective-permute-start.2 = (bf16[128,2048]{1,0:T(8,128)(2,1)}, bf16[128,2048]{1,0:T(8,128)(2,1)S(1)}, u32[]{:S(2)}, u32[]{:S(2)}) collective-permute-start(bf16[128,2048]{1,0:T(8,128)(2,1)} %bitcast.34), channel_id=1, source_target_pairs={{0,2},{1,3},{2,4},{3,5},{4,6},{5,7},{6,0},{7,1},{8,10},{9,11},{10,... | collective-permute-start | bytes 1572872 | tf_op jit(solution)/shard_map/ppermute | solution.py:198
  6.3 2.2 %collective-permute-start.1 = (bf16[128,2048]{1,0:T(8,128)(2,1)}, bf16[128,2048]{1,0:T(8,128)(2,1)S(1)}, u32[]{:S(2)}, u32[]{:S(2)}) collective-permute-start(bf16[128,2048]{1,0:T(8,128)(2,1)} %bitcast.35), channel_id=1, source_target_pairs={{0,6},{1,7},{2,0},{3,1},{4,2},{5,3},{6,4},{7,5},{8,14},{9,15},{10,... | collective-permute-start | bytes 1572872 | tf_op jit(solution)/shard_map/ppermute | solution.py:198
  8.6 0.9 copy-done.7
  9.5 0.7 copy-done.8
  10.2 0.3 shard_map.114.x_ref
  10.4 2.2 %copy-done = bf16[1,2,512,2048]{3,2,1,0:T(8,128)(2,1)S(1)} copy-done((bf16[1,2,512,2048]{3,2,1,0:T(8,128)(2,1)S(1)}, bf16[1,2,512,2048]{3,2,1,0:T(8,128)(2,1)}, u32[]{:S(2)}) %copy-start) | copy-done | bytes 4194328
  12.6 1.7 %shard_map.115 = (bf16[128,512]{1,0:T(8,128)(2,1)S(1)}, bf16[512,512]{1,0:T(8,128)(2,1)S(1)}, bf16[512,512]{1,0:T(8,128)(2,1)S(1)}, bf16[512,2048]{1,0:T(8,128)(2,1)S(1)}, f32[512,2048]{1,0:T(8,128)S(1)}) custom-call(bf16[256,512]{1,0:T(8,128)(2,1)S(1)} %shard_map.114.x_ref, bf16[2,512,2048]{2,1,0:T(8,128)(2,1)S(1)} %bitcast.10), custom_call_target="tpu_custom_call" | custom-call | flops 536870912 | bytes 4456448 | tf_op jit(solution)/shard_map/pallas_call | solution.py:23
  14.3 3.4 %collective-permute-start.6 = (bf16[128,512]{1,0:T(8,128)(2,1)S(1)}, bf16[128,512]{1,0:T(8,128)(2,1)S(1)}, u32[]{:S(2)}, u32[]{:S(2)}) collective-permute-start(bf16[128,512]{1,0:T(8,128)(2,1)S(1)} %get-tuple-element.90), channel_id=1, source_target_pairs={{0,8},{1,9},{2,10},{3,11},{4,12},{5,13},{6,14},{7,15}} | collective-permute-start | bytes 393224 | tf_op jit(solution)/shard_map/ppermute | solution.py:176
  17.8 1.7 %shard_map.116 = (bf16[128,512]{1,0:T(8,128)(2,1)S(1)}, bf16[512,512]{1,0:T(8,128)(2,1)S(1)}, bf16[512,512]{1,0:T(8,128)(2,1)S(1)}, bf16[512,2048]{1,0:T(8,128)(2,1)S(1)}, f32[512,2048]{1,0:T(8,128)S(1)}) custom-call(bf16[256,512]{1,0:T(8,128)(2,1)S(1)} %shard_map.114.x_ref, ...), custom_call_target="tpu_custom_call", output_to_operand_aliasing={{1}: (2, {}), {2}: (3, {}), {3}: (4, {}), {4}: (5, {})} | custom-call | flops 536870912 | bytes 11796480 | tf_op jit(solution)/shard_map/pallas_call | solution.py:23
  19.5 1.3 collective-permute-start.5
  20.8 19.5 %collective-permute-done.refs_1_ = bf16[128,2048]{1,0:T(8,128)(2,1)S(1)} collective-permute-done((bf16[128,2048]{1,0:T(8,128)(2,1)}, bf16[128,2048]{1,0:T(8,128)(2,1)S(1)}, u32[]{:S(2)}, u32[]{:S(2)}) %collective-permute-start) | collective-permute-done | bytes 524320 | tf_op jit(solution)/shard_map/ppermute | solution.py:198
  40.3 0.4 shard_map.111
  40.7 0.3 collective-permute-done.1.refs_1_
  41.0 0.4 shard_map.112
  41.4 0.5 collective-permute-start.3
  41.9 1.2 copy-done.1
  43.1 1.7 %shard_map.117 = (bf16[128,512]{1,0:T(8,128)(2,1)S(1)}, bf16[512,512]{1,0:T(8,128)(2,1)S(1)}, bf16[512,512]{1,0:T(8,128)(2,1)S(1)}, bf16[512,2048]{1,0:T(8,128)(2,1)S(1)}, f32[512,2048]{1,0:T(8,128)S(1)}) custom-call(bf16[128,512]{1,0:T(8,128)(2,1)S(1)} %collective-permute-done.6.x_ref, ...), custom_call_target="tpu_custom_call", output_to_operand_aliasing={{1}: (2, {}), {2}: (3, {}), {3}: (4, {}), {4}: (5, {})} | custom-call | flops 536870912 | bytes 11665408 | tf_op jit(solution)/shard_map/pallas_call | solution.py:23
  44.9 0.7 collective-permute-start.8
  45.6 1.7 %shard_map.118 = (bf16[128,512]{1,0:T(8,128)(2,1)S(1)}, bf16[512,512]{1,0:T(8,128)(2,1)S(1)}, bf16[512,512]{1,0:T(8,128)(2,1)S(1)}, bf16[512,2048]{1,0:T(8,128)(2,1)S(1)}, f32[512,2048]{1,0:T(8,128)S(1)}) custom-call(bf16[128,512]{1,0:T(8,128)(2,1)S(1)} %collective-permute-done.5.x_ref, ...), custom_call_target="tpu_custom_call", output_to_operand_aliasing={{1}: (2, {}), {2}: (3, {}), {3}: (4, {}), {4}: (5, {})} | custom-call | flops 536870912 | bytes 11665408 | tf_op jit(solution)/shard_map/pallas_call | solution.py:23
  47.3 0.7 collective-permute-start.7
  48.0 1.7 %shard_map.119 = (bf16[128,512]{1,0:T(8,128)(2,1)S(1)}, bf16[512,512]{1,0:T(8,128)(2,1)S(1)}, bf16[512,512]{1,0:T(8,128)(2,1)S(1)}, bf16[512,2048]{1,0:T(8,128)(2,1)S(1)}, f32[512,2048]{1,0:T(8,128)S(1)}) custom-call(bf16[128,512]{1,0:T(8,128)(2,1)S(1)} %collective-permute-done.8.x_ref, ...), custom_call_target="tpu_custom_call", output_to_operand_aliasing={{1}: (2, {}), {2}: (3, {}), {3}: (4, {}), {4}: (5, {})} | custom-call | flops 536870912 | bytes 11665408 | tf_op jit(solution)/shard_map/pallas_call | solution.py:23
  49.7 0.7 collective-permute-start.10
  50.4 1.7 %shard_map.120 = (bf16[128,512]{1,0:T(8,128)(2,1)S(1)}, bf16[512,512]{1,0:T(8,128)(2,1)S(1)}, bf16[512,512]{1,0:T(8,128)(2,1)S(1)}, bf16[512,2048]{1,0:T(8,128)(2,1)S(1)}, f32[512,2048]{1,0:T(8,128)S(1)}) custom-call(bf16[128,512]{1,0:T(8,128)(2,1)S(1)} %collective-permute-done.7.x_ref, ...), custom_call_target="tpu_custom_call", output_to_operand_aliasing={{1}: (2, {}), {2}: (3, {}), {3}: (4, {}), {4}: (5, {})} | custom-call | flops 536870912 | bytes 11665408 | tf_op jit(solution)/shard_map/pallas_call | solution.py:23
  52.1 0.8 collective-permute-start.9
  53.0 2.4 %shard_map.121 = (bf16[128,512]{1,0:T(8,128)(2,1)}, bf16[512,512]{1,0:T(8,128)(2,1)S(1)}, bf16[512,512]{1,0:T(8,128)(2,1)S(1)}, bf16[512,2048]{1,0:T(8,128)(2,1)S(1)}, f32[512,2048]{1,0:T(8,128)S(1)}) custom-call(bf16[128,512]{1,0:T(8,128)(2,1)S(1)} %collective-permute-done.10.x_ref, ...), custom_call_target="tpu_custom_call", output_to_operand_aliasing={{1}: (2, {}), {2}: (3, {}), {3}: (4, {}), {4}: (5, {})} | custom-call | flops 536870912 | bytes 11665408 | tf_op jit(solution)/shard_map/pallas_call | solution.py:23
  55.4 1.2 shard_map.123
  56.7 0.7 collective-permute-start.12
  57.4 2.4 %shard_map.122 = (bf16[128,512]{1,0:T(8,128)(2,1)}, bf16[512,512]{1,0:T(8,128)(2,1)S(1)}, bf16[512,512]{1,0:T(8,128)(2,1)S(1)}, bf16[512,2048]{1,0:T(8,128)(2,1)S(1)}, f32[512,2048]{1,0:T(8,128)S(1)}) custom-call(bf16[128,512]{1,0:T(8,128)(2,1)S(1)} %collective-permute-done.9.x_ref, ...), custom_call_target="tpu_custom_call", output_to_operand_aliasing={{1}: (2, {}), {2}: (3, {}), {3}: (4, {}), {4}: (5, {})} | custom-call | flops 536870912 | bytes 11665408 | tf_op jit(solution)/shard_map/pallas_call | solution.py:23
  59.7 1.2 shard_map.124
  61.0 0.7 collective-permute-start.11
  61.7 1.2 shard_map.125
  62.9 0.7 collective-permute-start.14
  63.6 1.2 shard_map.126
  64.9 0.7 collective-permute-start.13
  65.6 1.2 shard_map.127
  66.8 1.3 collective-permute-start.16
  68.1 1.2 shard_map.128
  69.4 1.5 collective-permute-start.15
  70.9 15.7 %collective-permute-done.16.grad_ref = bf16[128,512]{1,0:T(8,128)(2,1)S(1)} collective-permute-done((bf16[128,512]{1,0:T(8,128)(2,1)S(1)}, bf16[128,512]{1,0:T(8,128)(2,1)S(1)}, u32[]{:S(2)}, u32[]{:S(2)}) %collective-permute-start.16) | collective-permute-done | bytes 131104 | tf_op jit(solution)/shard_map/ppermute | solution.py:176
  86.6 0.5 shard_map.129
  87.0 2.3 %collective-permute-done.15.grad_ref = bf16[128,512]{1,0:T(8,128)(2,1)S(1)} collective-permute-done((bf16[128,512]{1,0:T(8,128)(2,1)S(1)}, bf16[128,512]{1,0:T(8,128)(2,1)S(1)}, u32[]{:S(2)}, u32[]{:S(2)}) %collective-permute-start.15) | collective-permute-done | bytes 131104 | tf_op jit(solution)/shard_map/ppermute | solution.py:176
  89.3 0.4 shard_map.130
  89.8 0.6 shard_map.113.known_ref
  90.4 2.8 %shard_map.131 = (f32[8,128,2048]{2,1,0:T(8,128)S(1)}, f32[8,128]{1,0:T(8,128)S(1)}) custom-call(f32[8,128,2048]{2,1,0:T(8,128)S(1)} %shard_map.113.known_ref, bf16[512,512]{1,0:T(8,128)(2,1)S(1)} %get-tuple-element.119.normed_ref, bf16[512,2048]{1,0:T(8,128)(2,1)S(1)} %get-tuple-element.142.upper_ref, ...), custom_call_target="tpu_custom_call", output_to_operand_aliasing={{0}: (0, {})} | custom-call | flops 1073741824 | bytes 13631488 | tf_op jit(solution)/shard_map/pallas_call | solution.py:23
  93.2 0.4 shard_map.136
  93.7 1.1 shard_map.132
  94.9 0.6 collective-permute-start.20
  95.4 0.2 collective-permute-done.23.refs_1_
  95.8 11.8 %collective-permute-start.24 = (bf16[128,2048]{1,0:T(8,128)(2,1)S(1)}, bf16[128,2048]{1,0:T(8,128)(2,1)S(1)}, u32[]{:S(2)}, u32[]{:S(2)}) collective-permute-start(bf16[128,2048]{1,0:T(8,128)(2,1)S(1)} %shard_map.137), channel_id=1, source_target_pairs={{0,2},{1,3},{6,4},{7,5},{8,10},{9,11},{14,12},{15,13},{16,18},{17,... | collective-permute-start | bytes 1572872 | tf_op jit(solution)/shard_map/ppermute | solution.py:198
  107.8 1.4 collective-permute-start.21
  109.2 10.6 %collective-permute-done.24.refs_2_ = bf16[128,2048]{1,0:T(8,128)(2,1)S(1)} collective-permute-done((bf16[128,2048]{1,0:T(8,128)(2,1)S(1)}, bf16[128,2048]{1,0:T(8,128)(2,1)S(1)}, u32[]{:S(2)}, u32[]{:S(2)}) %collective-permute-start.24) | collective-permute-done | bytes 524320 | tf_op jit(solution)/shard_map/ppermute | solution.py:198
  119.9 0.2 shard_map.138
  120.1 0.7 collective-permute-start.25
  121.0 8.0 %collective-permute-start.19 = (bf16[128,2048]{1,0:T(8,128)(2,1)S(1)}, bf16[128,2048]{1,0:T(8,128)(2,1)S(1)}, u32[]{:S(2)}, u32[]{:S(2)}) collective-permute-start(bf16[128,2048]{1,0:T(8,128)(2,1)S(1)} %shard_map.133), channel_id=1, source_target_pairs={{0,2},{1,3},{6,4},{7,5},{8,10},{9,11},{14,12},{15,13},{16,18},{17,... | collective-permute-start | bytes 1572872 | tf_op jit(solution)/shard_map/ppermute | solution.py:198
  129.0 2.0 %collective-permute-done.21.refs_2_ = bf16[128,2048]{1,0:T(8,128)(2,1)S(1)} collective-permute-done((bf16[128,2048]{1,0:T(8,128)(2,1)S(1)}, bf16[128,2048]{1,0:T(8,128)(2,1)S(1)}, u32[]{:S(2)}, u32[]{:S(2)}) %collective-permute-start.21) | collective-permute-done | bytes 524320 | tf_op jit(solution)/shard_map/ppermute | solution.py:198
  131.0 0.2 shard_map.135
  131.2 0.7 collective-permute-start.22
  131.9 0.2 shard_map.139
  132.1 1.4 collective-permute-start.26
  133.5 3.8 %shard_map.141 = bf16[1024,2048]{1,0:T(8,128)(2,1)} custom-call(f32[8,128]{1,0:T(8,128)S(1)} %get-tuple-element.145.sum_ref, f32[8,128,2048]{2,1,0:T(8,128)S(1)} %get-tuple-element.146.combined_ref), custom_call_target="tpu_custom_call" | custom-call | bytes 8392704 | tf_op jit(solution)/shard_map/pallas_call | solution.py:23
  137.4 4.1 %collective-permute-done.19.refs_2_ = bf16[128,2048]{1,0:T(8,128)(2,1)S(1)} collective-permute-done((bf16[128,2048]{1,0:T(8,128)(2,1)S(1)}, bf16[128,2048]{1,0:T(8,128)(2,1)S(1)}, u32[]{:S(2)}, u32[]{:S(2)}) %collective-permute-start.19) | collective-permute-done | bytes 524320 | tf_op jit(solution)/shard_map/ppermute | solution.py:198
  141.5 8.5 %collective-permute-done.26.refs_4_ = bf16[128,2048]{1,0:T(8,128)(2,1)S(1)} collective-permute-done((bf16[128,2048]{1,0:T(8,128)(2,1)S(1)}, bf16[128,2048]{1,0:T(8,128)(2,1)S(1)}, u32[]{:S(2)}, u32[]{:S(2)}) %collective-permute-start.26) | collective-permute-done | bytes 524320 | tf_op jit(solution)/shard_map/ppermute | solution.py:198
  150.0 2.4 %shard_map.140 = (bf16[128,2048]{1,0:T(8,128)(2,1)}, bf16[128,2048]{1,0:T(8,128)(2,1)}, f32[128,2048]{1,0:T(8,128)}) custom-call(f32[128,2048]{1,0:T(8,128)S(1)} %bitcast.32, bf16[128,2048]{1,0:T(8,128)(2,1)S(1)} %bitcast.37, bf16[2,512,2048]{2,1,0:T(8,128)(2,1)S(1)} %bitcast.26, bf16[128,2048]{1,0:T(8,128)(2,1)S(1)} %get-tuple-element.147.refs_0_, ...), custom_call_target="tpu_custom_call" | custom-call | bytes 8388608 | tf_op jit(solution)/shard_map/pallas_call | solution.py:23
  (39 shorter events, 0.7 us)
Async XLA Ops:
  0.6 39.6 %collective-permute-start = (bf16[128,2048]{1,0:T(8,128)(2,1)}, bf16[128,2048]{1,0:T(8,128)(2,1)S(1)}, u32[]{:S(2)}, u32[]{:S(2)}) collective-permute-start(bf16[128,2048]{1,0:T(8,128)(2,1)} %bitcast.33), channel_id=1, source_target_pairs={{0,4},{1,5},{2,6},{3,7},{4,0},{5,1},{6,2},{7,3},{8,12},{9,13},{10,... | collective-permute-start | bytes 1572872 | tf_op jit(solution)/shard_map/ppermute | solution.py:198
  4.8 35.9 %collective-permute-start.2 = (bf16[128,2048]{1,0:T(8,128)(2,1)}, bf16[128,2048]{1,0:T(8,128)(2,1)S(1)}, u32[]{:S(2)}, u32[]{:S(2)}) collective-permute-start(bf16[128,2048]{1,0:T(8,128)(2,1)} %bitcast.34), channel_id=1, source_target_pairs={{0,2},{1,3},{2,4},{3,5},{4,6},{5,7},{6,0},{7,1},{8,10},{9,11},{10,... | collective-permute-start | bytes 1572872 | tf_op jit(solution)/shard_map/ppermute | solution.py:198
  6.3 34.6 %collective-permute-start.1 = (bf16[128,2048]{1,0:T(8,128)(2,1)}, bf16[128,2048]{1,0:T(8,128)(2,1)S(1)}, u32[]{:S(2)}, u32[]{:S(2)}) collective-permute-start(bf16[128,2048]{1,0:T(8,128)(2,1)} %bitcast.35), channel_id=1, source_target_pairs={{0,6},{1,7},{2,0},{3,1},{4,2},{5,3},{6,4},{7,5},{8,14},{9,15},{10,... | collective-permute-start | bytes 1572872 | tf_op jit(solution)/shard_map/ppermute | solution.py:198
  8.6 0.9 copy-start.7
  9.5 0.7 copy-start.8
  10.4 2.2 %copy-start = (bf16[1,2,512,2048]{3,2,1,0:T(8,128)(2,1)S(1)}, bf16[1,2,512,2048]{3,2,1,0:T(8,128)(2,1)}, u32[]{:S(2)}) copy-start(bf16[1,2,512,2048]{3,2,1,0:T(8,128)(2,1)} %param.10) | copy-start | bytes 12582916
  14.3 27.6 %collective-permute-start.6 = (bf16[128,512]{1,0:T(8,128)(2,1)S(1)}, bf16[128,512]{1,0:T(8,128)(2,1)S(1)}, u32[]{:S(2)}, u32[]{:S(2)}) collective-permute-start(bf16[128,512]{1,0:T(8,128)(2,1)S(1)} %get-tuple-element.90), channel_id=1, source_target_pairs={{0,8},{1,9},{2,10},{3,11},{4,12},{5,13},{6,14},{7,15}} | collective-permute-start | bytes 393224 | tf_op jit(solution)/shard_map/ppermute | solution.py:176
  17.7 22.5 %copy-start.2 = (bf16[1,1,2,512,2048]{4,3,2,1,0:T(8,128)(2,1)S(1)}, bf16[1,1,2,512,2048]{4,3,2,1,0:T(8,128)(2,1)}, u32[]{:S(2)}) copy-start(bf16[1,1,2,512,2048]{4,3,2,1,0:T(8,128)(2,1)} %param.13) | copy-start | bytes 12582916
  17.8 22.5 %copy-start.5 = (bf16[1,128,2048]{2,1,0:T(8,128)(2,1)S(1)}, bf16[1,128,2048]{2,1,0:T(8,128)(2,1)}, u32[]{:S(2)}) copy-start(bf16[1,128,2048]{2,1,0:T(8,128)(2,1)} %param.12) | copy-start | bytes 1572868
  19.5 26.0 %collective-permute-start.5 = (bf16[128,512]{1,0:T(8,128)(2,1)S(1)}, bf16[128,512]{1,0:T(8,128)(2,1)S(1)}, u32[]{:S(2)}, u32[]{:S(2)}) collective-permute-start(bf16[128,512]{1,0:T(8,128)(2,1)S(1)} %get-tuple-element.89), channel_id=1, source_target_pairs={{0,8},{1,9},{2,10},{3,11},{4,12},{5,13},{6,14},{7,15}} | collective-permute-start | bytes 393224 | tf_op jit(solution)/shard_map/ppermute | solution.py:176
  41.0 2.2 %copy-start.1 = (bf16[1,2,512,2048]{3,2,1,0:T(8,128)(2,1)S(1)}, bf16[1,2,512,2048]{3,2,1,0:T(8,128)(2,1)}, u32[]{:S(2)}) copy-start(bf16[1,2,512,2048]{3,2,1,0:T(8,128)(2,1)} %param.10) | copy-start | bytes 12582916
  41.3 48.5 %collective-permute-start.4 = (bf16[2,128,2048]{2,1,0:T(8,128)(2,1)S(1)}, bf16[2,128,2048]{2,1,0:T(8,128)(2,1)S(1)}, u32[]{:S(2)}, u32[]{:S(2)}) collective-permute-start(bf16[2,128,2048]{2,1,0:T(8,128)(2,1)S(1)} %get-tuple-element.84), channel_id=1, source_target_pairs={{0,1},{1,0},{2,3},{3,2},{4,5},{5,4},{6,7},{7,6},{8,9},{9,8},{10,11... | collective-permute-start | bytes 3145736 | tf_op jit(solution)/shard_map/ppermute | solution.py:202
  41.4 48.4 %collective-permute-start.3 = (bf16[2,128,2048]{2,1,0:T(8,128)(2,1)S(1)}, bf16[2,128,2048]{2,1,0:T(8,128)(2,1)S(1)}, u32[]{:S(2)}, u32[]{:S(2)}) collective-permute-start(bf16[2,128,2048]{2,1,0:T(8,128)(2,1)S(1)} %get-tuple-element.83), channel_id=1, source_target_pairs={{0,1},{1,0},{2,3},{3,2},{4,5},{5,4},{6,7},{7,6},{8,9},{9,8},{10,11... | collective-permute-start | bytes 3145736 | tf_op jit(solution)/shard_map/ppermute | solution.py:202
  44.9 3.1 %collective-permute-start.8 = (bf16[128,512]{1,0:T(8,128)(2,1)S(1)}, bf16[128,512]{1,0:T(8,128)(2,1)S(1)}, u32[]{:S(2)}, u32[]{:S(2)}) collective-permute-start(bf16[128,512]{1,0:T(8,128)(2,1)S(1)} %get-tuple-element.100), channel_id=1, source_target_pairs={{8,16},{9,17},{10,18},{11,19},{12,20},{13,21},{14,22},{15,23}} | collective-permute-start | bytes 393224 | tf_op jit(solution)/shard_map/ppermute | solution.py:176
  47.3 3.1 %collective-permute-start.7 = (bf16[128,512]{1,0:T(8,128)(2,1)S(1)}, bf16[128,512]{1,0:T(8,128)(2,1)S(1)}, u32[]{:S(2)}, u32[]{:S(2)}) collective-permute-start(bf16[128,512]{1,0:T(8,128)(2,1)S(1)} %get-tuple-element.99), channel_id=1, source_target_pairs={{8,16},{9,17},{10,18},{11,19},{12,20},{13,21},{14,22},{15,23}} | collective-permute-start | bytes 393224 | tf_op jit(solution)/shard_map/ppermute | solution.py:176
  49.7 3.3 %collective-permute-start.10 = (bf16[128,512]{1,0:T(8,128)(2,1)S(1)}, bf16[128,512]{1,0:T(8,128)(2,1)S(1)}, u32[]{:S(2)}, u32[]{:S(2)}) collective-permute-start(bf16[128,512]{1,0:T(8,128)(2,1)S(1)} %get-tuple-element.110), channel_id=1, source_target_pairs={{16,24},{17,25},{18,26},{19,27},{20,28},{21,29},{22,30},{23,31}} | collective-permute-start | bytes 393224 | tf_op jit(solution)/shard_map/ppermute | solution.py:176
  52.1 5.2 %collective-permute-start.9 = (bf16[128,512]{1,0:T(8,128)(2,1)S(1)}, bf16[128,512]{1,0:T(8,128)(2,1)S(1)}, u32[]{:S(2)}, u32[]{:S(2)}) collective-permute-start(bf16[128,512]{1,0:T(8,128)(2,1)S(1)} %get-tuple-element.109), channel_id=1, source_target_pairs={{16,24},{17,25},{18,26},{19,27},{20,28},{21,29},{22,30},{23,31}} | collective-permute-start | bytes 393224 | tf_op jit(solution)/shard_map/ppermute | solution.py:176
  53.0 2.4 %copy-start.3 = (bf16[4,64,512]{2,1,0:T(8,128)(2,1)S(1)}, bf16[4,64,512]{2,1,0:T(8,128)(2,1)}, u32[]{:S(2)}) copy-start(bf16[4,64,512]{2,1,0:T(8,128)(2,1)} %param.15) | copy-start | bytes 786436
  56.7 5.0 %collective-permute-start.12 = (bf16[128,512]{1,0:T(8,128)(2,1)S(1)}, bf16[128,512]{1,0:T(8,128)(2,1)S(1)}, u32[]{:S(2)}, u32[]{:S(2)}) collective-permute-start(bf16[128,512]{1,0:T(8,128)(2,1)S(1)} %get-tuple-element.125), channel_id=1, source_target_pairs={{24,16},{25,17},{26,18},{27,19},{28,20},{29,21},{30,22},{31,23}} | collective-permute-start | bytes 393224 | tf_op jit(solution)/shard_map/ppermute | solution.py:176
  61.0 2.6 %collective-permute-start.11 = (bf16[128,512]{1,0:T(8,128)(2,1)S(1)}, bf16[128,512]{1,0:T(8,128)(2,1)S(1)}, u32[]{:S(2)}, u32[]{:S(2)}) collective-permute-start(bf16[128,512]{1,0:T(8,128)(2,1)S(1)} %get-tuple-element.124), channel_id=1, source_target_pairs={{24,16},{25,17},{26,18},{27,19},{28,20},{29,21},{30,22},{31,23}} | collective-permute-start | bytes 393224 | tf_op jit(solution)/shard_map/ppermute | solution.py:176
  62.9 2.6 %collective-permute-start.14 = (bf16[128,512]{1,0:T(8,128)(2,1)S(1)}, bf16[128,512]{1,0:T(8,128)(2,1)S(1)}, u32[]{:S(2)}, u32[]{:S(2)}) collective-permute-start(bf16[128,512]{1,0:T(8,128)(2,1)S(1)} %get-tuple-element.131), channel_id=1, source_target_pairs={{16,8},{17,9},{18,10},{19,11},{20,12},{21,13},{22,14},{23,15}} | collective-permute-start | bytes 393224 | tf_op jit(solution)/shard_map/ppermute | solution.py:176
  64.9 3.2 %collective-permute-start.13 = (bf16[128,512]{1,0:T(8,128)(2,1)S(1)}, bf16[128,512]{1,0:T(8,128)(2,1)S(1)}, u32[]{:S(2)}, u32[]{:S(2)}) collective-permute-start(bf16[128,512]{1,0:T(8,128)(2,1)S(1)} %get-tuple-element.130), channel_id=1, source_target_pairs={{16,8},{17,9},{18,10},{19,11},{20,12},{21,13},{22,14},{23,15}} | collective-permute-start | bytes 393224 | tf_op jit(solution)/shard_map/ppermute | solution.py:176
  66.8 19.8 %collective-permute-start.16 = (bf16[128,512]{1,0:T(8,128)(2,1)S(1)}, bf16[128,512]{1,0:T(8,128)(2,1)S(1)}, u32[]{:S(2)}, u32[]{:S(2)}) collective-permute-start(bf16[128,512]{1,0:T(8,128)(2,1)S(1)} %get-tuple-element.137), channel_id=1, source_target_pairs={{8,0},{9,1},{10,2},{11,3},{12,4},{13,5},{14,6},{15,7}} | collective-permute-start | bytes 393224 | tf_op jit(solution)/shard_map/ppermute | solution.py:176
  69.4 20.0 %collective-permute-start.15 = (bf16[128,512]{1,0:T(8,128)(2,1)S(1)}, bf16[128,512]{1,0:T(8,128)(2,1)S(1)}, u32[]{:S(2)}, u32[]{:S(2)}) collective-permute-start(bf16[128,512]{1,0:T(8,128)(2,1)S(1)} %get-tuple-element.136), channel_id=1, source_target_pairs={{8,0},{9,1},{10,2},{11,3},{12,4},{13,5},{14,6},{15,7}} | collective-permute-start | bytes 393224 | tf_op jit(solution)/shard_map/ppermute | solution.py:176
  93.7 2.0 %collective-permute-start.23 = (bf16[128,2048]{1,0:T(8,128)(2,1)S(1)}, bf16[128,2048]{1,0:T(8,128)(2,1)S(1)}, u32[]{:S(2)}, u32[]{:S(2)}) collective-permute-start(bf16[128,2048]{1,0:T(8,128)(2,1)S(1)} %get-tuple-element.154), channel_id=1, source_target_pairs={{0,1},{1,0},{2,3},{3,2},{4,5},{5,4},{6,7},{7,6},{8,9},{9,8},{10,11... | collective-permute-start | bytes 1572872 | tf_op jit(solution)/shard_map/ppermute | solution.py:202
  94.9 12.8 %collective-permute-start.20 = (bf16[128,2048]{1,0:T(8,128)(2,1)S(1)}, bf16[128,2048]{1,0:T(8,128)(2,1)S(1)}, u32[]{:S(2)}, u32[]{:S(2)}) collective-permute-start(bf16[128,2048]{1,0:T(8,128)(2,1)S(1)} %get-tuple-element.152), channel_id=1, source_target_pairs={{0,1},{1,0},{2,3},{3,2},{4,5},{5,4},{6,7},{7,6},{8,9},{9,8},{10,11... | collective-permute-start | bytes 1572872 | tf_op jit(solution)/shard_map/ppermute | solution.py:202
  95.8 24.1 %collective-permute-start.24 = (bf16[128,2048]{1,0:T(8,128)(2,1)S(1)}, bf16[128,2048]{1,0:T(8,128)(2,1)S(1)}, u32[]{:S(2)}, u32[]{:S(2)}) collective-permute-start(bf16[128,2048]{1,0:T(8,128)(2,1)S(1)} %shard_map.137), channel_id=1, source_target_pairs={{0,2},{1,3},{6,4},{7,5},{8,10},{9,11},{14,12},{15,13},{16,18},{17,... | collective-permute-start | bytes 1572872 | tf_op jit(solution)/shard_map/ppermute | solution.py:198
  107.6 13.2 %collective-permute-start.18 = (bf16[128,2048]{1,0:T(8,128)(2,1)S(1)}, bf16[128,2048]{1,0:T(8,128)(2,1)S(1)}, u32[]{:S(2)}, u32[]{:S(2)}) collective-permute-start(bf16[128,2048]{1,0:T(8,128)(2,1)S(1)} %get-tuple-element.150), channel_id=1, source_target_pairs={{0,1},{1,0},{2,3},{3,2},{4,5},{5,4},{6,7},{7,6},{8,9},{9,8},{10,11... | collective-permute-start | bytes 1572872 | tf_op jit(solution)/shard_map/ppermute | solution.py:202
  107.8 23.2 %collective-permute-start.21 = (bf16[128,2048]{1,0:T(8,128)(2,1)S(1)}, bf16[128,2048]{1,0:T(8,128)(2,1)S(1)}, u32[]{:S(2)}, u32[]{:S(2)}) collective-permute-start(bf16[128,2048]{1,0:T(8,128)(2,1)S(1)} %shard_map.134), channel_id=1, source_target_pairs={{0,2},{1,3},{6,4},{7,5},{8,10},{9,11},{14,12},{15,13},{16,18},{17,... | collective-permute-start | bytes 1572872 | tf_op jit(solution)/shard_map/ppermute | solution.py:198
  120.1 11.8 %collective-permute-start.25 = (bf16[128,2048]{1,0:T(8,128)(2,1)S(1)}, bf16[128,2048]{1,0:T(8,128)(2,1)S(1)}, u32[]{:S(2)}, u32[]{:S(2)}) collective-permute-start(bf16[128,2048]{1,0:T(8,128)(2,1)S(1)} %shard_map.138), channel_id=1, source_target_pairs={{2,4},{3,5},{4,2},{5,3},{10,12},{11,13},{12,10},{13,11},{18,20},{1... | collective-permute-start | bytes 1572872 | tf_op jit(solution)/shard_map/ppermute | solution.py:198
  120.8 16.6 %collective-permute-start.17 = (bf16[128,2048]{1,0:T(8,128)(2,1)S(1)}, bf16[128,2048]{1,0:T(8,128)(2,1)S(1)}, u32[]{:S(2)}, u32[]{:S(2)}) collective-permute-start(bf16[128,2048]{1,0:T(8,128)(2,1)S(1)} %get-tuple-element.148), channel_id=1, source_target_pairs={{0,1},{1,0},{2,3},{3,2},{4,5},{5,4},{6,7},{7,6},{8,9},{9,8},{10,11... | collective-permute-start | bytes 1572872 | tf_op jit(solution)/shard_map/ppermute | solution.py:202
  121.0 20.5 %collective-permute-start.19 = (bf16[128,2048]{1,0:T(8,128)(2,1)S(1)}, bf16[128,2048]{1,0:T(8,128)(2,1)S(1)}, u32[]{:S(2)}, u32[]{:S(2)}) collective-permute-start(bf16[128,2048]{1,0:T(8,128)(2,1)S(1)} %shard_map.133), channel_id=1, source_target_pairs={{0,2},{1,3},{6,4},{7,5},{8,10},{9,11},{14,12},{15,13},{16,18},{17,... | collective-permute-start | bytes 1572872 | tf_op jit(solution)/shard_map/ppermute | solution.py:198
  131.2 10.3 %collective-permute-start.22 = (bf16[128,2048]{1,0:T(8,128)(2,1)S(1)}, bf16[128,2048]{1,0:T(8,128)(2,1)S(1)}, u32[]{:S(2)}, u32[]{:S(2)}) collective-permute-start(bf16[128,2048]{1,0:T(8,128)(2,1)S(1)} %shard_map.135), channel_id=1, source_target_pairs={{2,4},{3,5},{4,2},{5,3},{10,12},{11,13},{12,10},{13,11},{18,20},{1... | collective-permute-start | bytes 1572872 | tf_op jit(solution)/shard_map/ppermute | solution.py:198
  132.1 17.9 %copy-start.4 = (f32[1,128,2048]{2,1,0:T(8,128)S(1)}, f32[1,128,2048]{2,1,0:T(8,128)}, u32[]{:S(2)}) copy-start(f32[1,128,2048]{2,1,0:T(8,128)} %param.14) | copy-start | bytes 3145732
  132.1 17.9 %copy-start.6 = (bf16[1,128,2048]{2,1,0:T(8,128)(2,1)S(1)}, bf16[1,128,2048]{2,1,0:T(8,128)(2,1)}, u32[]{:S(2)}) copy-start(bf16[1,128,2048]{2,1,0:T(8,128)(2,1)} %param.11) | copy-start | bytes 1572868
  132.1 17.9 %collective-permute-start.26 = (bf16[128,2048]{1,0:T(8,128)(2,1)S(1)}, bf16[128,2048]{1,0:T(8,128)(2,1)S(1)}, u32[]{:S(2)}, u32[]{:S(2)}) collective-permute-start(bf16[128,2048]{1,0:T(8,128)(2,1)S(1)} %shard_map.139), channel_id=1, source_target_pairs={{4,6},{5,7},{2,0},{3,1},{12,14},{13,15},{10,8},{11,9},{20,22},{21,... | collective-permute-start | bytes 1572872 | tf_op jit(solution)/shard_map/ppermute | solution.py:198

commit v3 on v2

v3 whole, which is shorter than its diff:
```python
import math

import jax
import jax.numpy as jnp
from jax import lax
from jax.experimental import pallas as pl
from jax.experimental.pallas import tpu as pltpu
from jax.sharding import PartitionSpec as P


gelu_coef = math.sqrt(2.0 / math.pi)
bf16, f32 = jnp.bfloat16, jnp.float32
whole = pl.BlockSpec(memory_space=pltpu.VMEM)
outside = pl.BlockSpec(memory_space=pl.ANY)


def held(array):
    return pltpu.with_memory_space_constraint(array, pltpu.VMEM)


def call(kernel, outs, arrays, aliases=None, limit=8, flops=0, transcendentals=0, written=(), scratch=(), read=()):
    moved = sum(math.prod(a.shape) * a.dtype.itemsize for a in arrays)
    return pl.pallas_call(
        kernel,
        out_shape=[pltpu.VMEM(shape, dtype) for shape, dtype in outs]
        + [jax.ShapeDtypeStruct(shape, dtype) for shape, dtype in written],
        in_specs=[outside] * len(read) + [whole] * len(arrays),
        out_specs=[whole] * len(outs) + [outside] * len(written),
        input_output_aliases=aliases or {},
        scratch_shapes=list(scratch),
        compiler_params=pltpu.CompilerParams(vmem_limit_bytes=limit << 20),
        cost_estimate=pl.CostEstimate(flops=flops, bytes_accessed=moved, transcendentals=transcendentals),
    )(*[pltpu.with_memory_space_constraint(a, pltpu.HBM) for a in read], *[held(a) for a in arrays])


def place_on_line():
    rank = lax.axis_index("dp")
    return rank >> 1, rank & 1


def across(left, right):
    return lax.dot_general(left, right, (((1,), (1,)), ((), ())), preferred_element_type=f32)


def down(left, right):
    return lax.dot_general(left, right, (((0,), (0,)), ((), ())), preferred_element_type=f32)


def normalize(inputs):
    values = inputs.astype(f32)
    center = jnp.mean(values, axis=-1, keepdims=True)
    shifted = values - center
    scaled = lax.rsqrt(jnp.mean(shifted * shifted, axis=-1, keepdims=True) + 1e-05)
    return shifted * scaled, scaled


slabs = 2
chunk_count = 2
halves = 2


def on_turn(turn):
    return pl.when(lax.axis_index("section") == turn)


def rows_of(ref, start, rows):
    return ref[...] if ref.shape[0] == rows else ref[start : start + rows, :]


def block_on(inputs, parts, weights_ref, out_ref, saved, place):
    x_out, normed_out, hidden_out, slope_out = saved
    normed_b = normalize(inputs)[0].astype(bf16)
    x_out[place, :] = inputs
    normed_out[place, :] = normed_b
    total = inputs.astype(f32)
    for part, ready in parts:
        ready(0)
        upper = jnp.dot(normed_b, weights_ref[0, :, part], preferred_element_type=f32)
        square = upper * upper
        bent = jnp.tanh(gelu_coef * upper * (1.0 + 0.044715 * square))
        half = 0.5 + 0.5 * bent
        hidden = (upper * half).astype(bf16)
        hidden_out[place, part] = hidden
        slope_out[place, part] = half + 0.5 * upper * (1.0 - bent * bent) * (
            gelu_coef * (1.0 + 3.0 * 0.044715 * square)
        )
        ready(1)
        total = total + across(hidden, weights_ref[1, :, part])
    out_ref[...] = total.astype(bf16)


def saved_shapes(tokens, width, channels):
    return [((tokens, width), bf16), ((tokens, width), bf16), ((tokens, channels), bf16), ((tokens, channels), f32)]


def enter(token_ids, embed, weights, rows):
    micro, per = token_ids.shape
    vocab, width = embed.shape
    channels = weights.shape[2]
    tokens = micro * per
    step = channels // slabs

    def kernel(ids_hbm, embed_hbm, weights_hbm, out_ref, embedded_ref, weights_ref, *rest):
        saved, (ids_ref, embed_ref, small, large) = rest[:4], rest[4:]
        first = [
            pltpu.make_async_copy(ids_hbm, ids_ref, small.at[0]),
            pltpu.make_async_copy(embed_hbm, embed_ref, small.at[1]),
        ]
        copies = {}
        for i in range(slabs):
            for m in (0, 1):
                part = pl.ds(i * step, step)
                copies[i, m] = pltpu.make_async_copy(
                    weights_hbm.at[m, :, part], weights_ref.at[m, :, part], large.at[2 * i + m]
                )

        @on_turn(0)
        def _():
            for copy in (*first, *copies.values()):
                copy.start()
            for copy in first:
                copy.wait()
            for m in range(micro):
                ids = ids_ref[m : m + 1, :]
                hot = (lax.broadcasted_iota(jnp.int32, (vocab, per), 0) == ids).astype(f32).astype(bf16)
                embedded_ref[m * per : (m + 1) * per, :] = down(hot, embed_ref[...]).astype(bf16)
            parts = [(pl.ds(i * step, step), lambda m, i=i: copies[i, m].wait()) for i in range(slabs)]
            block_on(embedded_ref[0:rows, :], parts, weights_ref, out_ref, saved, pl.ds(0, rows))

    got = call(
        kernel,
        [((rows, width), bf16), ((tokens, width), bf16), (weights.shape, bf16), *saved_shapes(tokens, width, channels)],
        [],
        read=[token_ids, embed, weights],
        flops=4 * rows * width * channels,
        scratch=[
            pltpu.VMEM(token_ids.shape, token_ids.dtype),
            pltpu.VMEM(embed.shape, embed.dtype),
            pltpu.SemaphoreType.DMA((2,)),
            pltpu.SemaphoreType.DMA((2 * slabs,)),
        ],
    )
    return got[0], got[1], got[2], got[3:]


def fetched(weights, held_weights):
    def kernel(weights_hbm, _, weights_ref, done):
        @pl.when(lax.axis_index("section") != 0)
        def _():
            copy = pltpu.make_async_copy(weights_hbm, weights_ref, done)
            copy.start()
            copy.wait()

    return call(
        kernel, [(weights.shape, bf16)], [held_weights], {1: 0}, read=[weights], scratch=[pltpu.SemaphoreType.DMA]
    )[0]


def forward(turn, inputs, weights, saved, start, rows, tokens):
    width = inputs.shape[1]
    channels = weights.shape[2]
    step = channels // slabs

    def kernel(x_ref, w_ref, *refs):
        out_ref, saved_out = refs[-5], refs[-4:]

        @on_turn(turn)
        def _():
            parts = [(pl.ds(i * step, step), lambda m: None) for i in range(slabs)]
            block_on(rows_of(x_ref, start, rows), parts, w_ref, out_ref, saved_out, pl.ds(start, rows))

    got = call(
        kernel,
        [((rows, width), bf16), *saved_shapes(tokens, width, channels)],
        [inputs, weights, *saved],
        {2 + i: 1 + i for i in range(4)},
        flops=4 * rows * width * channels,
        transcendentals=rows * channels,
    )
    return got[0], got[1:]


def backward(turn, grad, weights, saved, kept, start, rows, tokens, last):
    width = grad.shape[1]
    channels = weights.shape[2]
    step = channels // slabs
    outs = [((tokens, width), bf16), ((tokens, channels), bf16)]
    if not last:
        outs = outs + [((rows, width), bf16)]

    def kernel(grad_ref, w_ref, x_ref, slope_ref, *refs):
        refs = refs[len(kept) :]
        grad_out, upper_out = refs[:2]
        here = pl.ds(start, rows)

        @on_turn(turn)
        def _():
            grad = rows_of(grad_ref, start, rows)
            grad_out[here, :] = grad
            total = jnp.zeros((rows, width), f32)
            for i in range(slabs):
                part = pl.ds(i * step, step)
                back_hidden = jnp.dot(grad, w_ref[1, :, part], preferred_element_type=f32)
                back_upper = (back_hidden * slope_ref[here, part]).astype(bf16)
                upper_out[here, part] = back_upper
                if not last:
                    total = total + across(back_upper, w_ref[0, :, part])
            if not last:
                normed, scaled = normalize(x_ref[here, :])
                first = jnp.mean(total, axis=-1, keepdims=True)
                second = jnp.mean(total * normed, axis=-1, keepdims=True)
                refs[2][...] = (grad.astype(f32) + scaled * (total - first - normed * second)).astype(bf16)

    got = call(
        kernel,
        outs,
        [grad, weights, *saved, *kept],
        {4 + i: i for i in range(len(kept))},
        flops=(2 if last else 4) * rows * width * channels,
    )
    return (None if last else got[2]), got[:2]


def cut_up(tokens):
    count = chunk_count if tokens % 16 == 0 else 1
    units = tokens // 16 if count > 1 else 1
    lengths = [(units // count + (1 if c < units % count else 0)) * (tokens // units) for c in range(count)]
    return [(sum(lengths[:c]), lengths[c]) for c in range(count)]


def relay(token_ids, embed, weights, cotangent):
    count = lax.axis_size("section")
    tokens = token_ids.shape[0] * token_ids.shape[1]
    chunks = cut_up(tokens)
    width = embed.shape[1]
    saved, kept = [], []
    entered, embedded, here, saved = enter(token_ids, embed, weights, chunks[0][1])
    weights = fetched(weights, here)
    state = [embedded] * len(chunks)
    grads = [cotangent.reshape(tokens, width)] * len(chunks)

    def passed(array, source, target):
        return lax.ppermute(array, "section", [(source, target)])

    def back(hop, c):
        nonlocal kept
        out, kept = backward(hop, grads[c], weights, [saved[0], saved[3]], kept, *chunks[c], tokens, hop == 0)
        if hop:
            grads[c] = passed(out, hop, hop - 1)

    for hop in range(count):
        for c in range(len(chunks)):
            if hop or c:
                out, saved = forward(hop, state[c], weights, saved, *chunks[c], tokens)
            else:
                out = entered
            if hop + 1 < count:
                state[c] = passed(out, hop, hop + 1)
            else:
                back(hop, c)
    for hop in range(count - 2, -1, -1):
        for c in range(len(chunks)):
            back(hop, c)
    return saved[1], saved[2], kept[0], kept[1], weights


def along(array, pairs):
    return lax.ppermute(array, "dp", [(2 * a + c, 2 * b + c) for a, b in pairs for c in (0, 1)])


def swapped(array):
    return lax.ppermute(array, "dp", [(i, i ^ 1) for i in range(lax.axis_size("dp"))])


def known_rows(error, known, parts, mine):
    owned, channels = parts[0][1].shape[-2:]

    def kernel(error_ref, *refs):
        outs = refs[len(known) + len(parts) :]
        z, core = place_on_line()
        for (by, _, slot), ref in zip(parts, refs[len(known) :]):
            block = 2 * ((z + by) & 3) + (core if mine else 1 - core)
            rows = pl.ds(pl.multiple_of(block * owned, owned), owned)
            values = ref[...] if mine else ref[slot]
            if mine:
                outs[1][slot] = values
            outs[0][block] = 0.9 * values.astype(f32) + error_ref[rows, :].astype(f32)

    return call(
        kernel,
        [((8, owned, channels), f32)] + ([((len(parts), owned, channels), bf16)] if mine else []),
        [error, *known, *[a for _, a, _ in parts]],
        {1: 0} if known else {},
    )


def add_gradient(known, normed, upper, grad, hidden):
    blocks, owned, channels = known.shape
    rows, width = normed.shape
    step = channels // 4
    per = blocks // 2

    def kernel(known_ref, normed_ref, upper_ref, grad_ref, hidden_ref, out_ref, sum_ref):
        total = jnp.zeros((8, step), f32)
        for m, (left, right) in enumerate(((normed_ref, upper_ref), (grad_ref, hidden_ref))):
            turned = left[...].T
            for c in range(channels // step):
                part = pl.ds(c * step, step)
                gradient = jnp.dot(turned, right[:, part], preferred_element_type=f32)
                for b in range(per):
                    block = m * per + b
                    combined = known_ref[block, :, part] + 0.1 * gradient[b * owned : (b + 1) * owned]
                    out_ref[block, :, part] = combined
                    total = total + jnp.sum((combined * combined).reshape(owned // 8, 8, step), axis=0)
        sum_ref[...] = jnp.broadcast_to(jnp.sum(total, axis=(0, 1), keepdims=True), sum_ref.shape)

    return call(
        kernel,
        [(known.shape, f32), ((8, 128), f32)],
        [known, normed, upper, grad, hidden],
        {0: 0},
        limit=12,
        flops=4 * rows * width * channels,
    )


def scale_of(sum_ref, count):
    scale = jnp.sqrt(sum_ref[0:1, 0:1] * (1.0 / count) + 0.01)
    return scale, 1.0 / scale


def chips_in_order(z):
    upper_half = z >> 1
    return (3 - 3 * upper_half, 2 - upper_half, z ^ 1, z)


def packed_part(sums, combined, places):
    blocks, owned, channels = combined.shape
    count = blocks * owned * channels

    def kernel(sum_ref, combined_ref, *outs):
        z, core = place_on_line()
        order = chips_in_order(z)
        scale, inverse = scale_of(sum_ref, count)
        for i, place in enumerate(places):
            for j, side in enumerate((1 - core, core)):
                values = combined_ref[2 * order[place] + side]
                outs[2 * i + j][...] = (scale * jnp.tanh(values * inverse)).astype(bf16)

    return call(
        kernel,
        [((owned, channels), bf16)] * (2 * len(places)),
        [sums, combined],
        transcendentals=2 * len(places) * owned * channels,
    )


def fresh_worker(sums, combined):
    blocks, owned, channels = combined.shape
    count = blocks * owned * channels

    def kernel(sum_ref, combined_ref, out_ref, made, done):
        scale, inverse = scale_of(sum_ref, count)
        copies = []
        for b in range(blocks):
            values = combined_ref[b]
            packed = (scale * jnp.tanh(values * inverse)).astype(bf16)
            made[b] = (values - packed.astype(f32)).astype(bf16)
            copies.append(pltpu.make_async_copy(made.at[b], out_ref.at[pl.ds(b * owned, owned), :], done.at[b]))
            copies[-1].start()
        for copy in copies:
            copy.wait()

    return call(
        kernel,
        [],
        [sums, combined],
        transcendentals=count,
        written=[((blocks * owned, channels), bf16)],
        scratch=[pltpu.VMEM((blocks, owned, channels), bf16), pltpu.SemaphoreType.DMA((blocks,))],
    )[0]


def added(cut, count, *arrays):
    rows, channels = arrays[0].shape[0] // count, arrays[0].shape[1]

    def kernel(*refs):
        total = jnp.zeros((rows, channels), f32)
        for ref in refs[:-1]:
            total = total + rows_of(ref, cut * rows, rows).astype(f32)
        refs[-1][...] = total.astype(bf16)

    return call(kernel, [((rows, channels), bf16)], list(arrays))[0]


def prepared(mine, other, error, variance, replicas):
    def kernel(mine_ref, other_ref, error_ref, variance_ref, base_ref, rate_ref):
        base_ref[...] = (mine_ref[...].astype(f32) + other_ref[...].astype(f32)) * (1.0 / replicas) + error_ref[...]
        rate_ref[...] = 0.01 / (jnp.sqrt(variance_ref[...].astype(f32)) + 1e-08)

    return call(kernel, [(error.shape, f32), (error.shape, f32)], [mine, other, error, variance])


def server(base, rate, parts, weights, replicas):
    owned, channels = base.shape
    per = weights.shape[1] // owned
    cuts = 4 if owned % 64 == 0 else 1
    rows = owned // cuts
    flat = [a for part in parts for a in part]

    def kernel(base_ref, rate_ref, weights_ref, *refs):
        got, outs, (merged_ref, w_made, m_made, e_made, done) = refs[:-8], refs[-8:-5], refs[-5:]
        squares = jnp.zeros((8, channels), f32)
        for i in range(cuts):
            here = pl.ds(i * rows, rows)
            total = jnp.zeros((rows, channels), f32)
            at = 0
            for part in parts:
                high = part[0].shape[0]
                total = total + got[at + i * rows // high][pl.ds(i * rows % high, rows), :].astype(f32)
                at += len(part)
            merged = total * (1.0 / replicas) + base_ref[here, :]
            merged_ref[here, :] = merged
            squares = squares + jnp.sum((merged * merged).reshape(rows // 8, 8, channels), axis=0)
        mean = jnp.sum(squares, axis=(0, 1), keepdims=True) * (1.0 / (owned * channels))
        scale = jnp.sqrt(mean + 0.01)
        inverse = 1.0 / scale
        rank = lax.axis_index("dp")
        matrix = jnp.where(rank >= per, 1, 0)
        first = (rank - per * matrix) * owned
        copies = []
        for i in range(cuts):
            here = pl.ds(i * rows, rows)
            merged = merged_ref[here, :]
            values = (scale * jnp.tanh(merged * inverse)).astype(bf16)
            m_made[here, :] = values
            wide = values.astype(f32)
            e_made[here, :] = merged - wide
            own = weights_ref[matrix, pl.ds(pl.multiple_of(first + i * rows, rows), rows), :].astype(f32)
            w_made[here, :] = (own - wide * rate_ref[here, :]).astype(bf16)
            for j, made in enumerate((w_made, m_made, e_made)):
                copies.append(pltpu.make_async_copy(made.at[here, :], outs[j].at[here, :], done.at[3 * i + j]))
                copies[-1].start()
        for copy in copies:
            copy.wait()

    shape = (owned, channels)
    return call(
        kernel,
        [],
        [base, rate, weights, *flat],
        transcendentals=owned * channels,
        written=[(shape, bf16), (shape, bf16), (shape, f32)],
        scratch=[
            pltpu.VMEM(shape, f32),
            pltpu.VMEM(shape, bf16),
            pltpu.VMEM(shape, bf16),
            pltpu.VMEM(shape, f32),
            pltpu.SemaphoreType.DMA((3 * cuts,)),
        ],
    )


def turned_round(own, up, down):
    def kernel(own_ref, up_ref, lowerref, out_ref):
        z, _ = place_on_line()
        for ref, here in ((own_ref, jnp.logical_or(z == 0, z == 3)), (up_ref, z == 2), (lowerref, z == 1)):

            @pl.when(here)
            def _(ref=ref):
                out_ref[...] = ref[...]

    return call(kernel, [(own.shape, own.dtype)], [own, up, down])[0]


def on_a_line(token_ids, embed, weights, variance, momentum, error, server_error, cotangent):
    replicas = lax.axis_size("dp")
    up = along(momentum, [(i, (i + 1) % 4) for i in range(4)])
    lower = along(momentum, [(i, (i + 3) % 4) for i in range(4)])
    onward = turned_round(momentum, up, lower)
    onward = along(onward, [(0, 2), (2, 3), (3, 1), (1, 0)])
    known, out_a = known_rows(error, [], [(0, momentum, 0), (3, up, 1), (1, lower, 2)], True)
    in_a = swapped(out_a)
    known, out_b = known_rows(error, [known], [(2, onward, 0)], True)
    in_b = swapped(out_b)
    known = known_rows(error, [known], [(0, in_a, 0), (3, in_a, 1), (1, in_a, 2), (2, in_b, 0)], False)[0]
    normed, hidden, grad, upper, weights = relay(token_ids, embed, weights, cotangent)
    combined, sums = add_gradient(known, normed, upper, grad, hidden)
    names = ("far", "mid", "near", "own")
    made = packed_part(sums, combined, (0,)) + packed_part(sums, combined, (1, 2, 3))
    mine, other = {}, {}
    for i, name in enumerate(names):
        mine[name] = made[2 * i + 1]
        other[name] = swapped(made[2 * i])

    def summed(name, pairs, cut, count, *more):
        total = added(cut, count, mine[name], other[name], *more)
        return along(total, pairs)

    ends, inner, outer = [(0, 1), (3, 2)], [(1, 2), (2, 1)], [(2, 3), (1, 0)]
    both = range(halves)
    a1 = [summed("far", ends, h, halves) for h in both]
    a2 = [summed("mid", ends, h, halves) for h in both]
    a3 = [summed("near", ends, 0, 1)]
    b2 = [summed("far", inner, h, halves, a1[h]) for h in both]
    b3 = [summed("mid", inner, h, halves, a2[h]) for h in both]
    c3 = [summed("near", outer, h, halves, b2[h]) for h in both]
    new_worker = fresh_worker(sums, combined)
    base, rate = prepared(mine["own"], other["own"], server_error, variance, replicas)
    new_weights, new_momentum, new_server = server(base, rate, [a3, b3, c3], weights, replicas)
    return new_weights, new_momentum, new_worker, new_server


def in_general(token_ids, embed, weights, variance, momentum, error, server_error, cotangent):
    replicas = lax.axis_size("dp")
    width, channels = weights.shape[1:]
    owned = 2 * width // replicas
    shared = lax.all_gather(momentum, "dp", axis=0, tiled=True)
    normed, hidden, grad, upper, weights = relay(token_ids, embed, weights, cotangent)
    gradient = jnp.concatenate(
        [down(normed, upper), down(grad, hidden)], axis=0
    )
    combined = 0.9 * shared.astype(f32) + 0.1 * gradient + error.astype(f32)
    worker_scale = jnp.sqrt(jnp.mean(combined * combined) + 0.01)
    packed = (worker_scale * jnp.tanh(combined / worker_scale)).astype(bf16)
    new_worker = (combined - packed.astype(f32)).astype(bf16)
    total = lax.psum_scatter(packed.astype(f32), "dp", scatter_dimension=0, tiled=True)
    merged = total / replicas + server_error
    server_scale = jnp.sqrt(jnp.mean(merged * merged) + 0.01)
    values = (server_scale * jnp.tanh(merged / server_scale)).astype(bf16)
    wide = values.astype(f32)
    start = lax.axis_index("dp") * owned
    own = lax.dynamic_slice_in_dim(weights.reshape(2 * width, channels), start, owned, 0)
    step = 0.01 * wide / (jnp.sqrt(variance.astype(f32)) + 1e-08)
    return (own.astype(f32) - step).astype(bf16), values, new_worker, merged - wide


def local(token_ids, embed, weights, variance, momentum, worker_error, server_error, cotangent):
    _, _, width, channels = weights.shape
    plan = on_a_line if lax.axis_size("dp") == 8 else in_general
    new_weights, values, new_worker, new_server = plan(
        token_ids,
        embed,
        weights[0],
        variance[0],
        momentum[0],
        worker_error.reshape(2 * width, channels),
        server_error[0],
        cotangent,
    )
    return new_weights[None], values[None], new_worker.reshape(worker_error.shape), new_server[None]


def solution(mesh):
    in_specs = (
        P(None, "dp"),
        P(),
        P("section", None, None, None),
        P("section", "dp", None),
        P("section", "dp", None),
        P("section", "dp", None, None, None),
        P("section", "dp", None),
        P(None, "dp", None),
    )
    out_specs = (
        P("section", "dp", None),
        P("section", "dp", None),
        P("section", "dp", None, None, None),
        P("section", "dp", None),
    )
    return jax.shard_map(local, mesh=mesh, in_specs=in_specs, out_specs=out_specs, check_vma=False)
```

time: 153 us -> 144 us (0.941)
  waiting for transfers between devices: 63.2 us -> 81.4 us
  Pallas kernels: 36.6 us -> 21.7 us
  starting transfers between devices: 46.4 us -> 35 us
    pallas_call x31 -> x38, Pallas kernels: 36.6 us -> 21.7 us  [call(): pl.pallas_call(kernel, out_shape=[pltpu.VMEM(shape, dtype) for shape, dty...]
    ppermute x12, waiting for transfers between devices: 18 us -> 28.1 us  [passed(): return lax.ppermute(array, 'section', [(source, target)])]
    ppermute x9 -> x14, starting transfers between devices: 32 us -> 23.6 us  [along(): lax.ppermute(array, 'dp', [(2 * a + c, 2 * b + c) for a, b in pairs for c...]
    ppermute x9 -> x14, waiting for transfers between devices: 45 us -> 53.1 us  [along(): lax.ppermute(array, 'dp', [(2 * a + c, 2 * b + c) for a, b in pairs for c...]
    ppermute x12, starting transfers between devices: 13 us -> 10.5 us  [passed(): return lax.ppermute(array, 'section', [(source, target)])]
    unnamed x18 -> x12, local copies, waits for them, and re-layouts: 5.04 us -> 3.57 us
  transfers between devices with their start and end apart: 27 -> 32, of which waited for: 9 -> 14; matrix products, arithmetic and copies ran while one was open for 0% -> 0% of each run, Pallas kernels for 20% -> 11%
where the time goes in v3:
time: 144 us; the launch traced here: 143 us
  waiting for transfers between devices  81.4 us (57%)
  starting transfers between devices  35 us (24%)
  Pallas kernels  21.7 us (15%)
  local copies, waits for them, and re-layouts  3.57 us (2%)
    ppermute x14, waiting for transfers between devices, along(): lax.ppermute(array, 'dp', [(2 * a + c, 2 * b + c) for a, b in pairs for c...  53.1 us
    ppermute x12, waiting for transfers between devices, passed(): return lax.ppermute(array, 'section', [(source, target)])  28.1 us
    ppermute x14, starting transfers between devices, along(): lax.ppermute(array, 'dp', [(2 * a + c, 2 * b + c) for a, b in pairs for c...  23.6 us
    pallas_call x38, Pallas kernels, call(): pl.pallas_call(kernel, out_shape=[pltpu.VMEM(shape, dtype) for shape, dty...  21.7 us
    ppermute x12, starting transfers between devices, passed(): return lax.ppermute(array, 'section', [(source, target)])  10.5 us
    unnamed x12, local copies, waits for them, and re-layouts  3.57 us
  transfers between devices with their start and end apart: 32, of which 14 were waited for; matrix products, arithmetic and copies ran while one was open for 0% of the time, Pallas kernels for 11%

profile of v3, /device:TPU:0, one launch (start us, length us, event | category | flops | bytes accessed | tf_op | source)
XLA Modules:
  0.0 143.1 jit_solution(14811440475473346133)
XLA Ops:
  0.6 3.1 %collective-permute-start = (bf16[128,2048]{1,0:T(8,128)(2,1)}, bf16[128,2048]{1,0:T(8,128)(2,1)S(1)}, u32[]{:S(2)}, u32[]{:S(2)}) collective-permute-start(bf16[128,2048]{1,0:T(8,128)(2,1)} %bitcast.13), channel_id=1, source_target_pairs={{0,2},{1,3},{2,4},{3,5},{4,6},{5,7},{6,0},{7,1},{8,10},{9,11},{10,... | collective-permute-start | bytes 1572872 | tf_op jit(solution)/shard_map/ppermute | solution.py:268
  3.7 2.1 %collective-permute-start.1 = (bf16[128,2048]{1,0:T(8,128)(2,1)}, bf16[128,2048]{1,0:T(8,128)(2,1)S(1)}, u32[]{:S(2)}, u32[]{:S(2)}) collective-permute-start(bf16[128,2048]{1,0:T(8,128)(2,1)} %bitcast.14), channel_id=1, source_target_pairs={{0,6},{1,7},{2,0},{3,1},{4,2},{5,3},{6,4},{7,5},{8,14},{9,15},{10,... | collective-permute-start | bytes 1572872 | tf_op jit(solution)/shard_map/ppermute | solution.py:268
  5.8 13.0 %collective-permute-done.refs_1_.up_ref = bf16[128,2048]{1,0:T(8,128)(2,1)S(1)} collective-permute-done((bf16[128,2048]{1,0:T(8,128)(2,1)}, bf16[128,2048]{1,0:T(8,128)(2,1)S(1)}, u32[]{:S(2)}, u32[]{:S(2)}) %collective-permute-start) | collective-permute-done | bytes 524320 | tf_op jit(solution)/shard_map/ppermute | solution.py:268
  18.8 9.8 %collective-permute-done.1.refs_2_.lowerref = bf16[128,2048]{1,0:T(8,128)(2,1)S(1)} collective-permute-done((bf16[128,2048]{1,0:T(8,128)(2,1)}, bf16[128,2048]{1,0:T(8,128)(2,1)S(1)}, u32[]{:S(2)}, u32[]{:S(2)}) %collective-permute-start.1) | collective-permute-done | bytes 524320 | tf_op jit(solution)/shard_map/ppermute | solution.py:268
  28.6 2.2 %copy-done = bf16[1,1,2,512,2048]{4,3,2,1,0:T(8,128)(2,1)S(1)} copy-done((bf16[1,1,2,512,2048]{4,3,2,1,0:T(8,128)(2,1)S(1)}, bf16[1,1,2,512,2048]{4,3,2,1,0:T(8,128)(2,1)}, u32[]{:S(2)}) %copy-start) | copy-done | bytes 4194328
  30.8 1.0 copy-done.2
  31.8 0.5 shard_map.111
  32.4 4.2 %shard_map.115 = (bf16[128,512]{1,0:T(8,128)(2,1)S(1)}, bf16[256,512]{1,0:T(8,128)(2,1)S(1)}, bf16[2,512,2048]{2,1,0:T(8,128)(2,1)S(1)}, bf16[256,512]{1,0:T(8,1...) custom-call(s32[4,64]{1,0:T(4,128)} %ids_hbm.1, ...), custom_call_target="tpu_custom_call" | custom-call | flops 536870912 | tf_op jit(solution)/shard_map/pallas_call | solution.py:23
  36.7 1.3 collective-permute-start.6
  38.0 1.7 %shard_map.117 = (bf16[128,512]{1,0:T(8,128)(2,1)S(1)}, bf16[256,512]{1,0:T(8,128)(2,1)S(1)}, bf16[256,512]{1,0:T(8,128)(2,1)S(1)}, bf16[256,2048]{1,0:T(8,128)(2,1)S(1)}, f32[256,2048]{1,0:T(8,128)S(1)}) custom-call(bf16[256,512]{1,0:T(8,128)(2,1)S(1)} %get-tuple-element.89.x_ref, ...), custom_call_target="tpu_custom_call", output_to_operand_aliasing={{1}: (2, {}), {2}: (3, {}), {3}: (4, {}), {4}: (5, {})} | custom-call | flops 536870912 | bytes 8126464 | tf_op jit(solution)/shard_map/pallas_call | solution.py:23
  39.7 1.3 collective-permute-start.5
  41.1 1.4 collective-permute-start.2
  42.5 0.7 collective-permute-start.8
  43.1 1.6 %collective-permute-done.5.x_ref = bf16[128,512]{1,0:T(8,128)(2,1)S(1)} collective-permute-done((bf16[128,512]{1,0:T(8,128)(2,1)S(1)}, bf16[128,512]{1,0:T(8,128)(2,1)S(1)}, u32[]{:S(2)}, u32[]{:S(2)}) %collective-permute-start.5) | collective-permute-done | bytes 131104 | tf_op jit(solution)/shard_map/ppermute | solution.py:243
  44.7 0.7 collective-permute-start.7
  45.4 0.7 collective-permute-start.10
  46.1 0.7 collective-permute-start.9
  46.8 0.7 shard_map.122
  47.5 0.3 copy-done.4
  47.8 0.7 collective-permute-start.12
  48.5 0.7 shard_map.123
  49.2 6.3 %collective-permute-done.2.refs_1_ = bf16[128,2048]{1,0:T(8,128)(2,1)S(1)} collective-permute-done((bf16[128,2048]{1,0:T(8,128)(2,1)S(1)}, bf16[128,2048]{1,0:T(8,128)(2,1)S(1)}, u32[]{:S(2)}, u32[]{:S(2)}) %collective-permute-start.2) | collective-permute-done | bytes 524320 | tf_op jit(solution)/shard_map/ppermute | solution.py:268
  55.5 0.2 shard_map.113
  55.8 0.7 collective-permute-start.11
  56.5 0.7 collective-permute-start.14
  57.2 0.7 collective-permute-start.13
  57.9 1.3 collective-permute-start.16
  59.2 1.3 collective-permute-start.15
  60.5 19.9 %collective-permute-done.16.grad_ref = bf16[128,512]{1,0:T(8,128)(2,1)S(1)} collective-permute-done((bf16[128,512]{1,0:T(8,128)(2,1)S(1)}, bf16[128,512]{1,0:T(8,128)(2,1)S(1)}, u32[]{:S(2)}, u32[]{:S(2)}) %collective-permute-start.16) | collective-permute-done | bytes 131104 | tf_op jit(solution)/shard_map/ppermute | solution.py:243
  80.4 0.4 shard_map.130
  80.9 6.7 %collective-permute-done.15.grad_ref = bf16[128,512]{1,0:T(8,128)(2,1)S(1)} collective-permute-done((bf16[128,512]{1,0:T(8,128)(2,1)S(1)}, bf16[128,512]{1,0:T(8,128)(2,1)S(1)}, u32[]{:S(2)}, u32[]{:S(2)}) %collective-permute-start.15) | collective-permute-done | bytes 131104 | tf_op jit(solution)/shard_map/ppermute | solution.py:243
  87.5 0.7 shard_map.131
  88.2 0.6 shard_map.114.known_ref
  88.9 2.8 %shard_map.132 = (f32[8,128,2048]{2,1,0:T(8,128)S(1)}, f32[8,128]{1,0:T(8,128)S(1)}) custom-call(f32[8,128,2048]{2,1,0:T(8,128)S(1)} %shard_map.114.known_ref, bf16[256,512]{1,0:T(8,128)(2,1)S(1)} %get-tuple-element.125.normed_ref, bf16[256,2048]{1,0:T(8,128)(2,1)S(1)} %get-tuple-element.148.upper_ref, ...), custom_call_target="tpu_custom_call", output_to_operand_aliasing={{0}: (0, {})} | custom-call | flops 1073741824 | bytes 11010048 | tf_op jit(solution)/shard_map/pallas_call | solution.py:23
  91.7 0.4 shard_map.140
  92.2 1.1 shard_map.133
  93.3 0.6 collective-permute-start.20
  93.9 0.1 collective-permute-done.25.refs_1_
  94.1 3.0 %collective-permute-start.26 = (bf16[64,2048]{1,0:T(8,128)(2,1)S(1)}, bf16[64,2048]{1,0:T(8,128)(2,1)S(1)}, u32[]{:S(2)}, u32[]{:S(2)}) collective-permute-start(bf16[64,2048]{1,0:T(8,128)(2,1)S(1)} %shard_map.141), channel_id=1, source_target_pairs={{0,2},{1,3},{6,4},{7,5},{8,10},{9,11},{14,12},{15,13},{16,18},{17,... | collective-permute-start | bytes 786440 | tf_op jit(solution)/shard_map/ppermute | solution.py:268
  97.3 1.3 collective-permute-start.29
  98.6 1.3 collective-permute-start.21
  100.1 1.5 %collective-permute-start.23 = (bf16[64,2048]{1,0:T(8,128)(2,1)S(1)}, bf16[64,2048]{1,0:T(8,128)(2,1)S(1)}, u32[]{:S(2)}, u32[]{:S(2)}) collective-permute-start(bf16[64,2048]{1,0:T(8,128)(2,1)S(1)} %shard_map.138), channel_id=1, source_target_pairs={{0,2},{1,3},{6,4},{7,5},{8,10},{9,11},{14,12},{15,13},{16,18},{17,... | collective-permute-start | bytes 786440 | tf_op jit(solution)/shard_map/ppermute | solution.py:268
  101.7 0.1 shard_map.135
  101.8 2.0 %collective-permute-done.26.refs_2_ = bf16[64,2048]{1,0:T(8,128)(2,1)S(1)} collective-permute-done((bf16[64,2048]{1,0:T(8,128)(2,1)S(1)}, bf16[64,2048]{1,0:T(8,128)(2,1)S(1)}, u32[]{:S(2)}, u32[]{:S(2)}) %collective-permute-start.26) | collective-permute-done | bytes 262176 | tf_op jit(solution)/shard_map/ppermute | solution.py:268
  103.9 0.7 collective-permute-start.27
  104.6 4.8 %collective-permute-done.29.refs_2_ = bf16[64,2048]{1,0:T(8,128)(2,1)S(1)} collective-permute-done((bf16[64,2048]{1,0:T(8,128)(2,1)S(1)}, bf16[64,2048]{1,0:T(8,128)(2,1)S(1)}, u32[]{:S(2)}, u32[]{:S(2)}) %collective-permute-start.29) | collective-permute-done | bytes 262176 | tf_op jit(solution)/shard_map/ppermute | solution.py:268
  109.6 0.7 collective-permute-start.30
  110.2 4.8 %collective-permute-done.21.refs_2_ = bf16[64,2048]{1,0:T(8,128)(2,1)S(1)} collective-permute-done((bf16[64,2048]{1,0:T(8,128)(2,1)S(1)}, bf16[64,2048]{1,0:T(8,128)(2,1)S(1)}, u32[]{:S(2)}, u32[]{:S(2)}) %collective-permute-start.21) | collective-permute-done | bytes 262176 | tf_op jit(solution)/shard_map/ppermute | solution.py:268
  115.1 4.4 %collective-permute-start.19 = (bf16[128,2048]{1,0:T(8,128)(2,1)S(1)}, bf16[128,2048]{1,0:T(8,128)(2,1)S(1)}, u32[]{:S(2)}, u32[]{:S(2)}) collective-permute-start(bf16[128,2048]{1,0:T(8,128)(2,1)S(1)} %shard_map.135), channel_id=1, source_target_pairs={{0,2},{1,3},{6,4},{7,5},{8,10},{9,11},{14,12},{15,13},{16,18},{17,... | collective-permute-start | bytes 1572872 | tf_op jit(solution)/shard_map/ppermute | solution.py:268
  119.5 0.1 shard_map.137
  119.6 1.1 collective-permute-done.23.refs_2_
  120.7 0.7 collective-permute-start.22
  121.4 0.1 shard_map.139
  121.5 0.7 collective-permute-start.24
  122.2 0.1 shard_map.143
  122.3 1.3 collective-permute-start.28
  123.6 0.1 shard_map.146
  123.7 1.4 collective-permute-start.31
  125.2 3.8 %shard_map.148 = bf16[1024,2048]{1,0:T(8,128)(2,1)} custom-call(f32[8,128]{1,0:T(8,128)S(1)} %get-tuple-element.151.sum_ref, f32[8,128,2048]{2,1,0:T(8,128)S(1)} %get-tuple-element.152.combined_ref), custom_call_target="tpu_custom_call" | custom-call | bytes 8392704 | tf_op jit(solution)/shard_map/pallas_call | solution.py:23
  129.0 0.6 shard_map.134
  129.6 1.6 %collective-permute-done.19.refs_0_ = bf16[128,2048]{1,0:T(8,128)(2,1)S(1)} collective-permute-done((bf16[128,2048]{1,0:T(8,128)(2,1)S(1)}, bf16[128,2048]{1,0:T(8,128)(2,1)S(1)}, u32[]{:S(2)}, u32[]{:S(2)}) %collective-permute-start.19) | collective-permute-done | bytes 524320 | tf_op jit(solution)/shard_map/ppermute | solution.py:268
  131.3 6.4 %collective-permute-done.28.refs_3_ = bf16[64,2048]{1,0:T(8,128)(2,1)S(1)} collective-permute-done((bf16[64,2048]{1,0:T(8,128)(2,1)S(1)}, bf16[64,2048]{1,0:T(8,128)(2,1)S(1)}, u32[]{:S(2)}, u32[]{:S(2)}) %collective-permute-start.28) | collective-permute-done | bytes 262176 | tf_op jit(solution)/shard_map/ppermute | solution.py:268
  137.7 3.1 %collective-permute-done.31.refs_4_ = bf16[64,2048]{1,0:T(8,128)(2,1)S(1)} collective-permute-done((bf16[64,2048]{1,0:T(8,128)(2,1)S(1)}, bf16[64,2048]{1,0:T(8,128)(2,1)S(1)}, u32[]{:S(2)}, u32[]{:S(2)}) %collective-permute-start.31) | collective-permute-done | bytes 262176 | tf_op jit(solution)/shard_map/ppermute | solution.py:268
  140.8 2.1 %shard_map.147 = (bf16[128,2048]{1,0:T(8,128)(2,1)}, bf16[128,2048]{1,0:T(8,128)(2,1)}, f32[128,2048]{1,0:T(8,128)}) custom-call(f32[128,2048]{1,0:T(8,128)S(1)} %get-tuple-element.155.base_ref, f32[128,2048]{1,0:T(8,128)S(1)} %get-tuple-element.156.rate_ref, bf16[2,512,2048]{2,1,0:T(8,128)(2,1)S(1)} %shard_map.116.w_ref.weights_ref, ...), custom_call_target="tpu_custom_call" | custom-call | bytes 7864320 | tf_op jit(solution)/shard_map/pallas_call | solution.py:23
  (50 shorter events, 1.1 us)
Async XLA Ops:
  0.6 18.2 %collective-permute-start = (bf16[128,2048]{1,0:T(8,128)(2,1)}, bf16[128,2048]{1,0:T(8,128)(2,1)S(1)}, u32[]{:S(2)}, u32[]{:S(2)}) collective-permute-start(bf16[128,2048]{1,0:T(8,128)(2,1)} %bitcast.13), channel_id=1, source_target_pairs={{0,2},{1,3},{2,4},{3,5},{4,6},{5,7},{6,0},{7,1},{8,10},{9,11},{10,... | collective-permute-start | bytes 1572872 | tf_op jit(solution)/shard_map/ppermute | solution.py:268
  3.7 24.8 %collective-permute-start.1 = (bf16[128,2048]{1,0:T(8,128)(2,1)}, bf16[128,2048]{1,0:T(8,128)(2,1)S(1)}, u32[]{:S(2)}, u32[]{:S(2)}) collective-permute-start(bf16[128,2048]{1,0:T(8,128)(2,1)} %bitcast.14), channel_id=1, source_target_pairs={{0,6},{1,7},{2,0},{3,1},{4,2},{5,3},{6,4},{7,5},{8,14},{9,15},{10,... | collective-permute-start | bytes 1572872 | tf_op jit(solution)/shard_map/ppermute | solution.py:268
  28.6 2.2 %copy-start = (bf16[1,1,2,512,2048]{4,3,2,1,0:T(8,128)(2,1)S(1)}, bf16[1,1,2,512,2048]{4,3,2,1,0:T(8,128)(2,1)}, u32[]{:S(2)}) copy-start(bf16[1,1,2,512,2048]{4,3,2,1,0:T(8,128)(2,1)} %param.13) | copy-start | bytes 12582916
  30.8 1.0 copy-start.2
  32.3 55.9 %collective-permute-start.3 = (bf16[3,128,2048]{2,1,0:T(8,128)(2,1)S(1)}, bf16[3,128,2048]{2,1,0:T(8,128)(2,1)S(1)}, u32[]{:S(2)}, u32[]{:S(2)}) collective-permute-start(bf16[3,128,2048]{2,1,0:T(8,128)(2,1)S(1)} %get-tuple-element.87), channel_id=1, source_target_pairs={{0,1},{1,0},{2,3},{3,2},{4,5},{5,4},{6,7},{7,6},{8,9},{9,8},{10,11... | collective-permute-start | bytes 4718600 | tf_op jit(solution)/shard_map/ppermute | solution.py:272
  36.7 5.8 %collective-permute-start.6 = (bf16[128,512]{1,0:T(8,128)(2,1)S(1)}, bf16[128,512]{1,0:T(8,128)(2,1)S(1)}, u32[]{:S(2)}, u32[]{:S(2)}) collective-permute-start(bf16[128,512]{1,0:T(8,128)(2,1)S(1)} %get-tuple-element.96), channel_id=1, source_target_pairs={{0,8},{1,9},{2,10},{3,11},{4,12},{5,13},{6,14},{7,15}} | collective-permute-start | bytes 393224 | tf_op jit(solution)/shard_map/ppermute | solution.py:243
  39.7 5.0 %collective-permute-start.5 = (bf16[128,512]{1,0:T(8,128)(2,1)S(1)}, bf16[128,512]{1,0:T(8,128)(2,1)S(1)}, u32[]{:S(2)}, u32[]{:S(2)}) collective-permute-start(bf16[128,512]{1,0:T(8,128)(2,1)S(1)} %get-tuple-element.95), channel_id=1, source_target_pairs={{0,8},{1,9},{2,10},{3,11},{4,12},{5,13},{6,14},{7,15}} | collective-permute-start | bytes 393224 | tf_op jit(solution)/shard_map/ppermute | solution.py:243
  41.1 14.4 %collective-permute-start.2 = (bf16[128,2048]{1,0:T(8,128)(2,1)S(1)}, bf16[128,2048]{1,0:T(8,128)(2,1)S(1)}, u32[]{:S(2)}, u32[]{:S(2)}) collective-permute-start(bf16[128,2048]{1,0:T(8,128)(2,1)S(1)} %shard_map.112), channel_id=1, source_target_pairs={{0,4},{1,5},{4,6},{5,7},{6,2},{7,3},{2,0},{3,1},{8,12},{9,13},{12,... | collective-permute-start | bytes 1572872 | tf_op jit(solution)/shard_map/ppermute | solution.py:268
  42.5 2.9 %collective-permute-start.8 = (bf16[128,512]{1,0:T(8,128)(2,1)S(1)}, bf16[128,512]{1,0:T(8,128)(2,1)S(1)}, u32[]{:S(2)}, u32[]{:S(2)}) collective-permute-start(bf16[128,512]{1,0:T(8,128)(2,1)S(1)} %get-tuple-element.106), channel_id=1, source_target_pairs={{8,16},{9,17},{10,18},{11,19},{12,20},{13,21},{14,22},{15,23}} | collective-permute-start | bytes 393224 | tf_op jit(solution)/shard_map/ppermute | solution.py:243
  44.7 1.4 collective-permute-start.7
  45.4 1.4 collective-permute-start.10
  46.1 2.4 %collective-permute-start.9 = (bf16[128,512]{1,0:T(8,128)(2,1)S(1)}, bf16[128,512]{1,0:T(8,128)(2,1)S(1)}, u32[]{:S(2)}, u32[]{:S(2)}) collective-permute-start(bf16[128,512]{1,0:T(8,128)(2,1)S(1)} %get-tuple-element.115), channel_id=1, source_target_pairs={{16,24},{17,25},{18,26},{19,27},{20,28},{21,29},{22,30},{23,31}} | collective-permute-start | bytes 393224 | tf_op jit(solution)/shard_map/ppermute | solution.py:243
  46.8 1.0 copy-start.4
  47.8 8.6 %collective-permute-start.12 = (bf16[128,512]{1,0:T(8,128)(2,1)S(1)}, bf16[128,512]{1,0:T(8,128)(2,1)S(1)}, u32[]{:S(2)}, u32[]{:S(2)}) collective-permute-start(bf16[128,512]{1,0:T(8,128)(2,1)S(1)} %get-tuple-element.131), channel_id=1, source_target_pairs={{24,16},{25,17},{26,18},{27,19},{28,20},{29,21},{30,22},{31,23}} | collective-permute-start | bytes 393224 | tf_op jit(solution)/shard_map/ppermute | solution.py:243
  48.5 7.0 %copy-start.1 = (bf16[1,1,2,512,2048]{4,3,2,1,0:T(8,128)(2,1)S(1)}, bf16[1,1,2,512,2048]{4,3,2,1,0:T(8,128)(2,1)}, u32[]{:S(2)}) copy-start(bf16[1,1,2,512,2048]{4,3,2,1,0:T(8,128)(2,1)} %param.13) | copy-start | bytes 12582916
  55.7 32.6 %collective-permute-start.4 = (bf16[1,128,2048]{2,1,0:T(8,128)(2,1)S(1)}, bf16[1,128,2048]{2,1,0:T(8,128)(2,1)S(1)}, u32[]{:S(2)}, u32[]{:S(2)}) collective-permute-start(bf16[1,128,2048]{2,1,0:T(8,128)(2,1)S(1)} %get-tuple-element.88), channel_id=1, source_target_pairs={{0,1},{1,0},{2,3},{3,2},{4,5},{5,4},{6,7},{7,6},{8,9},{9,8},{10,11... | collective-permute-start | bytes 1572872 | tf_op jit(solution)/shard_map/ppermute | solution.py:272
  55.8 1.4 collective-permute-start.11
  56.5 1.4 collective-permute-start.14
  57.2 2.0 %collective-permute-start.13 = (bf16[128,512]{1,0:T(8,128)(2,1)S(1)}, bf16[128,512]{1,0:T(8,128)(2,1)S(1)}, u32[]{:S(2)}, u32[]{:S(2)}) collective-permute-start(bf16[128,512]{1,0:T(8,128)(2,1)S(1)} %get-tuple-element.136), channel_id=1, source_target_pairs={{16,8},{17,9},{18,10},{19,11},{20,12},{21,13},{22,14},{23,15}} | collective-permute-start | bytes 393224 | tf_op jit(solution)/shard_map/ppermute | solution.py:243
  57.9 22.5 %collective-permute-start.16 = (bf16[128,512]{1,0:T(8,128)(2,1)S(1)}, bf16[128,512]{1,0:T(8,128)(2,1)S(1)}, u32[]{:S(2)}, u32[]{:S(2)}) collective-permute-start(bf16[128,512]{1,0:T(8,128)(2,1)S(1)} %get-tuple-element.143), channel_id=1, source_target_pairs={{8,0},{9,1},{10,2},{11,3},{12,4},{13,5},{14,6},{15,7}} | collective-permute-start | bytes 393224 | tf_op jit(solution)/shard_map/ppermute | solution.py:243
  59.2 28.3 %collective-permute-start.15 = (bf16[128,512]{1,0:T(8,128)(2,1)S(1)}, bf16[128,512]{1,0:T(8,128)(2,1)S(1)}, u32[]{:S(2)}, u32[]{:S(2)}) collective-permute-start(bf16[128,512]{1,0:T(8,128)(2,1)S(1)} %get-tuple-element.142), channel_id=1, source_target_pairs={{8,0},{9,1},{10,2},{11,3},{12,4},{13,5},{14,6},{15,7}} | collective-permute-start | bytes 393224 | tf_op jit(solution)/shard_map/ppermute | solution.py:243
  92.1 2.0 %collective-permute-start.25 = (bf16[128,2048]{1,0:T(8,128)(2,1)S(1)}, bf16[128,2048]{1,0:T(8,128)(2,1)S(1)}, u32[]{:S(2)}, u32[]{:S(2)}) collective-permute-start(bf16[128,2048]{1,0:T(8,128)(2,1)S(1)} %get-tuple-element.162), channel_id=1, source_target_pairs={{0,1},{1,0},{2,3},{3,2},{4,5},{5,4},{6,7},{7,6},{8,9},{9,8},{10,11... | collective-permute-start | bytes 1572872 | tf_op jit(solution)/shard_map/ppermute | solution.py:272
  93.3 5.3 %collective-permute-start.20 = (bf16[128,2048]{1,0:T(8,128)(2,1)S(1)}, bf16[128,2048]{1,0:T(8,128)(2,1)S(1)}, u32[]{:S(2)}, u32[]{:S(2)}) collective-permute-start(bf16[128,2048]{1,0:T(8,128)(2,1)S(1)} %get-tuple-element.160), channel_id=1, source_target_pairs={{0,1},{1,0},{2,3},{3,2},{4,5},{5,4},{6,7},{7,6},{8,9},{9,8},{10,11... | collective-permute-start | bytes 1572872 | tf_op jit(solution)/shard_map/ppermute | solution.py:272
  93.8 6.3 %collective-permute-start.18 = (bf16[128,2048]{1,0:T(8,128)(2,1)S(1)}, bf16[128,2048]{1,0:T(8,128)(2,1)S(1)}, u32[]{:S(2)}, u32[]{:S(2)}) collective-permute-start(bf16[128,2048]{1,0:T(8,128)(2,1)S(1)} %get-tuple-element.158), channel_id=1, source_target_pairs={{0,1},{1,0},{2,3},{3,2},{4,5},{5,4},{6,7},{7,6},{8,9},{9,8},{10,11... | collective-permute-start | bytes 1572872 | tf_op jit(solution)/shard_map/ppermute | solution.py:272
  94.1 9.7 %collective-permute-start.26 = (bf16[64,2048]{1,0:T(8,128)(2,1)S(1)}, bf16[64,2048]{1,0:T(8,128)(2,1)S(1)}, u32[]{:S(2)}, u32[]{:S(2)}) collective-permute-start(bf16[64,2048]{1,0:T(8,128)(2,1)S(1)} %shard_map.141), channel_id=1, source_target_pairs={{0,2},{1,3},{6,4},{7,5},{8,10},{9,11},{14,12},{15,13},{16,18},{17,... | collective-permute-start | bytes 786440 | tf_op jit(solution)/shard_map/ppermute | solution.py:268
  97.3 12.2 %collective-permute-start.29 = (bf16[64,2048]{1,0:T(8,128)(2,1)S(1)}, bf16[64,2048]{1,0:T(8,128)(2,1)S(1)}, u32[]{:S(2)}, u32[]{:S(2)}) collective-permute-start(bf16[64,2048]{1,0:T(8,128)(2,1)S(1)} %shard_map.144), channel_id=1, source_target_pairs={{0,2},{1,3},{6,4},{7,5},{8,10},{9,11},{14,12},{15,13},{16,18},{17,... | collective-permute-start | bytes 786440 | tf_op jit(solution)/shard_map/ppermute | solution.py:268
  98.6 16.4 %collective-permute-start.21 = (bf16[64,2048]{1,0:T(8,128)(2,1)S(1)}, bf16[64,2048]{1,0:T(8,128)(2,1)S(1)}, u32[]{:S(2)}, u32[]{:S(2)}) collective-permute-start(bf16[64,2048]{1,0:T(8,128)(2,1)S(1)} %shard_map.136), channel_id=1, source_target_pairs={{0,2},{1,3},{6,4},{7,5},{8,10},{9,11},{14,12},{15,13},{16,18},{17,... | collective-permute-start | bytes 786440 | tf_op jit(solution)/shard_map/ppermute | solution.py:268
  100.0 23.8 %collective-permute-start.17 = (bf16[128,2048]{1,0:T(8,128)(2,1)S(1)}, bf16[128,2048]{1,0:T(8,128)(2,1)S(1)}, u32[]{:S(2)}, u32[]{:S(2)}) collective-permute-start(bf16[128,2048]{1,0:T(8,128)(2,1)S(1)} %get-tuple-element.154), channel_id=1, source_target_pairs={{0,1},{1,0},{2,3},{3,2},{4,5},{5,4},{6,7},{7,6},{8,9},{9,8},{10,11... | collective-permute-start | bytes 1572872 | tf_op jit(solution)/shard_map/ppermute | solution.py:272
  100.1 20.6 %collective-permute-start.23 = (bf16[64,2048]{1,0:T(8,128)(2,1)S(1)}, bf16[64,2048]{1,0:T(8,128)(2,1)S(1)}, u32[]{:S(2)}, u32[]{:S(2)}) collective-permute-start(bf16[64,2048]{1,0:T(8,128)(2,1)S(1)} %shard_map.138), channel_id=1, source_target_pairs={{0,2},{1,3},{6,4},{7,5},{8,10},{9,11},{14,12},{15,13},{16,18},{17,... | collective-permute-start | bytes 786440 | tf_op jit(solution)/shard_map/ppermute | solution.py:268
  103.9 17.5 %collective-permute-start.27 = (bf16[64,2048]{1,0:T(8,128)(2,1)S(1)}, bf16[64,2048]{1,0:T(8,128)(2,1)S(1)}, u32[]{:S(2)}, u32[]{:S(2)}) collective-permute-start(bf16[64,2048]{1,0:T(8,128)(2,1)S(1)} %shard_map.142), channel_id=1, source_target_pairs={{2,4},{3,5},{4,2},{5,3},{10,12},{11,13},{12,10},{13,11},{18,20},{1... | collective-permute-start | bytes 786440 | tf_op jit(solution)/shard_map/ppermute | solution.py:268
  109.6 12.7 %collective-permute-start.30 = (bf16[64,2048]{1,0:T(8,128)(2,1)S(1)}, bf16[64,2048]{1,0:T(8,128)(2,1)S(1)}, u32[]{:S(2)}, u32[]{:S(2)}) collective-permute-start(bf16[64,2048]{1,0:T(8,128)(2,1)S(1)} %shard_map.145), channel_id=1, source_target_pairs={{2,4},{3,5},{4,2},{5,3},{10,12},{11,13},{12,10},{13,11},{18,20},{1... | collective-permute-start | bytes 786440 | tf_op jit(solution)/shard_map/ppermute | solution.py:268
  115.1 16.2 %collective-permute-start.19 = (bf16[128,2048]{1,0:T(8,128)(2,1)S(1)}, bf16[128,2048]{1,0:T(8,128)(2,1)S(1)}, u32[]{:S(2)}, u32[]{:S(2)}) collective-permute-start(bf16[128,2048]{1,0:T(8,128)(2,1)S(1)} %shard_map.135), channel_id=1, source_target_pairs={{0,2},{1,3},{6,4},{7,5},{8,10},{9,11},{14,12},{15,13},{16,18},{17,... | collective-permute-start | bytes 1572872 | tf_op jit(solution)/shard_map/ppermute | solution.py:268
  120.7 8.9 %collective-permute-start.22 = (bf16[64,2048]{1,0:T(8,128)(2,1)S(1)}, bf16[64,2048]{1,0:T(8,128)(2,1)S(1)}, u32[]{:S(2)}, u32[]{:S(2)}) collective-permute-start(bf16[64,2048]{1,0:T(8,128)(2,1)S(1)} %shard_map.137), channel_id=1, source_target_pairs={{2,4},{3,5},{4,2},{5,3},{10,12},{11,13},{12,10},{13,11},{18,20},{1... | collective-permute-start | bytes 786440 | tf_op jit(solution)/shard_map/ppermute | solution.py:268
  121.5 8.1 %collective-permute-start.24 = (bf16[64,2048]{1,0:T(8,128)(2,1)S(1)}, bf16[64,2048]{1,0:T(8,128)(2,1)S(1)}, u32[]{:S(2)}, u32[]{:S(2)}) collective-permute-start(bf16[64,2048]{1,0:T(8,128)(2,1)S(1)} %shard_map.139), channel_id=1, source_target_pairs={{2,4},{3,5},{4,2},{5,3},{10,12},{11,13},{12,10},{13,11},{18,20},{1... | collective-permute-start | bytes 786440 | tf_op jit(solution)/shard_map/ppermute | solution.py:268
  122.3 15.4 %collective-permute-start.28 = (bf16[64,2048]{1,0:T(8,128)(2,1)S(1)}, bf16[64,2048]{1,0:T(8,128)(2,1)S(1)}, u32[]{:S(2)}, u32[]{:S(2)}) collective-permute-start(bf16[64,2048]{1,0:T(8,128)(2,1)S(1)} %shard_map.143), channel_id=1, source_target_pairs={{4,6},{5,7},{2,0},{3,1},{12,14},{13,15},{10,8},{11,9},{20,22},{21,... | collective-permute-start | bytes 786440 | tf_op jit(solution)/shard_map/ppermute | solution.py:268
  123.7 5.3 %copy-start.3 = (f32[1,128,2048]{2,1,0:T(8,128)S(1)}, f32[1,128,2048]{2,1,0:T(8,128)}, u32[]{:S(2)}) copy-start(f32[1,128,2048]{2,1,0:T(8,128)} %param.14) | copy-start | bytes 3145732
  123.7 5.3 %copy-start.5 = (bf16[1,128,2048]{2,1,0:T(8,128)(2,1)S(1)}, bf16[1,128,2048]{2,1,0:T(8,128)(2,1)}, u32[]{:S(2)}) copy-start(bf16[1,128,2048]{2,1,0:T(8,128)(2,1)} %param.11) | copy-start | bytes 1572868
  123.7 17.1 %collective-permute-start.31 = (bf16[64,2048]{1,0:T(8,128)(2,1)S(1)}, bf16[64,2048]{1,0:T(8,128)(2,1)S(1)}, u32[]{:S(2)}, u32[]{:S(2)}) collective-permute-start(bf16[64,2048]{1,0:T(8,128)(2,1)S(1)} %shard_map.146), channel_id=1, source_target_pairs={{4,6},{5,7},{2,0},{3,1},{12,14},{13,15},{10,8},{11,9},{20,22},{21,... | collective-permute-start | bytes 786440 | tf_op jit(solution)/shard_map/ppermute | solution.py:268

commit v4 on v3

--- a/solution.py
+++ b/solution.py
@@ -72,7 +72,7 @@
     normed_b = normalize(inputs)[0].astype(bf16)
     x_out[place, :] = inputs
     normed_out[place, :] = normed_b
-    total = inputs.astype(f32)
+    total = inputs.astype(f32) if out_ref is not None else None
     for part, ready in parts:
         ready(0)
         upper = jnp.dot(normed_b, weights_ref[0, :, part], preferred_element_type=f32)
@@ -85,8 +85,10 @@
             gelu_coef * (1.0 + 3.0 * 0.044715 * square)
         )
         ready(1)
-        total = total + across(hidden, weights_ref[1, :, part])
-    out_ref[...] = total.astype(bf16)
+        if out_ref is not None:
+            total = total + across(hidden, weights_ref[1, :, part])
+    if out_ref is not None:
+        out_ref[...] = total.astype(bf16)
 
 
 def saved_shapes(tokens, width, channels):
@@ -116,10 +118,12 @@
 
         @on_turn(0)
         def _():
-            for copy in (*first, *copies.values()):
+            for copy in (*first, *(copies[i, 0] for i in range(slabs))):
                 copy.start()
             for copy in first:
                 copy.wait()
+            for i in range(slabs):
+                copies[i, 1].start()
             for m in range(micro):
                 ids = ids_ref[m : m + 1, :]
                 hot = (lax.broadcasted_iota(jnp.int32, (vocab, per), 0) == ids).astype(f32).astype(bf16)
@@ -156,28 +160,30 @@
     )[0]
 
 
-def forward(turn, inputs, weights, saved, start, rows, tokens):
+def forward(turn, inputs, weights, saved, start, rows, tokens, last):
     width = inputs.shape[1]
     channels = weights.shape[2]
     step = channels // slabs
+    outs = saved_shapes(tokens, width, channels) + ([] if last else [((rows, width), bf16)])
 
     def kernel(x_ref, w_ref, *refs):
-        out_ref, saved_out = refs[-5], refs[-4:]
+        refs = refs[len(saved) :]
 
         @on_turn(turn)
         def _():
             parts = [(pl.ds(i * step, step), lambda m: None) for i in range(slabs)]
-            block_on(rows_of(x_ref, start, rows), parts, w_ref, out_ref, saved_out, pl.ds(start, rows))
+            out_ref = None if last else refs[4]
+            block_on(rows_of(x_ref, start, rows), parts, w_ref, out_ref, refs[:4], pl.ds(start, rows))
 
     got = call(
         kernel,
-        [((rows, width), bf16), *saved_shapes(tokens, width, channels)],
+        outs,
         [inputs, weights, *saved],
-        {2 + i: 1 + i for i in range(4)},
-        flops=4 * rows * width * channels,
+        {2 + i: i for i in range(4)},
+        flops=(2 if last else 4) * rows * width * channels,
         transcendentals=rows * channels,
     )
-    return got[0], got[1:]
+    return (None if last else got[4]), got[:4]
 
 
 def backward(turn, grad, weights, saved, kept, start, rows, tokens, last):
@@ -251,7 +257,7 @@
     for hop in range(count):
         for c in range(len(chunks)):
             if hop or c:
-                out, saved = forward(hop, state[c], weights, saved, *chunks[c], tokens)
+                out, saved = forward(hop, state[c], weights, saved, *chunks[c], tokens, hop + 1 == count)
             else:
                 out = entered
             if hop + 1 < count:
@@ -278,8 +284,8 @@
     def kernel(error_ref, *refs):
         outs = refs[len(known) + len(parts) :]
         z, core = place_on_line()
-        for (by, _, slot), ref in zip(parts, refs[len(known) :]):
-            block = 2 * ((z + by) & 3) + (core if mine else 1 - core)
+        for (chip, _, slot), ref in zip(parts, refs[len(known) :]):
+            block = 2 * chip(z) + (core if mine else 1 - core)
             rows = pl.ds(pl.multiple_of(block * owned, owned), owned)
             values = ref[...] if mine else ref[slot]
             if mine:
@@ -461,37 +467,40 @@
     )
 
 
-def turned_round(own, up, down):
-    def kernel(own_ref, up_ref, lowerref, out_ref):
+def turned_round(own, inner):
+    def kernel(own_ref, inner_ref, out_ref):
         z, _ = place_on_line()
-        for ref, here in ((own_ref, jnp.logical_or(z == 0, z == 3)), (up_ref, z == 2), (lowerref, z == 1)):
+        at_end = jnp.logical_or(z == 0, z == 3)
+        for ref, here in ((own_ref, at_end), (inner_ref, jnp.logical_not(at_end))):
 
             @pl.when(here)
             def _(ref=ref):
                 out_ref[...] = ref[...]
 
-    return call(kernel, [(own.shape, own.dtype)], [own, up, down])[0]
+    return call(kernel, [(own.shape, own.dtype)], [own, inner])[0]
 
 
 def on_a_line(token_ids, embed, weights, variance, momentum, error, server_error, cotangent):
     replicas = lax.axis_size("dp")
-    up = along(momentum, [(i, (i + 1) % 4) for i in range(4)])
-    lower = along(momentum, [(i, (i + 3) % 4) for i in range(4)])
-    onward = turned_round(momentum, up, lower)
+    inner = along(momentum, [(1, 2), (2, 1), (0, 3), (3, 0)])
+    beside = along(momentum, [(0, 1), (1, 0), (2, 3), (3, 2)])
+    onward = turned_round(momentum, inner)
     onward = along(onward, [(0, 2), (2, 3), (3, 1), (1, 0)])
-    known, out_a = known_rows(error, [], [(0, momentum, 0), (3, up, 1), (1, lower, 2)], True)
+    first = [(lambda z: z, momentum, 0), (lambda z: 3 - z, inner, 1), (lambda z: z ^ 1, beside, 2)]
+    known, out_a = known_rows(error, [], first, True)
     in_a = swapped(out_a)
-    known, out_b = known_rows(error, [known], [(2, onward, 0)], True)
+    known, out_b = known_rows(error, [known], [(lambda z: z ^ 2, onward, 0)], True)
     in_b = swapped(out_b)
-    known = known_rows(error, [known], [(0, in_a, 0), (3, in_a, 1), (1, in_a, 2), (2, in_b, 0)], False)[0]
+    rest = [(chip, in_a, slot) for chip, _, slot in first] + [(lambda z: z ^ 2, in_b, 0)]
+    known = known_rows(error, [known], rest, False)[0]
     normed, hidden, grad, upper, weights = relay(token_ids, embed, weights, cotangent)
     combined, sums = add_gradient(known, normed, upper, grad, hidden)
-    names = ("far", "mid", "near", "own")
-    made = packed_part(sums, combined, (0,)) + packed_part(sums, combined, (1, 2, 3))
-    mine, other = {}, {}
-    for i, name in enumerate(names):
-        mine[name] = made[2 * i + 1]
-        other[name] = swapped(made[2 * i])
+    far_out, far = packed_part(sums, combined, (0,))
+    made = packed_part(sums, combined, (1, 2, 3))
+    mine = {"far": far, "mid": made[1], "near": made[3], "own": made[5]}
+    other = {}
+    for name, out in (("far", far_out), ("mid", made[0]), ("near", made[2]), ("own", made[4])):
+        other[name] = swapped(out)
 
     def summed(name, pairs, cut, count, *more):
         total = added(cut, count, mine[name], other[name], *more)
@@ -499,7 +508,8 @@
 
     ends, inner, outer = [(0, 1), (3, 2)], [(1, 2), (2, 1)], [(2, 3), (1, 0)]
     both = range(halves)
-    a1 = [summed("far", ends, h, halves) for h in both]
+    both_ways = [(0, 1), (1, 0), (2, 3), (3, 2)]
+    a1 = [summed("far", ends if h else both_ways, h, halves) for h in both]
     a2 = [summed("mid", ends, h, halves) for h in both]
     a3 = [summed("near", ends, 0, 1)]
     b2 = [summed("far", inner, h, halves, a1[h]) for h in both]

time: 144 us -> 142 us (0.986)
  Pallas kernels: 21.7 us -> 19.9 us
  local copies, waits for them, and re-layouts: 3.57 us -> 5.17 us
    ppermute x14, waiting for transfers between devices: 53.1 us -> 49.6 us  [along(): lax.ppermute(array, 'dp', [(2 * a + c, 2 * b + c) for a, b in pairs for c...]
    ppermute x12, waiting for transfers between devices: 28.1 us -> 30.5 us  [passed(): return lax.ppermute(array, 'section', [(source, target)])]
    pallas_call x38, Pallas kernels: 21.7 us -> 19.9 us  [call(): pl.pallas_call(kernel, out_shape=[pltpu.VMEM(shape, dtype) for shape, dty...]
    unnamed x12 -> x14, local copies, waits for them, and re-layouts: 3.57 us -> 5.17 us
  transfers between devices with their start and end apart: 32 -> 32, of which waited for: 14 -> 14; matrix products, arithmetic and copies ran while one was open for 0% -> 0% of each run, Pallas kernels for 11% -> 10%
where the time goes in v4:
time: 142 us; the launch traced here: 141 us
  waiting for transfers between devices  80.2 us (56%)
  starting transfers between devices  34.1 us (24%)
  Pallas kernels  19.9 us (14%)
  local copies, waits for them, and re-layouts  5.17 us (4%)
  between operations  1.45 us (1%)
    ppermute x14, waiting for transfers between devices, along(): lax.ppermute(array, 'dp', [(2 * a + c, 2 * b + c) for a, b in pairs for c...  49.6 us
    ppermute x12, waiting for transfers between devices, passed(): return lax.ppermute(array, 'section', [(source, target)])  30.5 us
    ppermute x14, starting transfers between devices, along(): lax.ppermute(array, 'dp', [(2 * a + c, 2 * b + c) for a, b in pairs for c...  22.5 us
    pallas_call x38, Pallas kernels, call(): pl.pallas_call(kernel, out_shape=[pltpu.VMEM(shape, dtype) for shape, dty...  19.9 us
    ppermute x12, starting transfers between devices, passed(): return lax.ppermute(array, 'section', [(source, target)])  10.7 us
    unnamed x14, local copies, waits for them, and re-layouts  5.17 us
  transfers between devices with their start and end apart: 32, of which 14 were waited for; matrix products, arithmetic and copies ran while one was open for 0% of the time, Pallas kernels for 10%

profile of v4, /device:TPU:0, one launch (start us, length us, event | category | flops | bytes accessed | tf_op | source)
XLA Modules:
  0.0 140.8 jit_solution(7535443720653812096)
XLA Ops:
  0.6 5.1 %collective-permute-start = (bf16[128,2048]{1,0:T(8,128)(2,1)}, bf16[128,2048]{1,0:T(8,128)(2,1)S(1)}, u32[]{:S(2)}, u32[]{:S(2)}) collective-permute-start(bf16[128,2048]{1,0:T(8,128)(2,1)} %bitcast.13), channel_id=1, source_target_pairs={{2,4},{3,5},{4,2},{5,3},{0,6},{1,7},{6,0},{7,1},{10,12},{11,13},{1... | collective-permute-start | bytes 1572872 | tf_op jit(solution)/shard_map/ppermute | solution.py:274
  5.8 13.1 %collective-permute-done.refs_1_.inner_ref = bf16[128,2048]{1,0:T(8,128)(2,1)S(1)} collective-permute-done((bf16[128,2048]{1,0:T(8,128)(2,1)}, bf16[128,2048]{1,0:T(8,128)(2,1)S(1)}, u32[]{:S(2)}, u32[]{:S(2)}) %collective-permute-start) | collective-permute-done | bytes 524320 | tf_op jit(solution)/shard_map/ppermute | solution.py:274
  18.9 10.4 %collective-permute-done.1.refs_2_ = bf16[128,2048]{1,0:T(8,128)(2,1)S(1)} collective-permute-done((bf16[128,2048]{1,0:T(8,128)(2,1)}, bf16[128,2048]{1,0:T(8,128)(2,1)S(1)}, u32[]{:S(2)}, u32[]{:S(2)}) %collective-permute-start.1) | collective-permute-done | bytes 524320 | tf_op jit(solution)/shard_map/ppermute | solution.py:274
  29.2 2.2 %copy-done = bf16[1,1,2,512,2048]{4,3,2,1,0:T(8,128)(2,1)S(1)} copy-done((bf16[1,1,2,512,2048]{4,3,2,1,0:T(8,128)(2,1)S(1)}, bf16[1,1,2,512,2048]{4,3,2,1,0:T(8,128)(2,1)}, u32[]{:S(2)}) %copy-start) | copy-done | bytes 4194328
  31.4 1.0 copy-done.2
  32.5 0.5 shard_map.111
  33.1 4.0 %shard_map.115 = (bf16[128,512]{1,0:T(8,128)(2,1)S(1)}, bf16[256,512]{1,0:T(8,128)(2,1)S(1)}, bf16[2,512,2048]{2,1,0:T(8,128)(2,1)S(1)}, bf16[256,512]{1,0:T(8,1...) custom-call(s32[4,64]{1,0:T(4,128)} %ids_hbm.1, ...), custom_call_target="tpu_custom_call" | custom-call | flops 536870912 | tf_op jit(solution)/shard_map/pallas_call | solution.py:23
  37.1 1.3 collective-permute-start.6
  38.4 1.0 copy-done.3
  39.5 0.7 collective-permute-start.2
  40.1 1.7 %shard_map.117 = (bf16[256,512]{1,0:T(8,128)(2,1)S(1)}, bf16[256,512]{1,0:T(8,128)(2,1)S(1)}, bf16[256,2048]{1,0:T(8,128)(2,1)S(1)}, f32[256,2048]{1,0:T(8,128)S(1)}, bf16[128,512]{1,0:T(8,128)(2,1)S(1)}) custom-call(bf16[256,512]{1,0:T(8,128)(2,1)S(1)} %get-tuple-element.89.x_ref, ...), custom_call_target="tpu_custom_call", output_to_operand_aliasing={{0}: (2, {}), {1}: (3, {}), {2}: (4, {}), {3}: (5, {})} | custom-call | flops 536870912 | bytes 8126464 | tf_op jit(solution)/shard_map/pallas_call | solution.py:23
  41.9 1.3 collective-permute-start.5
  43.2 0.7 collective-permute-start.8
  43.9 2.7 %collective-permute-done.5.x_ref = bf16[128,512]{1,0:T(8,128)(2,1)S(1)} collective-permute-done((bf16[128,512]{1,0:T(8,128)(2,1)S(1)}, bf16[128,512]{1,0:T(8,128)(2,1)S(1)}, u32[]{:S(2)}, u32[]{:S(2)}) %collective-permute-start.5) | collective-permute-done | bytes 131104 | tf_op jit(solution)/shard_map/ppermute | solution.py:249
  46.6 0.7 collective-permute-start.7
  47.3 0.7 collective-permute-start.10
  48.0 0.7 collective-permute-start.9
  48.7 0.9 copy-done.5
  49.6 0.8 collective-permute-start.12
  50.5 3.3 %collective-permute-done.2.refs_1_ = bf16[128,2048]{1,0:T(8,128)(2,1)S(1)} collective-permute-done((bf16[128,2048]{1,0:T(8,128)(2,1)S(1)}, bf16[128,2048]{1,0:T(8,128)(2,1)S(1)}, u32[]{:S(2)}, u32[]{:S(2)}) %collective-permute-start.2) | collective-permute-done | bytes 524320 | tf_op jit(solution)/shard_map/ppermute | solution.py:274
  53.8 0.2 shard_map.113
  54.1 0.7 collective-permute-start.11
  54.8 0.7 collective-permute-start.14
  55.5 0.7 collective-permute-start.13
  56.2 1.3 collective-permute-start.16
  57.6 1.3 collective-permute-start.15
  58.9 21.2 %collective-permute-done.16.grad_ref = bf16[128,512]{1,0:T(8,128)(2,1)S(1)} collective-permute-done((bf16[128,512]{1,0:T(8,128)(2,1)S(1)}, bf16[128,512]{1,0:T(8,128)(2,1)S(1)}, u32[]{:S(2)}, u32[]{:S(2)}) %collective-permute-start.16) | collective-permute-done | bytes 131104 | tf_op jit(solution)/shard_map/ppermute | solution.py:249
  80.1 0.4 shard_map.130
  80.5 6.6 %collective-permute-done.15.grad_ref = bf16[128,512]{1,0:T(8,128)(2,1)S(1)} collective-permute-done((bf16[128,512]{1,0:T(8,128)(2,1)S(1)}, bf16[128,512]{1,0:T(8,128)(2,1)S(1)}, u32[]{:S(2)}, u32[]{:S(2)}) %collective-permute-start.15) | collective-permute-done | bytes 131104 | tf_op jit(solution)/shard_map/ppermute | solution.py:249
  87.1 0.5 shard_map.131
  87.6 0.6 shard_map.114.known_ref
  88.3 2.8 %shard_map.132 = (f32[8,128,2048]{2,1,0:T(8,128)S(1)}, f32[8,128]{1,0:T(8,128)S(1)}) custom-call(f32[8,128,2048]{2,1,0:T(8,128)S(1)} %shard_map.114.known_ref, bf16[256,512]{1,0:T(8,128)(2,1)S(1)} %get-tuple-element.125.normed_ref, bf16[256,2048]{1,0:T(8,128)(2,1)S(1)} %get-tuple-element.148.upper_ref, ...), custom_call_target="tpu_custom_call", output_to_operand_aliasing={{0}: (0, {})} | custom-call | flops 1073741824 | bytes 11010048 | tf_op jit(solution)/shard_map/pallas_call | solution.py:23
  91.0 0.4 shard_map.140
  91.5 1.1 shard_map.133
  92.7 0.6 collective-permute-start.20
  93.3 0.1 collective-permute-done.25.refs_1_
  93.5 1.4 %collective-permute-start.26 = (bf16[64,2048]{1,0:T(8,128)(2,1)S(1)}, bf16[64,2048]{1,0:T(8,128)(2,1)S(1)}, u32[]{:S(2)}, u32[]{:S(2)}) collective-permute-start(bf16[64,2048]{1,0:T(8,128)(2,1)S(1)} %shard_map.141), channel_id=1, source_target_pairs={{0,2},{1,3},{2,0},{3,1},{4,6},{5,7},{6,4},{7,5},{8,10},{9,11},{10,... | collective-permute-start | bytes 786440 | tf_op jit(solution)/shard_map/ppermute | solution.py:274
  95.0 2.6 %collective-permute-start.29 = (bf16[64,2048]{1,0:T(8,128)(2,1)S(1)}, bf16[64,2048]{1,0:T(8,128)(2,1)S(1)}, u32[]{:S(2)}, u32[]{:S(2)}) collective-permute-start(bf16[64,2048]{1,0:T(8,128)(2,1)S(1)} %shard_map.144), channel_id=1, source_target_pairs={{0,2},{1,3},{6,4},{7,5},{8,10},{9,11},{14,12},{15,13},{16,18},{17,... | collective-permute-start | bytes 786440 | tf_op jit(solution)/shard_map/ppermute | solution.py:274
  97.7 1.3 collective-permute-start.21
  99.1 1.5 %collective-permute-start.23 = (bf16[64,2048]{1,0:T(8,128)(2,1)S(1)}, bf16[64,2048]{1,0:T(8,128)(2,1)S(1)}, u32[]{:S(2)}, u32[]{:S(2)}) collective-permute-start(bf16[64,2048]{1,0:T(8,128)(2,1)S(1)} %shard_map.138), channel_id=1, source_target_pairs={{0,2},{1,3},{6,4},{7,5},{8,10},{9,11},{14,12},{15,13},{16,18},{17,... | collective-permute-start | bytes 786440 | tf_op jit(solution)/shard_map/ppermute | solution.py:274
  100.7 0.1 shard_map.135
  100.8 1.3 collective-permute-done.26.refs_2_
  102.1 0.1 shard_map.142
  102.2 0.7 collective-permute-start.27
  102.9 4.4 %collective-permute-done.29.refs_2_ = bf16[64,2048]{1,0:T(8,128)(2,1)S(1)} collective-permute-done((bf16[64,2048]{1,0:T(8,128)(2,1)S(1)}, bf16[64,2048]{1,0:T(8,128)(2,1)S(1)}, u32[]{:S(2)}, u32[]{:S(2)}) %collective-permute-start.29) | collective-permute-done | bytes 262176 | tf_op jit(solution)/shard_map/ppermute | solution.py:274
  107.3 0.1 shard_map.145
  107.4 0.7 collective-permute-start.30
  108.0 4.8 %collective-permute-done.21.refs_2_ = bf16[64,2048]{1,0:T(8,128)(2,1)S(1)} collective-permute-done((bf16[64,2048]{1,0:T(8,128)(2,1)S(1)}, bf16[64,2048]{1,0:T(8,128)(2,1)S(1)}, u32[]{:S(2)}, u32[]{:S(2)}) %collective-permute-start.21) | collective-permute-done | bytes 262176 | tf_op jit(solution)/shard_map/ppermute | solution.py:274
  112.9 4.4 %collective-permute-start.19 = (bf16[128,2048]{1,0:T(8,128)(2,1)S(1)}, bf16[128,2048]{1,0:T(8,128)(2,1)S(1)}, u32[]{:S(2)}, u32[]{:S(2)}) collective-permute-start(bf16[128,2048]{1,0:T(8,128)(2,1)S(1)} %shard_map.135), channel_id=1, source_target_pairs={{0,2},{1,3},{6,4},{7,5},{8,10},{9,11},{14,12},{15,13},{16,18},{17,... | collective-permute-start | bytes 1572872 | tf_op jit(solution)/shard_map/ppermute | solution.py:274
  117.3 0.1 shard_map.137
  117.4 1.1 collective-permute-done.23.refs_2_
  118.5 0.7 collective-permute-start.22
  119.2 0.1 shard_map.139
  119.3 0.7 collective-permute-start.24
  120.0 0.1 shard_map.143
  120.1 1.3 collective-permute-start.28
  121.4 0.1 shard_map.146
  121.5 1.4 %collective-permute-start.31 = (bf16[64,2048]{1,0:T(8,128)(2,1)S(1)}, bf16[64,2048]{1,0:T(8,128)(2,1)S(1)}, u32[]{:S(2)}, u32[]{:S(2)}) collective-permute-start(bf16[64,2048]{1,0:T(8,128)(2,1)S(1)} %shard_map.146), channel_id=1, source_target_pairs={{4,6},{5,7},{2,0},{3,1},{12,14},{13,15},{10,8},{11,9},{20,22},{21,... | collective-permute-start | bytes 786440 | tf_op jit(solution)/shard_map/ppermute | solution.py:274
  123.0 3.8 %shard_map.148 = bf16[1024,2048]{1,0:T(8,128)(2,1)} custom-call(f32[8,128]{1,0:T(8,128)S(1)} %get-tuple-element.151.sum_ref, f32[8,128,2048]{2,1,0:T(8,128)S(1)} %get-tuple-element.152.combined_ref), custom_call_target="tpu_custom_call" | custom-call | bytes 8392704 | tf_op jit(solution)/shard_map/pallas_call | solution.py:23
  126.8 0.6 shard_map.134
  127.4 1.6 %collective-permute-done.19.refs_0_ = bf16[128,2048]{1,0:T(8,128)(2,1)S(1)} collective-permute-done((bf16[128,2048]{1,0:T(8,128)(2,1)S(1)}, bf16[128,2048]{1,0:T(8,128)(2,1)S(1)}, u32[]{:S(2)}, u32[]{:S(2)}) %collective-permute-start.19) | collective-permute-done | bytes 524320 | tf_op jit(solution)/shard_map/ppermute | solution.py:274
  129.1 6.4 %collective-permute-done.28.refs_3_ = bf16[64,2048]{1,0:T(8,128)(2,1)S(1)} collective-permute-done((bf16[64,2048]{1,0:T(8,128)(2,1)S(1)}, bf16[64,2048]{1,0:T(8,128)(2,1)S(1)}, u32[]{:S(2)}, u32[]{:S(2)}) %collective-permute-start.28) | collective-permute-done | bytes 262176 | tf_op jit(solution)/shard_map/ppermute | solution.py:274
  135.5 3.1 %collective-permute-done.31.refs_4_ = bf16[64,2048]{1,0:T(8,128)(2,1)S(1)} collective-permute-done((bf16[64,2048]{1,0:T(8,128)(2,1)S(1)}, bf16[64,2048]{1,0:T(8,128)(2,1)S(1)}, u32[]{:S(2)}, u32[]{:S(2)}) %collective-permute-start.31) | collective-permute-done | bytes 262176 | tf_op jit(solution)/shard_map/ppermute | solution.py:274
  138.6 2.1 %shard_map.147 = (bf16[128,2048]{1,0:T(8,128)(2,1)}, bf16[128,2048]{1,0:T(8,128)(2,1)}, f32[128,2048]{1,0:T(8,128)}) custom-call(f32[128,2048]{1,0:T(8,128)S(1)} %get-tuple-element.155.base_ref, f32[128,2048]{1,0:T(8,128)S(1)} %get-tuple-element.156.rate_ref, bf16[2,512,2048]{2,1,0:T(8,128)(2,1)S(1)} %shard_map.116.w_ref.weights_ref, ...), custom_call_target="tpu_custom_call" | custom-call | bytes 7864320 | tf_op jit(solution)/shard_map/pallas_call | solution.py:23
  (52 shorter events, 0.9 us)
Async XLA Ops:
  0.6 18.2 %collective-permute-start = (bf16[128,2048]{1,0:T(8,128)(2,1)}, bf16[128,2048]{1,0:T(8,128)(2,1)S(1)}, u32[]{:S(2)}, u32[]{:S(2)}) collective-permute-start(bf16[128,2048]{1,0:T(8,128)(2,1)} %bitcast.13), channel_id=1, source_target_pairs={{2,4},{3,5},{4,2},{5,3},{0,6},{1,7},{6,0},{7,1},{10,12},{11,13},{1... | collective-permute-start | bytes 1572872 | tf_op jit(solution)/shard_map/ppermute | solution.py:274
  5.8 23.5 %collective-permute-start.1 = (bf16[128,2048]{1,0:T(8,128)(2,1)}, bf16[128,2048]{1,0:T(8,128)(2,1)S(1)}, u32[]{:S(2)}, u32[]{:S(2)}) collective-permute-start(bf16[128,2048]{1,0:T(8,128)(2,1)} %bitcast.14), channel_id=1, source_target_pairs={{0,2},{1,3},{2,0},{3,1},{4,6},{5,7},{6,4},{7,5},{8,10},{9,11},{10,... | collective-permute-start | bytes 1572872 | tf_op jit(solution)/shard_map/ppermute | solution.py:274
  29.2 2.2 %copy-start = (bf16[1,1,2,512,2048]{4,3,2,1,0:T(8,128)(2,1)S(1)}, bf16[1,1,2,512,2048]{4,3,2,1,0:T(8,128)(2,1)}, u32[]{:S(2)}) copy-start(bf16[1,1,2,512,2048]{4,3,2,1,0:T(8,128)(2,1)} %param.13) | copy-start | bytes 12582916
  31.4 1.0 copy-start.2
  33.0 54.6 %collective-permute-start.3 = (bf16[3,128,2048]{2,1,0:T(8,128)(2,1)S(1)}, bf16[3,128,2048]{2,1,0:T(8,128)(2,1)S(1)}, u32[]{:S(2)}, u32[]{:S(2)}) collective-permute-start(bf16[3,128,2048]{2,1,0:T(8,128)(2,1)S(1)} %get-tuple-element.87), channel_id=1, source_target_pairs={{0,1},{1,0},{2,3},{3,2},{4,5},{5,4},{6,7},{7,6},{8,9},{9,8},{10,11... | collective-permute-start | bytes 4718600 | tf_op jit(solution)/shard_map/ppermute | solution.py:278
  37.1 6.1 %collective-permute-start.6 = (bf16[128,512]{1,0:T(8,128)(2,1)S(1)}, bf16[128,512]{1,0:T(8,128)(2,1)S(1)}, u32[]{:S(2)}, u32[]{:S(2)}) collective-permute-start(bf16[128,512]{1,0:T(8,128)(2,1)S(1)} %get-tuple-element.96), channel_id=1, source_target_pairs={{0,8},{1,9},{2,10},{3,11},{4,12},{5,13},{6,14},{7,15}} | collective-permute-start | bytes 393224 | tf_op jit(solution)/shard_map/ppermute | solution.py:249
  38.4 1.0 copy-start.3
  39.5 14.4 %collective-permute-start.2 = (bf16[128,2048]{1,0:T(8,128)(2,1)S(1)}, bf16[128,2048]{1,0:T(8,128)(2,1)S(1)}, u32[]{:S(2)}, u32[]{:S(2)}) collective-permute-start(bf16[128,2048]{1,0:T(8,128)(2,1)S(1)} %shard_map.112), channel_id=1, source_target_pairs={{0,4},{1,5},{4,6},{5,7},{6,2},{7,3},{2,0},{3,1},{8,12},{9,13},{12,... | collective-permute-start | bytes 1572872 | tf_op jit(solution)/shard_map/ppermute | solution.py:274
  41.9 4.7 %collective-permute-start.5 = (bf16[128,512]{1,0:T(8,128)(2,1)S(1)}, bf16[128,512]{1,0:T(8,128)(2,1)S(1)}, u32[]{:S(2)}, u32[]{:S(2)}) collective-permute-start(bf16[128,512]{1,0:T(8,128)(2,1)S(1)} %get-tuple-element.95), channel_id=1, source_target_pairs={{0,8},{1,9},{2,10},{3,11},{4,12},{5,13},{6,14},{7,15}} | collective-permute-start | bytes 393224 | tf_op jit(solution)/shard_map/ppermute | solution.py:249
  43.2 4.0 %collective-permute-start.8 = (bf16[128,512]{1,0:T(8,128)(2,1)S(1)}, bf16[128,512]{1,0:T(8,128)(2,1)S(1)}, u32[]{:S(2)}, u32[]{:S(2)}) collective-permute-start(bf16[128,512]{1,0:T(8,128)(2,1)S(1)} %get-tuple-element.106), channel_id=1, source_target_pairs={{8,16},{9,17},{10,18},{11,19},{12,20},{13,21},{14,22},{15,23}} | collective-permute-start | bytes 393224 | tf_op jit(solution)/shard_map/ppermute | solution.py:249
  46.6 1.4 collective-permute-start.7
  47.3 1.4 collective-permute-start.10
  48.0 2.5 %collective-permute-start.9 = (bf16[128,512]{1,0:T(8,128)(2,1)S(1)}, bf16[128,512]{1,0:T(8,128)(2,1)S(1)}, u32[]{:S(2)}, u32[]{:S(2)}) collective-permute-start(bf16[128,512]{1,0:T(8,128)(2,1)S(1)} %get-tuple-element.115), channel_id=1, source_target_pairs={{16,24},{17,25},{18,26},{19,27},{20,28},{21,29},{22,30},{23,31}} | collective-permute-start | bytes 393224 | tf_op jit(solution)/shard_map/ppermute | solution.py:249
  48.7 1.0 copy-start.5
  49.6 5.2 %collective-permute-start.12 = (bf16[128,512]{1,0:T(8,128)(2,1)S(1)}, bf16[128,512]{1,0:T(8,128)(2,1)S(1)}, u32[]{:S(2)}, u32[]{:S(2)}) collective-permute-start(bf16[128,512]{1,0:T(8,128)(2,1)S(1)} %get-tuple-element.131), channel_id=1, source_target_pairs={{24,16},{25,17},{26,18},{27,19},{28,20},{29,21},{30,22},{31,23}} | collective-permute-start | bytes 393224 | tf_op jit(solution)/shard_map/ppermute | solution.py:249
  50.5 3.4 %copy-start.1 = (bf16[1,1,2,512,2048]{4,3,2,1,0:T(8,128)(2,1)S(1)}, bf16[1,1,2,512,2048]{4,3,2,1,0:T(8,128)(2,1)}, u32[]{:S(2)}) copy-start(bf16[1,1,2,512,2048]{4,3,2,1,0:T(8,128)(2,1)} %param.13) | copy-start | bytes 12582916
  54.0 33.6 %collective-permute-start.4 = (bf16[1,128,2048]{2,1,0:T(8,128)(2,1)S(1)}, bf16[1,128,2048]{2,1,0:T(8,128)(2,1)S(1)}, u32[]{:S(2)}, u32[]{:S(2)}) collective-permute-start(bf16[1,128,2048]{2,1,0:T(8,128)(2,1)S(1)} %get-tuple-element.88), channel_id=1, source_target_pairs={{0,1},{1,0},{2,3},{3,2},{4,5},{5,4},{6,7},{7,6},{8,9},{9,8},{10,11... | collective-permute-start | bytes 1572872 | tf_op jit(solution)/shard_map/ppermute | solution.py:278
  54.1 1.4 collective-permute-start.11
  54.8 1.4 collective-permute-start.14
  55.5 2.0 %collective-permute-start.13 = (bf16[128,512]{1,0:T(8,128)(2,1)S(1)}, bf16[128,512]{1,0:T(8,128)(2,1)S(1)}, u32[]{:S(2)}, u32[]{:S(2)}) collective-permute-start(bf16[128,512]{1,0:T(8,128)(2,1)S(1)} %get-tuple-element.136), channel_id=1, source_target_pairs={{16,8},{17,9},{18,10},{19,11},{20,12},{21,13},{22,14},{23,15}} | collective-permute-start | bytes 393224 | tf_op jit(solution)/shard_map/ppermute | solution.py:249
  56.2 23.8 %collective-permute-start.16 = (bf16[128,512]{1,0:T(8,128)(2,1)S(1)}, bf16[128,512]{1,0:T(8,128)(2,1)S(1)}, u32[]{:S(2)}, u32[]{:S(2)}) collective-permute-start(bf16[128,512]{1,0:T(8,128)(2,1)S(1)} %get-tuple-element.143), channel_id=1, source_target_pairs={{8,0},{9,1},{10,2},{11,3},{12,4},{13,5},{14,6},{15,7}} | collective-permute-start | bytes 393224 | tf_op jit(solution)/shard_map/ppermute | solution.py:249
  57.6 29.6 %collective-permute-start.15 = (bf16[128,512]{1,0:T(8,128)(2,1)S(1)}, bf16[128,512]{1,0:T(8,128)(2,1)S(1)}, u32[]{:S(2)}, u32[]{:S(2)}) collective-permute-start(bf16[128,512]{1,0:T(8,128)(2,1)S(1)} %get-tuple-element.142), channel_id=1, source_target_pairs={{8,0},{9,1},{10,2},{11,3},{12,4},{13,5},{14,6},{15,7}} | collective-permute-start | bytes 393224 | tf_op jit(solution)/shard_map/ppermute | solution.py:249
  91.5 2.0 %collective-permute-start.25 = (bf16[128,2048]{1,0:T(8,128)(2,1)S(1)}, bf16[128,2048]{1,0:T(8,128)(2,1)S(1)}, u32[]{:S(2)}, u32[]{:S(2)}) collective-permute-start(bf16[128,2048]{1,0:T(8,128)(2,1)S(1)} %get-tuple-element.162), channel_id=1, source_target_pairs={{0,1},{1,0},{2,3},{3,2},{4,5},{5,4},{6,7},{7,6},{8,9},{9,8},{10,11... | collective-permute-start | bytes 1572872 | tf_op jit(solution)/shard_map/ppermute | solution.py:278
  92.7 4.9 %collective-permute-start.20 = (bf16[128,2048]{1,0:T(8,128)(2,1)S(1)}, bf16[128,2048]{1,0:T(8,128)(2,1)S(1)}, u32[]{:S(2)}, u32[]{:S(2)}) collective-permute-start(bf16[128,2048]{1,0:T(8,128)(2,1)S(1)} %get-tuple-element.160), channel_id=1, source_target_pairs={{0,1},{1,0},{2,3},{3,2},{4,5},{5,4},{6,7},{7,6},{8,9},{9,8},{10,11... | collective-permute-start | bytes 1572872 | tf_op jit(solution)/shard_map/ppermute | solution.py:278
  93.2 5.9 %collective-permute-start.18 = (bf16[128,2048]{1,0:T(8,128)(2,1)S(1)}, bf16[128,2048]{1,0:T(8,128)(2,1)S(1)}, u32[]{:S(2)}, u32[]{:S(2)}) collective-permute-start(bf16[128,2048]{1,0:T(8,128)(2,1)S(1)} %get-tuple-element.158), channel_id=1, source_target_pairs={{0,1},{1,0},{2,3},{3,2},{4,5},{5,4},{6,7},{7,6},{8,9},{9,8},{10,11... | collective-permute-start | bytes 1572872 | tf_op jit(solution)/shard_map/ppermute | solution.py:278
  93.5 8.6 %collective-permute-start.26 = (bf16[64,2048]{1,0:T(8,128)(2,1)S(1)}, bf16[64,2048]{1,0:T(8,128)(2,1)S(1)}, u32[]{:S(2)}, u32[]{:S(2)}) collective-permute-start(bf16[64,2048]{1,0:T(8,128)(2,1)S(1)} %shard_map.141), channel_id=1, source_target_pairs={{0,2},{1,3},{2,0},{3,1},{4,6},{5,7},{6,4},{7,5},{8,10},{9,11},{10,... | collective-permute-start | bytes 786440 | tf_op jit(solution)/shard_map/ppermute | solution.py:274
  95.0 12.3 %collective-permute-start.29 = (bf16[64,2048]{1,0:T(8,128)(2,1)S(1)}, bf16[64,2048]{1,0:T(8,128)(2,1)S(1)}, u32[]{:S(2)}, u32[]{:S(2)}) collective-permute-start(bf16[64,2048]{1,0:T(8,128)(2,1)S(1)} %shard_map.144), channel_id=1, source_target_pairs={{0,2},{1,3},{6,4},{7,5},{8,10},{9,11},{14,12},{15,13},{16,18},{17,... | collective-permute-start | bytes 786440 | tf_op jit(solution)/shard_map/ppermute | solution.py:274
  97.7 15.2 %collective-permute-start.21 = (bf16[64,2048]{1,0:T(8,128)(2,1)S(1)}, bf16[64,2048]{1,0:T(8,128)(2,1)S(1)}, u32[]{:S(2)}, u32[]{:S(2)}) collective-permute-start(bf16[64,2048]{1,0:T(8,128)(2,1)S(1)} %shard_map.136), channel_id=1, source_target_pairs={{0,2},{1,3},{6,4},{7,5},{8,10},{9,11},{14,12},{15,13},{16,18},{17,... | collective-permute-start | bytes 786440 | tf_op jit(solution)/shard_map/ppermute | solution.py:274
  99.0 22.5 %collective-permute-start.17 = (bf16[128,2048]{1,0:T(8,128)(2,1)S(1)}, bf16[128,2048]{1,0:T(8,128)(2,1)S(1)}, u32[]{:S(2)}, u32[]{:S(2)}) collective-permute-start(bf16[128,2048]{1,0:T(8,128)(2,1)S(1)} %get-tuple-element.154), channel_id=1, source_target_pairs={{0,1},{1,0},{2,3},{3,2},{4,5},{5,4},{6,7},{7,6},{8,9},{9,8},{10,11... | collective-permute-start | bytes 1572872 | tf_op jit(solution)/shard_map/ppermute | solution.py:278
  99.1 19.3 %collective-permute-start.23 = (bf16[64,2048]{1,0:T(8,128)(2,1)S(1)}, bf16[64,2048]{1,0:T(8,128)(2,1)S(1)}, u32[]{:S(2)}, u32[]{:S(2)}) collective-permute-start(bf16[64,2048]{1,0:T(8,128)(2,1)S(1)} %shard_map.138), channel_id=1, source_target_pairs={{0,2},{1,3},{6,4},{7,5},{8,10},{9,11},{14,12},{15,13},{16,18},{17,... | collective-permute-start | bytes 786440 | tf_op jit(solution)/shard_map/ppermute | solution.py:274
  102.2 17.1 %collective-permute-start.27 = (bf16[64,2048]{1,0:T(8,128)(2,1)S(1)}, bf16[64,2048]{1,0:T(8,128)(2,1)S(1)}, u32[]{:S(2)}, u32[]{:S(2)}) collective-permute-start(bf16[64,2048]{1,0:T(8,128)(2,1)S(1)} %shard_map.142), channel_id=1, source_target_pairs={{2,4},{3,5},{4,2},{5,3},{10,12},{11,13},{12,10},{13,11},{18,20},{1... | collective-permute-start | bytes 786440 | tf_op jit(solution)/shard_map/ppermute | solution.py:274
  107.4 12.7 %collective-permute-start.30 = (bf16[64,2048]{1,0:T(8,128)(2,1)S(1)}, bf16[64,2048]{1,0:T(8,128)(2,1)S(1)}, u32[]{:S(2)}, u32[]{:S(2)}) collective-permute-start(bf16[64,2048]{1,0:T(8,128)(2,1)S(1)} %shard_map.145), channel_id=1, source_target_pairs={{2,4},{3,5},{4,2},{5,3},{10,12},{11,13},{12,10},{13,11},{18,20},{1... | collective-permute-start | bytes 786440 | tf_op jit(solution)/shard_map/ppermute | solution.py:274
  112.9 16.2 %collective-permute-start.19 = (bf16[128,2048]{1,0:T(8,128)(2,1)S(1)}, bf16[128,2048]{1,0:T(8,128)(2,1)S(1)}, u32[]{:S(2)}, u32[]{:S(2)}) collective-permute-start(bf16[128,2048]{1,0:T(8,128)(2,1)S(1)} %shard_map.135), channel_id=1, source_target_pairs={{0,2},{1,3},{6,4},{7,5},{8,10},{9,11},{14,12},{15,13},{16,18},{17,... | collective-permute-start | bytes 1572872 | tf_op jit(solution)/shard_map/ppermute | solution.py:274
  118.5 8.9 %collective-permute-start.22 = (bf16[64,2048]{1,0:T(8,128)(2,1)S(1)}, bf16[64,2048]{1,0:T(8,128)(2,1)S(1)}, u32[]{:S(2)}, u32[]{:S(2)}) collective-permute-start(bf16[64,2048]{1,0:T(8,128)(2,1)S(1)} %shard_map.137), channel_id=1, source_target_pairs={{2,4},{3,5},{4,2},{5,3},{10,12},{11,13},{12,10},{13,11},{18,20},{1... | collective-permute-start | bytes 786440 | tf_op jit(solution)/shard_map/ppermute | solution.py:274
  119.3 8.1 %collective-permute-start.24 = (bf16[64,2048]{1,0:T(8,128)(2,1)S(1)}, bf16[64,2048]{1,0:T(8,128)(2,1)S(1)}, u32[]{:S(2)}, u32[]{:S(2)}) collective-permute-start(bf16[64,2048]{1,0:T(8,128)(2,1)S(1)} %shard_map.139), channel_id=1, source_target_pairs={{2,4},{3,5},{4,2},{5,3},{10,12},{11,13},{12,10},{13,11},{18,20},{1... | collective-permute-start | bytes 786440 | tf_op jit(solution)/shard_map/ppermute | solution.py:274
  120.1 15.4 %collective-permute-start.28 = (bf16[64,2048]{1,0:T(8,128)(2,1)S(1)}, bf16[64,2048]{1,0:T(8,128)(2,1)S(1)}, u32[]{:S(2)}, u32[]{:S(2)}) collective-permute-start(bf16[64,2048]{1,0:T(8,128)(2,1)S(1)} %shard_map.143), channel_id=1, source_target_pairs={{4,6},{5,7},{2,0},{3,1},{12,14},{13,15},{10,8},{11,9},{20,22},{21,... | collective-permute-start | bytes 786440 | tf_op jit(solution)/shard_map/ppermute | solution.py:274
  121.5 5.3 %copy-start.4 = (f32[1,128,2048]{2,1,0:T(8,128)S(1)}, f32[1,128,2048]{2,1,0:T(8,128)}, u32[]{:S(2)}) copy-start(f32[1,128,2048]{2,1,0:T(8,128)} %param.14) | copy-start | bytes 3145732
  121.5 5.3 %copy-start.6 = (bf16[1,128,2048]{2,1,0:T(8,128)(2,1)S(1)}, bf16[1,128,2048]{2,1,0:T(8,128)(2,1)}, u32[]{:S(2)}) copy-start(bf16[1,128,2048]{2,1,0:T(8,128)(2,1)} %param.11) | copy-start | bytes 1572868
  121.5 17.1 %collective-permute-start.31 = (bf16[64,2048]{1,0:T(8,128)(2,1)S(1)}, bf16[64,2048]{1,0:T(8,128)(2,1)S(1)}, u32[]{:S(2)}, u32[]{:S(2)}) collective-permute-start(bf16[64,2048]{1,0:T(8,128)(2,1)S(1)} %shard_map.146), channel_id=1, source_target_pairs={{4,6},{5,7},{2,0},{3,1},{12,14},{13,15},{10,8},{11,9},{20,22},{21,... | collective-permute-start | bytes 786440 | tf_op jit(solution)/shard_map/ppermute | solution.py:274

commit v5 on v4

--- a/solution.py
+++ b/solution.py
@@ -147,8 +147,8 @@
     return got[0], got[1], got[2], got[3:]
 
 
-def fetched(weights, held_weights):
-    def kernel(weights_hbm, _, weights_ref, done):
+def fetched(weights, held_weights, after):
+    def kernel(weights_hbm, _, __, weights_ref, ___, done):
         @pl.when(lax.axis_index("section") != 0)
         def _():
             copy = pltpu.make_async_copy(weights_hbm, weights_ref, done)
@@ -156,8 +156,13 @@
             copy.wait()
 
     return call(
-        kernel, [(weights.shape, bf16)], [held_weights], {1: 0}, read=[weights], scratch=[pltpu.SemaphoreType.DMA]
-    )[0]
+        kernel,
+        [(weights.shape, bf16), (after.shape, after.dtype)],
+        [held_weights, after],
+        {1: 0, 2: 1},
+        read=[weights],
+        scratch=[pltpu.SemaphoreType.DMA],
+    )
 
 
 def forward(turn, inputs, weights, saved, start, rows, tokens, last):
@@ -241,7 +246,7 @@
     width = embed.shape[1]
     saved, kept = [], []
     entered, embedded, here, saved = enter(token_ids, embed, weights, chunks[0][1])
-    weights = fetched(weights, here)
+    elsewhere, weights = weights, here
     state = [embedded] * len(chunks)
     grads = [cotangent.reshape(tokens, width)] * len(chunks)
 
@@ -264,6 +269,9 @@
                 state[c] = passed(out, hop, hop + 1)
             else:
                 back(hop, c)
+        if hop == 0:
+            weights, first = fetched(elsewhere, weights, saved[0])
+            saved = [first, *saved[1:]]
     for hop in range(count - 2, -1, -1):
         for c in range(len(chunks)):
             back(hop, c)

time: 142 us -> 141 us (level)
  no operation moved by 1% of the time
where the time goes in v5:
time: 141 us
  waiting for transfers between devices  81 us (57%)
  starting transfers between devices  34.1 us (24%)
  Pallas kernels  20 us (14%)
  local copies, waits for them, and re-layouts  4.17 us (3%)
  between operations  1.45 us (1%)
    ppermute x14, waiting for transfers between devices, along(): lax.ppermute(array, 'dp', [(2 * a + c, 2 * b + c) for a, b in pairs for c...  49.9 us
    ppermute x12, waiting for transfers between devices, passed(): return lax.ppermute(array, 'section', [(source, target)])  30.9 us
    ppermute x14, starting transfers between devices, along(): lax.ppermute(array, 'dp', [(2 * a + c, 2 * b + c) for a, b in pairs for c...  22.5 us
    pallas_call x38, Pallas kernels, call(): pl.pallas_call(kernel, out_shape=[pltpu.VMEM(shape, dtype) for shape, dty...  20 us
    ppermute x12, starting transfers between devices, passed(): return lax.ppermute(array, 'section', [(source, target)])  10.7 us
    unnamed x14, local copies, waits for them, and re-layouts  4.17 us
  transfers between devices with their start and end apart: 32, of which 14 were waited for; matrix products, arithmetic and copies ran while one was open for 0% of the time, Pallas kernels for 10%

profile of v5, /device:TPU:0, one launch (start us, length us, event | category | flops | bytes accessed | tf_op | source)
XLA Modules:
  0.0 140.7 jit_solution(5367099303367934905)
XLA Ops:
  0.6 5.1 %collective-permute-start = (bf16[128,2048]{1,0:T(8,128)(2,1)}, bf16[128,2048]{1,0:T(8,128)(2,1)S(1)}, u32[]{:S(2)}, u32[]{:S(2)}) collective-permute-start(bf16[128,2048]{1,0:T(8,128)(2,1)} %bitcast.13), channel_id=1, source_target_pairs={{2,4},{3,5},{4,2},{5,3},{0,6},{1,7},{6,0},{7,1},{10,12},{11,13},{1... | collective-permute-start | bytes 1572872 | tf_op jit(solution)/shard_map/ppermute | solution.py:282
  5.8 13.1 %collective-permute-done.refs_1_.inner_ref = bf16[128,2048]{1,0:T(8,128)(2,1)S(1)} collective-permute-done((bf16[128,2048]{1,0:T(8,128)(2,1)}, bf16[128,2048]{1,0:T(8,128)(2,1)S(1)}, u32[]{:S(2)}, u32[]{:S(2)}) %collective-permute-start) | collective-permute-done | bytes 524320 | tf_op jit(solution)/shard_map/ppermute | solution.py:282
  18.9 10.4 %collective-permute-done.1.refs_2_ = bf16[128,2048]{1,0:T(8,128)(2,1)S(1)} collective-permute-done((bf16[128,2048]{1,0:T(8,128)(2,1)}, bf16[128,2048]{1,0:T(8,128)(2,1)S(1)}, u32[]{:S(2)}, u32[]{:S(2)}) %collective-permute-start.1) | collective-permute-done | bytes 524320 | tf_op jit(solution)/shard_map/ppermute | solution.py:282
  29.2 2.2 %copy-done = bf16[1,1,2,512,2048]{4,3,2,1,0:T(8,128)(2,1)S(1)} copy-done((bf16[1,1,2,512,2048]{4,3,2,1,0:T(8,128)(2,1)S(1)}, bf16[1,1,2,512,2048]{4,3,2,1,0:T(8,128)(2,1)}, u32[]{:S(2)}) %copy-start) | copy-done | bytes 4194328
  31.4 1.0 copy-done.2
  32.5 0.5 shard_map.111
  33.0 0.1 collective-permute-start.3
  33.1 4.1 %shard_map.115 = (bf16[128,512]{1,0:T(8,128)(2,1)S(1)}, bf16[256,512]{1,0:T(8,128)(2,1)S(1)}, bf16[2,512,2048]{2,1,0:T(8,128)(2,1)S(1)}, bf16[256,512]{1,0:T(8,1...) custom-call(s32[4,64]{1,0:T(4,128)} %ids_hbm.1, ...), custom_call_target="tpu_custom_call" | custom-call | flops 536870912 | tf_op jit(solution)/shard_map/pallas_call | solution.py:23
  37.1 1.3 collective-permute-start.6
  38.5 0.7 collective-permute-start.2
  39.2 1.7 %shard_map.116 = (bf16[256,512]{1,0:T(8,128)(2,1)S(1)}, bf16[256,512]{1,0:T(8,128)(2,1)S(1)}, bf16[256,2048]{1,0:T(8,128)(2,1)S(1)}, f32[256,2048]{1,0:T(8,128)S(1)}, bf16[128,512]{1,0:T(8,128)(2,1)S(1)}) custom-call(bf16[256,512]{1,0:T(8,128)(2,1)S(1)} %get-tuple-element.91.x_ref, ...), custom_call_target="tpu_custom_call", output_to_operand_aliasing={{0}: (2, {}), {1}: (3, {}), {2}: (4, {}), {3}: (5, {})} | custom-call | flops 536870912 | bytes 8126464 | tf_op jit(solution)/shard_map/pallas_call | solution.py:23
  40.9 1.3 collective-permute-start.5
  42.3 0.7 collective-permute-start.8
  43.0 2.6 %collective-permute-done.5.x_ref = bf16[128,512]{1,0:T(8,128)(2,1)S(1)} collective-permute-done((bf16[128,512]{1,0:T(8,128)(2,1)S(1)}, bf16[128,512]{1,0:T(8,128)(2,1)S(1)}, u32[]{:S(2)}, u32[]{:S(2)}) %collective-permute-start.5) | collective-permute-done | bytes 131104 | tf_op jit(solution)/shard_map/ppermute | solution.py:254
  45.6 0.7 collective-permute-start.7
  46.3 0.7 collective-permute-start.10
  47.0 0.7 collective-permute-start.9
  47.7 0.9 copy-done.5
  48.6 0.8 collective-permute-start.12
  49.5 3.3 %collective-permute-done.2.refs_1_ = bf16[128,2048]{1,0:T(8,128)(2,1)S(1)} collective-permute-done((bf16[128,2048]{1,0:T(8,128)(2,1)S(1)}, bf16[128,2048]{1,0:T(8,128)(2,1)S(1)}, u32[]{:S(2)}, u32[]{:S(2)}) %collective-permute-start.2) | collective-permute-done | bytes 524320 | tf_op jit(solution)/shard_map/ppermute | solution.py:282
  52.9 0.2 shard_map.113
  53.1 0.7 collective-permute-start.11
  53.9 0.7 collective-permute-start.14
  54.6 0.7 collective-permute-start.13
  55.3 1.3 collective-permute-start.16
  56.6 1.3 collective-permute-start.15
  57.9 21.7 %collective-permute-done.16.grad_ref = bf16[128,512]{1,0:T(8,128)(2,1)S(1)} collective-permute-done((bf16[128,512]{1,0:T(8,128)(2,1)S(1)}, bf16[128,512]{1,0:T(8,128)(2,1)S(1)}, u32[]{:S(2)}, u32[]{:S(2)}) %collective-permute-start.16) | collective-permute-done | bytes 131104 | tf_op jit(solution)/shard_map/ppermute | solution.py:254
  79.6 0.4 shard_map.130
  80.0 6.6 %collective-permute-done.15.grad_ref = bf16[128,512]{1,0:T(8,128)(2,1)S(1)} collective-permute-done((bf16[128,512]{1,0:T(8,128)(2,1)S(1)}, bf16[128,512]{1,0:T(8,128)(2,1)S(1)}, u32[]{:S(2)}, u32[]{:S(2)}) %collective-permute-start.15) | collective-permute-done | bytes 131104 | tf_op jit(solution)/shard_map/ppermute | solution.py:254
  86.7 0.5 shard_map.131
  87.1 0.6 shard_map.114.known_ref
  87.8 2.8 %shard_map.132 = (f32[8,128,2048]{2,1,0:T(8,128)S(1)}, f32[8,128]{1,0:T(8,128)S(1)}) custom-call(f32[8,128,2048]{2,1,0:T(8,128)S(1)} %shard_map.114.known_ref, bf16[256,512]{1,0:T(8,128)(2,1)S(1)} %get-tuple-element.129.normed_ref, bf16[256,2048]{1,0:T(8,128)(2,1)S(1)} %get-tuple-element.152.upper_ref, ...), custom_call_target="tpu_custom_call", output_to_operand_aliasing={{0}: (0, {})} | custom-call | flops 1073741824 | bytes 11010048 | tf_op jit(solution)/shard_map/pallas_call | solution.py:23
  90.6 0.4 shard_map.140
  91.1 1.1 shard_map.133
  92.2 0.6 collective-permute-start.20
  92.8 0.1 collective-permute-done.25.refs_1_
  93.0 1.8 %collective-permute-start.26 = (bf16[64,2048]{1,0:T(8,128)(2,1)S(1)}, bf16[64,2048]{1,0:T(8,128)(2,1)S(1)}, u32[]{:S(2)}, u32[]{:S(2)}) collective-permute-start(bf16[64,2048]{1,0:T(8,128)(2,1)S(1)} %shard_map.141), channel_id=1, source_target_pairs={{0,2},{1,3},{2,0},{3,1},{4,6},{5,7},{6,4},{7,5},{8,10},{9,11},{10,... | collective-permute-start | bytes 786440 | tf_op jit(solution)/shard_map/ppermute | solution.py:282
  94.9 2.2 %collective-permute-start.29 = (bf16[64,2048]{1,0:T(8,128)(2,1)S(1)}, bf16[64,2048]{1,0:T(8,128)(2,1)S(1)}, u32[]{:S(2)}, u32[]{:S(2)}) collective-permute-start(bf16[64,2048]{1,0:T(8,128)(2,1)S(1)} %shard_map.144), channel_id=1, source_target_pairs={{0,2},{1,3},{6,4},{7,5},{8,10},{9,11},{14,12},{15,13},{16,18},{17,... | collective-permute-start | bytes 786440 | tf_op jit(solution)/shard_map/ppermute | solution.py:282
  97.2 1.3 collective-permute-start.21
  98.7 1.5 %collective-permute-start.23 = (bf16[64,2048]{1,0:T(8,128)(2,1)S(1)}, bf16[64,2048]{1,0:T(8,128)(2,1)S(1)}, u32[]{:S(2)}, u32[]{:S(2)}) collective-permute-start(bf16[64,2048]{1,0:T(8,128)(2,1)S(1)} %shard_map.138), channel_id=1, source_target_pairs={{0,2},{1,3},{6,4},{7,5},{8,10},{9,11},{14,12},{15,13},{16,18},{17,... | collective-permute-start | bytes 786440 | tf_op jit(solution)/shard_map/ppermute | solution.py:282
  100.2 0.1 shard_map.135
  100.3 1.3 collective-permute-done.26.refs_2_
  101.6 0.1 shard_map.142
  101.7 0.7 collective-permute-start.27
  102.4 4.7 %collective-permute-done.29.refs_2_ = bf16[64,2048]{1,0:T(8,128)(2,1)S(1)} collective-permute-done((bf16[64,2048]{1,0:T(8,128)(2,1)S(1)}, bf16[64,2048]{1,0:T(8,128)(2,1)S(1)}, u32[]{:S(2)}, u32[]{:S(2)}) %collective-permute-start.29) | collective-permute-done | bytes 262176 | tf_op jit(solution)/shard_map/ppermute | solution.py:282
  107.1 0.1 shard_map.145
  107.2 0.7 collective-permute-start.30
  107.9 4.8 %collective-permute-done.21.refs_2_ = bf16[64,2048]{1,0:T(8,128)(2,1)S(1)} collective-permute-done((bf16[64,2048]{1,0:T(8,128)(2,1)S(1)}, bf16[64,2048]{1,0:T(8,128)(2,1)S(1)}, u32[]{:S(2)}, u32[]{:S(2)}) %collective-permute-start.21) | collective-permute-done | bytes 262176 | tf_op jit(solution)/shard_map/ppermute | solution.py:282
  112.7 4.4 %collective-permute-start.19 = (bf16[128,2048]{1,0:T(8,128)(2,1)S(1)}, bf16[128,2048]{1,0:T(8,128)(2,1)S(1)}, u32[]{:S(2)}, u32[]{:S(2)}) collective-permute-start(bf16[128,2048]{1,0:T(8,128)(2,1)S(1)} %shard_map.135), channel_id=1, source_target_pairs={{0,2},{1,3},{6,4},{7,5},{8,10},{9,11},{14,12},{15,13},{16,18},{17,... | collective-permute-start | bytes 1572872 | tf_op jit(solution)/shard_map/ppermute | solution.py:282
  117.1 0.1 shard_map.137
  117.2 1.1 collective-permute-done.23.refs_2_
  118.3 0.7 collective-permute-start.22
  119.0 0.1 shard_map.139
  119.1 0.7 collective-permute-start.24
  119.8 0.1 shard_map.143
  119.9 1.3 collective-permute-start.28
  121.2 0.1 shard_map.146
  121.4 1.4 %collective-permute-start.31 = (bf16[64,2048]{1,0:T(8,128)(2,1)S(1)}, bf16[64,2048]{1,0:T(8,128)(2,1)S(1)}, u32[]{:S(2)}, u32[]{:S(2)}) collective-permute-start(bf16[64,2048]{1,0:T(8,128)(2,1)S(1)} %shard_map.146), channel_id=1, source_target_pairs={{4,6},{5,7},{2,0},{3,1},{12,14},{13,15},{10,8},{11,9},{20,22},{21,... | collective-permute-start | bytes 786440 | tf_op jit(solution)/shard_map/ppermute | solution.py:282
  122.8 3.8 %shard_map.148 = bf16[1024,2048]{1,0:T(8,128)(2,1)} custom-call(f32[8,128]{1,0:T(8,128)S(1)} %get-tuple-element.155.sum_ref, f32[8,128,2048]{2,1,0:T(8,128)S(1)} %get-tuple-element.156.combined_ref), custom_call_target="tpu_custom_call" | custom-call | bytes 8392704 | tf_op jit(solution)/shard_map/pallas_call | solution.py:23
  126.7 0.6 shard_map.134
  127.3 1.6 %collective-permute-done.19.refs_0_ = bf16[128,2048]{1,0:T(8,128)(2,1)S(1)} collective-permute-done((bf16[128,2048]{1,0:T(8,128)(2,1)S(1)}, bf16[128,2048]{1,0:T(8,128)(2,1)S(1)}, u32[]{:S(2)}, u32[]{:S(2)}) %collective-permute-start.19) | collective-permute-done | bytes 524320 | tf_op jit(solution)/shard_map/ppermute | solution.py:282
  128.9 6.4 %collective-permute-done.28.refs_3_ = bf16[64,2048]{1,0:T(8,128)(2,1)S(1)} collective-permute-done((bf16[64,2048]{1,0:T(8,128)(2,1)S(1)}, bf16[64,2048]{1,0:T(8,128)(2,1)S(1)}, u32[]{:S(2)}, u32[]{:S(2)}) %collective-permute-start.28) | collective-permute-done | bytes 262176 | tf_op jit(solution)/shard_map/ppermute | solution.py:282
  135.3 3.1 %collective-permute-done.31.refs_4_ = bf16[64,2048]{1,0:T(8,128)(2,1)S(1)} collective-permute-done((bf16[64,2048]{1,0:T(8,128)(2,1)S(1)}, bf16[64,2048]{1,0:T(8,128)(2,1)S(1)}, u32[]{:S(2)}, u32[]{:S(2)}) %collective-permute-start.31) | collective-permute-done | bytes 262176 | tf_op jit(solution)/shard_map/ppermute | solution.py:282
  138.5 2.1 %shard_map.147 = (bf16[128,2048]{1,0:T(8,128)(2,1)}, bf16[128,2048]{1,0:T(8,128)(2,1)}, f32[128,2048]{1,0:T(8,128)}) custom-call(f32[128,2048]{1,0:T(8,128)S(1)} %get-tuple-element.159.base_ref, f32[128,2048]{1,0:T(8,128)S(1)} %get-tuple-element.160.rate_ref, bf16[2,512,2048]{2,1,0:T(8,128)(2,1)S(1)} %get-tuple-element.99.w_ref.weights_ref, ...), custom_call_target="tpu_custom_call" | custom-call | bytes 7864320 | tf_op jit(solution)/shard_map/pallas_call | solution.py:23
  (52 shorter events, 0.9 us)
Async XLA Ops:
  0.6 18.2 %collective-permute-start = (bf16[128,2048]{1,0:T(8,128)(2,1)}, bf16[128,2048]{1,0:T(8,128)(2,1)S(1)}, u32[]{:S(2)}, u32[]{:S(2)}) collective-permute-start(bf16[128,2048]{1,0:T(8,128)(2,1)} %bitcast.13), channel_id=1, source_target_pairs={{2,4},{3,5},{4,2},{5,3},{0,6},{1,7},{6,0},{7,1},{10,12},{11,13},{1... | collective-permute-start | bytes 1572872 | tf_op jit(solution)/shard_map/ppermute | solution.py:282
  5.8 23.5 %collective-permute-start.1 = (bf16[128,2048]{1,0:T(8,128)(2,1)}, bf16[128,2048]{1,0:T(8,128)(2,1)S(1)}, u32[]{:S(2)}, u32[]{:S(2)}) collective-permute-start(bf16[128,2048]{1,0:T(8,128)(2,1)} %bitcast.14), channel_id=1, source_target_pairs={{0,2},{1,3},{2,0},{3,1},{4,6},{5,7},{6,4},{7,5},{8,10},{9,11},{10,... | collective-permute-start | bytes 1572872 | tf_op jit(solution)/shard_map/ppermute | solution.py:282
  29.2 2.2 %copy-start = (bf16[1,1,2,512,2048]{4,3,2,1,0:T(8,128)(2,1)S(1)}, bf16[1,1,2,512,2048]{4,3,2,1,0:T(8,128)(2,1)}, u32[]{:S(2)}) copy-start(bf16[1,1,2,512,2048]{4,3,2,1,0:T(8,128)(2,1)} %param.13) | copy-start | bytes 12582916
  31.4 1.0 copy-start.2
  33.0 54.1 %collective-permute-start.3 = (bf16[3,128,2048]{2,1,0:T(8,128)(2,1)S(1)}, bf16[3,128,2048]{2,1,0:T(8,128)(2,1)S(1)}, u32[]{:S(2)}, u32[]{:S(2)}) collective-permute-start(bf16[3,128,2048]{2,1,0:T(8,128)(2,1)S(1)} %get-tuple-element.89), channel_id=1, source_target_pairs={{0,1},{1,0},{2,3},{3,2},{4,5},{5,4},{6,7},{7,6},{8,9},{9,8},{10,11... | collective-permute-start | bytes 4718600 | tf_op jit(solution)/shard_map/ppermute | solution.py:286
  33.1 5.4 %copy-start.3 = (bf16[1,128,2048]{2,1,0:T(8,128)(2,1)S(1)}, bf16[1,128,2048]{2,1,0:T(8,128)(2,1)}, u32[]{:S(2)}) copy-start(bf16[1,128,2048]{2,1,0:T(8,128)(2,1)} %param.12) | copy-start | bytes 1572868
  37.1 5.1 %collective-permute-start.6 = (bf16[128,512]{1,0:T(8,128)(2,1)S(1)}, bf16[128,512]{1,0:T(8,128)(2,1)S(1)}, u32[]{:S(2)}, u32[]{:S(2)}) collective-permute-start(bf16[128,512]{1,0:T(8,128)(2,1)S(1)} %get-tuple-element.100), channel_id=1, source_target_pairs={{0,8},{1,9},{2,10},{3,11},{4,12},{5,13},{6,14},{7,15}} | collective-permute-start | bytes 393224 | tf_op jit(solution)/shard_map/ppermute | solution.py:254
  38.5 14.3 %collective-permute-start.2 = (bf16[128,2048]{1,0:T(8,128)(2,1)S(1)}, bf16[128,2048]{1,0:T(8,128)(2,1)S(1)}, u32[]{:S(2)}, u32[]{:S(2)}) collective-permute-start(bf16[128,2048]{1,0:T(8,128)(2,1)S(1)} %shard_map.112), channel_id=1, source_target_pairs={{0,4},{1,5},{4,6},{5,7},{6,2},{7,3},{2,0},{3,1},{8,12},{9,13},{12,... | collective-permute-start | bytes 1572872 | tf_op jit(solution)/shard_map/ppermute | solution.py:282
  40.9 4.7 %collective-permute-start.5 = (bf16[128,512]{1,0:T(8,128)(2,1)S(1)}, bf16[128,512]{1,0:T(8,128)(2,1)S(1)}, u32[]{:S(2)}, u32[]{:S(2)}) collective-permute-start(bf16[128,512]{1,0:T(8,128)(2,1)S(1)} %get-tuple-element.97), channel_id=1, source_target_pairs={{0,8},{1,9},{2,10},{3,11},{4,12},{5,13},{6,14},{7,15}} | collective-permute-start | bytes 393224 | tf_op jit(solution)/shard_map/ppermute | solution.py:254
  42.3 4.0 %collective-permute-start.8 = (bf16[128,512]{1,0:T(8,128)(2,1)S(1)}, bf16[128,512]{1,0:T(8,128)(2,1)S(1)}, u32[]{:S(2)}, u32[]{:S(2)}) collective-permute-start(bf16[128,512]{1,0:T(8,128)(2,1)S(1)} %get-tuple-element.110), channel_id=1, source_target_pairs={{8,16},{9,17},{10,18},{11,19},{12,20},{13,21},{14,22},{15,23}} | collective-permute-start | bytes 393224 | tf_op jit(solution)/shard_map/ppermute | solution.py:254
  45.6 1.4 collective-permute-start.7
  46.3 1.4 collective-permute-start.10
  47.0 2.5 %collective-permute-start.9 = (bf16[128,512]{1,0:T(8,128)(2,1)S(1)}, bf16[128,512]{1,0:T(8,128)(2,1)S(1)}, u32[]{:S(2)}, u32[]{:S(2)}) collective-permute-start(bf16[128,512]{1,0:T(8,128)(2,1)S(1)} %get-tuple-element.119), channel_id=1, source_target_pairs={{16,24},{17,25},{18,26},{19,27},{20,28},{21,29},{22,30},{23,31}} | collective-permute-start | bytes 393224 | tf_op jit(solution)/shard_map/ppermute | solution.py:254
  47.7 1.0 copy-start.5
  48.6 5.2 %collective-permute-start.12 = (bf16[128,512]{1,0:T(8,128)(2,1)S(1)}, bf16[128,512]{1,0:T(8,128)(2,1)S(1)}, u32[]{:S(2)}, u32[]{:S(2)}) collective-permute-start(bf16[128,512]{1,0:T(8,128)(2,1)S(1)} %get-tuple-element.135), channel_id=1, source_target_pairs={{24,16},{25,17},{26,18},{27,19},{28,20},{29,21},{30,22},{31,23}} | collective-permute-start | bytes 393224 | tf_op jit(solution)/shard_map/ppermute | solution.py:254
  49.5 3.4 %copy-start.1 = (bf16[1,1,2,512,2048]{4,3,2,1,0:T(8,128)(2,1)S(1)}, bf16[1,1,2,512,2048]{4,3,2,1,0:T(8,128)(2,1)}, u32[]{:S(2)}) copy-start(bf16[1,1,2,512,2048]{4,3,2,1,0:T(8,128)(2,1)} %param.13) | copy-start | bytes 12582916
  53.0 34.1 %collective-permute-start.4 = (bf16[1,128,2048]{2,1,0:T(8,128)(2,1)S(1)}, bf16[1,128,2048]{2,1,0:T(8,128)(2,1)S(1)}, u32[]{:S(2)}, u32[]{:S(2)}) collective-permute-start(bf16[1,128,2048]{2,1,0:T(8,128)(2,1)S(1)} %get-tuple-element.90), channel_id=1, source_target_pairs={{0,1},{1,0},{2,3},{3,2},{4,5},{5,4},{6,7},{7,6},{8,9},{9,8},{10,11... | collective-permute-start | bytes 1572872 | tf_op jit(solution)/shard_map/ppermute | solution.py:286
  53.1 1.4 collective-permute-start.11
  53.9 1.4 collective-permute-start.14
  54.6 2.0 %collective-permute-start.13 = (bf16[128,512]{1,0:T(8,128)(2,1)S(1)}, bf16[128,512]{1,0:T(8,128)(2,1)S(1)}, u32[]{:S(2)}, u32[]{:S(2)}) collective-permute-start(bf16[128,512]{1,0:T(8,128)(2,1)S(1)} %get-tuple-element.140), channel_id=1, source_target_pairs={{16,8},{17,9},{18,10},{19,11},{20,12},{21,13},{22,14},{23,15}} | collective-permute-start | bytes 393224 | tf_op jit(solution)/shard_map/ppermute | solution.py:254
  55.3 24.3 %collective-permute-start.16 = (bf16[128,512]{1,0:T(8,128)(2,1)S(1)}, bf16[128,512]{1,0:T(8,128)(2,1)S(1)}, u32[]{:S(2)}, u32[]{:S(2)}) collective-permute-start(bf16[128,512]{1,0:T(8,128)(2,1)S(1)} %get-tuple-element.147), channel_id=1, source_target_pairs={{8,0},{9,1},{10,2},{11,3},{12,4},{13,5},{14,6},{15,7}} | collective-permute-start | bytes 393224 | tf_op jit(solution)/shard_map/ppermute | solution.py:254
  56.6 30.0 %collective-permute-start.15 = (bf16[128,512]{1,0:T(8,128)(2,1)S(1)}, bf16[128,512]{1,0:T(8,128)(2,1)S(1)}, u32[]{:S(2)}, u32[]{:S(2)}) collective-permute-start(bf16[128,512]{1,0:T(8,128)(2,1)S(1)} %get-tuple-element.146), channel_id=1, source_target_pairs={{8,0},{9,1},{10,2},{11,3},{12,4},{13,5},{14,6},{15,7}} | collective-permute-start | bytes 393224 | tf_op jit(solution)/shard_map/ppermute | solution.py:254
  91.0 2.0 %collective-permute-start.25 = (bf16[128,2048]{1,0:T(8,128)(2,1)S(1)}, bf16[128,2048]{1,0:T(8,128)(2,1)S(1)}, u32[]{:S(2)}, u32[]{:S(2)}) collective-permute-start(bf16[128,2048]{1,0:T(8,128)(2,1)S(1)} %get-tuple-element.166), channel_id=1, source_target_pairs={{0,1},{1,0},{2,3},{3,2},{4,5},{5,4},{6,7},{7,6},{8,9},{9,8},{10,11... | collective-permute-start | bytes 1572872 | tf_op jit(solution)/shard_map/ppermute | solution.py:286
  92.2 4.9 %collective-permute-start.20 = (bf16[128,2048]{1,0:T(8,128)(2,1)S(1)}, bf16[128,2048]{1,0:T(8,128)(2,1)S(1)}, u32[]{:S(2)}, u32[]{:S(2)}) collective-permute-start(bf16[128,2048]{1,0:T(8,128)(2,1)S(1)} %get-tuple-element.164), channel_id=1, source_target_pairs={{0,1},{1,0},{2,3},{3,2},{4,5},{5,4},{6,7},{7,6},{8,9},{9,8},{10,11... | collective-permute-start | bytes 1572872 | tf_op jit(solution)/shard_map/ppermute | solution.py:286
  92.7 5.9 %collective-permute-start.18 = (bf16[128,2048]{1,0:T(8,128)(2,1)S(1)}, bf16[128,2048]{1,0:T(8,128)(2,1)S(1)}, u32[]{:S(2)}, u32[]{:S(2)}) collective-permute-start(bf16[128,2048]{1,0:T(8,128)(2,1)S(1)} %get-tuple-element.162), channel_id=1, source_target_pairs={{0,1},{1,0},{2,3},{3,2},{4,5},{5,4},{6,7},{7,6},{8,9},{9,8},{10,11... | collective-permute-start | bytes 1572872 | tf_op jit(solution)/shard_map/ppermute | solution.py:286
  93.0 8.6 %collective-permute-start.26 = (bf16[64,2048]{1,0:T(8,128)(2,1)S(1)}, bf16[64,2048]{1,0:T(8,128)(2,1)S(1)}, u32[]{:S(2)}, u32[]{:S(2)}) collective-permute-start(bf16[64,2048]{1,0:T(8,128)(2,1)S(1)} %shard_map.141), channel_id=1, source_target_pairs={{0,2},{1,3},{2,0},{3,1},{4,6},{5,7},{6,4},{7,5},{8,10},{9,11},{10,... | collective-permute-start | bytes 786440 | tf_op jit(solution)/shard_map/ppermute | solution.py:282
  94.9 12.3 %collective-permute-start.29 = (bf16[64,2048]{1,0:T(8,128)(2,1)S(1)}, bf16[64,2048]{1,0:T(8,128)(2,1)S(1)}, u32[]{:S(2)}, u32[]{:S(2)}) collective-permute-start(bf16[64,2048]{1,0:T(8,128)(2,1)S(1)} %shard_map.144), channel_id=1, source_target_pairs={{0,2},{1,3},{6,4},{7,5},{8,10},{9,11},{14,12},{15,13},{16,18},{17,... | collective-permute-start | bytes 786440 | tf_op jit(solution)/shard_map/ppermute | solution.py:282
  97.2 15.5 %collective-permute-start.21 = (bf16[64,2048]{1,0:T(8,128)(2,1)S(1)}, bf16[64,2048]{1,0:T(8,128)(2,1)S(1)}, u32[]{:S(2)}, u32[]{:S(2)}) collective-permute-start(bf16[64,2048]{1,0:T(8,128)(2,1)S(1)} %shard_map.136), channel_id=1, source_target_pairs={{0,2},{1,3},{6,4},{7,5},{8,10},{9,11},{14,12},{15,13},{16,18},{17,... | collective-permute-start | bytes 786440 | tf_op jit(solution)/shard_map/ppermute | solution.py:282
  98.5 22.9 %collective-permute-start.17 = (bf16[128,2048]{1,0:T(8,128)(2,1)S(1)}, bf16[128,2048]{1,0:T(8,128)(2,1)S(1)}, u32[]{:S(2)}, u32[]{:S(2)}) collective-permute-start(bf16[128,2048]{1,0:T(8,128)(2,1)S(1)} %get-tuple-element.158), channel_id=1, source_target_pairs={{0,1},{1,0},{2,3},{3,2},{4,5},{5,4},{6,7},{7,6},{8,9},{9,8},{10,11... | collective-permute-start | bytes 1572872 | tf_op jit(solution)/shard_map/ppermute | solution.py:286
  98.7 19.7 %collective-permute-start.23 = (bf16[64,2048]{1,0:T(8,128)(2,1)S(1)}, bf16[64,2048]{1,0:T(8,128)(2,1)S(1)}, u32[]{:S(2)}, u32[]{:S(2)}) collective-permute-start(bf16[64,2048]{1,0:T(8,128)(2,1)S(1)} %shard_map.138), channel_id=1, source_target_pairs={{0,2},{1,3},{6,4},{7,5},{8,10},{9,11},{14,12},{15,13},{16,18},{17,... | collective-permute-start | bytes 786440 | tf_op jit(solution)/shard_map/ppermute | solution.py:282
  101.7 17.4 %collective-permute-start.27 = (bf16[64,2048]{1,0:T(8,128)(2,1)S(1)}, bf16[64,2048]{1,0:T(8,128)(2,1)S(1)}, u32[]{:S(2)}, u32[]{:S(2)}) collective-permute-start(bf16[64,2048]{1,0:T(8,128)(2,1)S(1)} %shard_map.142), channel_id=1, source_target_pairs={{2,4},{3,5},{4,2},{5,3},{10,12},{11,13},{12,10},{13,11},{18,20},{1... | collective-permute-start | bytes 786440 | tf_op jit(solution)/shard_map/ppermute | solution.py:282
  107.2 12.7 %collective-permute-start.30 = (bf16[64,2048]{1,0:T(8,128)(2,1)S(1)}, bf16[64,2048]{1,0:T(8,128)(2,1)S(1)}, u32[]{:S(2)}, u32[]{:S(2)}) collective-permute-start(bf16[64,2048]{1,0:T(8,128)(2,1)S(1)} %shard_map.145), channel_id=1, source_target_pairs={{2,4},{3,5},{4,2},{5,3},{10,12},{11,13},{12,10},{13,11},{18,20},{1... | collective-permute-start | bytes 786440 | tf_op jit(solution)/shard_map/ppermute | solution.py:282
  112.7 16.2 %collective-permute-start.19 = (bf16[128,2048]{1,0:T(8,128)(2,1)S(1)}, bf16[128,2048]{1,0:T(8,128)(2,1)S(1)}, u32[]{:S(2)}, u32[]{:S(2)}) collective-permute-start(bf16[128,2048]{1,0:T(8,128)(2,1)S(1)} %shard_map.135), channel_id=1, source_target_pairs={{0,2},{1,3},{6,4},{7,5},{8,10},{9,11},{14,12},{15,13},{16,18},{17,... | collective-permute-start | bytes 1572872 | tf_op jit(solution)/shard_map/ppermute | solution.py:282
  118.3 8.9 %collective-permute-start.22 = (bf16[64,2048]{1,0:T(8,128)(2,1)S(1)}, bf16[64,2048]{1,0:T(8,128)(2,1)S(1)}, u32[]{:S(2)}, u32[]{:S(2)}) collective-permute-start(bf16[64,2048]{1,0:T(8,128)(2,1)S(1)} %shard_map.137), channel_id=1, source_target_pairs={{2,4},{3,5},{4,2},{5,3},{10,12},{11,13},{12,10},{13,11},{18,20},{1... | collective-permute-start | bytes 786440 | tf_op jit(solution)/shard_map/ppermute | solution.py:282
  119.1 8.1 %collective-permute-start.24 = (bf16[64,2048]{1,0:T(8,128)(2,1)S(1)}, bf16[64,2048]{1,0:T(8,128)(2,1)S(1)}, u32[]{:S(2)}, u32[]{:S(2)}) collective-permute-start(bf16[64,2048]{1,0:T(8,128)(2,1)S(1)} %shard_map.139), channel_id=1, source_target_pairs={{2,4},{3,5},{4,2},{5,3},{10,12},{11,13},{12,10},{13,11},{18,20},{1... | collective-permute-start | bytes 786440 | tf_op jit(solution)/shard_map/ppermute | solution.py:282
  119.9 15.4 %collective-permute-start.28 = (bf16[64,2048]{1,0:T(8,128)(2,1)S(1)}, bf16[64,2048]{1,0:T(8,128)(2,1)S(1)}, u32[]{:S(2)}, u32[]{:S(2)}) collective-permute-start(bf16[64,2048]{1,0:T(8,128)(2,1)S(1)} %shard_map.143), channel_id=1, source_target_pairs={{4,6},{5,7},{2,0},{3,1},{12,14},{13,15},{10,8},{11,9},{20,22},{21,... | collective-permute-start | bytes 786440 | tf_op jit(solution)/shard_map/ppermute | solution.py:282
  121.3 5.3 %copy-start.4 = (f32[1,128,2048]{2,1,0:T(8,128)S(1)}, f32[1,128,2048]{2,1,0:T(8,128)}, u32[]{:S(2)}) copy-start(f32[1,128,2048]{2,1,0:T(8,128)} %param.14) | copy-start | bytes 3145732
  121.3 5.3 %copy-start.6 = (bf16[1,128,2048]{2,1,0:T(8,128)(2,1)S(1)}, bf16[1,128,2048]{2,1,0:T(8,128)(2,1)}, u32[]{:S(2)}) copy-start(bf16[1,128,2048]{2,1,0:T(8,128)(2,1)} %param.11) | copy-start | bytes 1572868
  121.4 17.1 %collective-permute-start.31 = (bf16[64,2048]{1,0:T(8,128)(2,1)S(1)}, bf16[64,2048]{1,0:T(8,128)(2,1)S(1)}, u32[]{:S(2)}, u32[]{:S(2)}) collective-permute-start(bf16[64,2048]{1,0:T(8,128)(2,1)S(1)} %shard_map.146), channel_id=1, source_target_pairs={{4,6},{5,7},{2,0},{3,1},{12,14},{13,15},{10,8},{11,9},{20,22},{21,... | collective-permute-start | bytes 786440 | tf_op jit(solution)/shard_map/ppermute | solution.py:282
